TPU v7x, 32 devices: a whole 2x2x4 slice. The times are simulated.
32 devices in a mesh: dom: 16 (over z, y, x), sub: 2 (over core).
Axes of the slice: x: 2, y: 2, z: 4, core: 2. Of those that a mesh axis runs over, the one named last changes fastest.
Arguments:
- node_feats: float32 [8192, 128], P(('dom', 'sub')), may hold values from -6 to 6
- edge_in: float32 [2, 256, 128], replicated, may hold values from -0.375 to 0.375
- edge_out: float32 [2, 128, 128], replicated, may hold values from -0.5 to 0.5
- node_in: float32 [2, 256, 128], replicated, may hold values from -0.375 to 0.375
- node_out: float32 [2, 128, 128], replicated, may hold values from -0.5 to 0.5
- decoder: float32 [128], replicated, may hold values from -0.5 to 0.5
- edge_index: int32 [2, 40960], P(None, ('dom', 'sub')), may hold values from 0 to 255
- halo_index: int32 [32, 4, 64], P(('dom', 'sub')), may hold values from 0 to 255, as said below
- target: float32 [8192], P(('dom', 'sub')), may hold values from -6 to 6
Outputs:
- loss: float32 [], replicated
- prediction: float32 [8192], P(('dom', 'sub'))
- grad_edge_in: float32 [2, 256, 128], replicated
- grad_edge_out: float32 [2, 128, 128], replicated
- grad_node_in: float32 [2, 256, 128], replicated
- grad_node_out: float32 [2, 128, 128], replicated
- grad_decoder: float32 [128], replicated
Inputs may be any that keep to these rules, and one draw needn't show every extreme that they name: For each sub-partition the 256 entries halo_index[p] are distinct local node numbers; entry [p, k, j] and entry [q, k', j] of the neighbour q across direction k name the same physical mesh node.
All inputs are finite; a program needn't handle non-finite values.
Results may differ from a plain program's by a relative error of at most 0.0003.
Values sent between devices are 32-bit elements; how exact they have to be, the bound alone decides.
No kernel may reach another device: no remote copies, remote signals or barrier semaphores. Data moves between devices by JAX's collectives and lax.ppermute only.
A program may use at most 64 MiB of HBM per device.

v0:
```python
import functools

import jax
import jax.numpy as jnp
from jax import lax
from jax.experimental import pallas as pl
from jax.experimental.pallas import tpu as pltpu
from jax.sharding import PartitionSpec as P

F32 = jnp.float32
BF16 = jnp.bfloat16
VMEM = pl.BlockSpec(memory_space=pltpu.VMEM)
EXTRA = 8


def halves(x):
    high = x.astype(BF16)
    low = (x - high.astype(F32)).astype(BF16)
    return high, low


def side(x):
    return jnp.concatenate(halves(x), axis=1)


def fold(x):
    width = x.shape[1] // 2
    return x[:, :width] + x[:, width:]


def dot(a, b, dims=((1,), (0,))):
    return lax.dot_general(a, b, (dims, ((), ())), preferred_element_type=F32)


def mm(x, w):
    wide = side(w)
    return fold(dot(side(x), jnp.concatenate([wide, wide], axis=0)))


def mmt(x, w):
    high, low = halves(w)
    both = jnp.concatenate(
        [jnp.concatenate([high, high], axis=1), jnp.concatenate([low, low], axis=1)], axis=0
    )
    return fold(dot(side(x), both, ((1,), (1,))))


def tmm(x, y):
    wide = fold(dot(side(x), side(y), ((0,), (0,))))
    width = x.shape[1]
    return wide[:width] + wide[width:]


def silu_parts(v):
    gate = 1.0 / (1.0 + jnp.exp(-v))
    return v * gate, gate * (1.0 + v * (1.0 - gate))


def row_of(column):
    n = column.shape[0]
    eye = lax.broadcasted_iota(jnp.int32, (n, n), 0) == lax.broadcasted_iota(jnp.int32, (n, n), 1)
    return jnp.sum(jnp.where(eye, column, 0.0), axis=0, keepdims=True)


def onehot(mask):
    return jnp.where(mask, 1.0, 0.0).astype(BF16)


def edge_forward(features, weight_in, recv, send, recv_t, slope_ref, chunk):
    width = features.shape[1]
    to_recv = side(mm(features, weight_in[:width]))
    to_send = side(mm(features, weight_in[width:]))
    total = None
    for start in range(0, recv.shape[0], chunk):
        rows = pl.ds(start, chunk)
        pre = fold(dot(recv[rows, :], to_recv) + dot(send[rows, :], to_send))
        act, slope = silu_parts(pre)
        slope_ref[rows, :] = slope
        part = dot(recv_t[:, rows], side(act))
        total = part if total is None else total + part
    return fold(total)


def edge_backward(local_grad, weight_out, recv, recv_t, send_t, slope_ref, chunk):
    spread = side(mmt(local_grad, weight_out))
    total_r = total_s = None
    for start in range(0, recv.shape[0], chunk):
        rows = pl.ds(start, chunk)
        grad = side(fold(dot(recv[rows, :], spread)) * slope_ref[rows, :])
        part_r = dot(recv_t[:, rows], grad)
        part_s = dot(send_t[:, rows], grad)
        total_r = part_r if total_r is None else total_r + part_r
        total_s = part_s if total_s is None else total_s + part_s
    return fold(total_r), fold(total_s)


def node_forward(features, summed, weight_in, weight_out):
    width = features.shape[1]
    pre = mm(features, weight_in[:width]) + mm(summed, weight_in[width:])
    act, slope = silu_parts(pre)
    return features + mm(act, weight_out), act, slope


def put_blocks(value, refs):
    size = refs[0].shape[0]
    for at, ref in enumerate(refs):
        ref[...] = value[at * size : (at + 1) * size]


def take_sum(own, came):
    parts = [
        ref[...] + came[at][...] if came[at] is not None else ref[...]
        for at, ref in enumerate(own)
    ]
    return jnp.concatenate(parts, axis=0)


def even(axis):
    return lax.rem(lax.axis_index(axis), 2) == 0


def first_kernel(
    chunk, feats, index, halo, weight_in, weight_out,
    flat_out, recv, send, recv_t, send_t, h_out, slope, q_out, *blocks
):
    nodes = feats.shape[0]
    edges = index.shape[1]
    lanes = 128
    count = edges // lanes
    size = halo.shape[2]
    pieces = [index[0:1, pl.ds(b * lanes, lanes)] for b in range(count)]
    pieces += [index[1:2, pl.ds(b * lanes, lanes)] for b in range(count)]
    table = jnp.concatenate(pieces, axis=0).astype(F32)
    lists = jnp.concatenate([halo[0].astype(F32), jnp.zeros((4, lanes - size), F32)], axis=1)
    rest = jnp.zeros((lanes - 2 * count - 4, lanes), F32)
    columns = jnp.concatenate([table, lists, rest], axis=0).T
    by_dir = [columns[:size, 2 * count + k : 2 * count + k + 1] for k in range(4)]
    dom_even, sub_even = even("dom"), even("sub")
    flat = jnp.concatenate(
        [
            jnp.where(dom_even, by_dir[1], by_dir[0]),
            jnp.where(dom_even, by_dir[0], by_dir[1]),
            jnp.where(sub_even, by_dir[3], by_dir[2]),
            jnp.where(sub_even, by_dir[2], by_dir[3]),
        ],
        axis=0,
    )
    flat_row = row_of(flat)
    flat_out[...] = jnp.broadcast_to(flat, flat_out.shape)
    for b in range(count):
        rows = pl.ds(b * lanes, lanes)
        recv[rows, :] = onehot(columns[:, b : b + 1] == flat_row)
        send[rows, :] = onehot(columns[:, count + b : count + b + 1] == flat_row)
        recv_t[:, rows] = onehot(flat == table[b : b + 1])
        send_t[:, rows] = onehot(flat == table[count + b : count + b + 1])
    place = onehot(flat == lax.broadcasted_iota(jnp.int32, (nodes, nodes), 1).astype(F32))
    features = fold(dot(place, side(feats[...])))
    h_out[...] = features
    q = edge_forward(features, weight_in[0], recv, send, recv_t, slope, chunk)
    q_out[...] = q
    put_blocks(mm(q, weight_out[0]), blocks)


def middle_kernel(
    chunk, layer, names, *refs
):
    own, refs = refs[:4], refs[4:]
    came, refs = unpack(names, refs)
    (h, recv, send, recv_t, node_in, node_out, edge_in, edge_out,
     agg_out, h_out, node_act, node_slope, slope, q_out, *blocks) = refs
    summed = take_sum(own, came)
    agg_out[...] = summed
    features, act, gate = node_forward(h[...], summed, node_in[layer], node_out[layer])
    h_out[...] = features
    node_act[...] = act
    node_slope[...] = gate
    q = edge_forward(features, edge_in[layer + 1], recv, send, recv_t, slope, chunk)
    q_out[...] = q
    put_blocks(mm(q, edge_out[layer + 1]), blocks)


def unpack(names, refs):
    came = []
    at = 0
    for there in names:
        came.append(refs[at] if there else None)
        at += there
    return came, refs[at:]


def last_kernel(
    layer, count, names, *refs
):
    own, refs = refs[:4], refs[4:]
    came, refs = unpack(names, refs)
    (h, flat_ref, target, decoder, node_in, node_out,
     agg_out, node_act, pre_grad_out, top_grad_out, through_out, pred_out, tail_out, *blocks) = refs
    nodes, width = h.shape
    summed = take_sum(own, came)
    agg_out[...] = summed
    features, act, gate = node_forward(h[...], summed, node_in[layer], node_out[layer])
    node_act[...] = act
    weights = decoder[...]
    predicted = jnp.sum(features * weights, axis=1, keepdims=True)
    flat = flat_ref[:, 0:1]
    here = flat == lax.broadcasted_iota(jnp.int32, (nodes, nodes), 1).astype(F32)
    pred_out[...] = jnp.sum(jnp.where(here, predicted, 0.0), axis=0, keepdims=True)
    wanted = jnp.sum(jnp.where(here, target[...], 0.0), axis=1, keepdims=True)
    misfit = predicted - wanted
    seed = 2.0 * misfit / count
    decoder_grad = jnp.sum(seed * features, axis=0, keepdims=True)
    loss = jnp.broadcast_to(jnp.sum(misfit * misfit, axis=0, keepdims=True), (1, width))
    tail_out[...] = jnp.concatenate([decoder_grad, loss, jnp.zeros((EXTRA - 2, width), F32)], 0)
    top = seed * weights
    top_grad_out[...] = top
    pre_grad = mmt(top, node_out[layer]) * gate
    pre_grad_out[...] = pre_grad
    through_out[...] = top + mmt(pre_grad, node_in[layer, :width])
    put_blocks(mmt(pre_grad, node_in[layer, width:]), blocks)


def node_grads_kernel(h, summed, act, pre_grad, top_grad, out):
    width = h.shape[1]
    out[0:width, :] = tmm(h[...], pre_grad[...])
    out[width : 2 * width, :] = tmm(summed[...], pre_grad[...])
    out[2 * width :, :] = tmm(act[...], top_grad[...])


def edge_grads_kernel(h, q, local_grad, to_recv, to_send, out):
    width = h.shape[1]
    out[0:width, :] = tmm(h[...], to_recv[...])
    out[width : 2 * width, :] = tmm(h[...], to_send[...])
    out[2 * width :, :] = tmm(q[...], local_grad[...])


def back_kernel(
    chunk, layer, names, *refs
):
    own, refs = refs[:4], refs[4:]
    came, refs = unpack(names, refs)
    (through, node_slope, recv, recv_t, send_t, slope, edge_in, edge_out, node_in, node_out,
     local_out, recv_out, send_out, top_out, pre_out, *blocks) = refs
    width = through.shape[1]
    local_grad = take_sum(own, came)
    local_out[...] = local_grad
    to_recv, to_send = edge_backward(
        local_grad, edge_out[layer], recv, recv_t, send_t, slope, chunk
    )
    recv_out[...] = to_recv
    send_out[...] = to_send
    top = (
        through[...]
        + mmt(to_recv, edge_in[layer, :width])
        + mmt(to_send, edge_in[layer, width:])
    )
    top_out[...] = top
    pre_grad = mmt(top, node_out[layer - 1]) * node_slope[...]
    pre_out[...] = pre_grad
    put_blocks(mmt(pre_grad, node_in[layer - 1, width:]), blocks)


def split_rows(value, ref, first):
    per = ref.shape[1] - EXTRA
    at = 0
    while at < value.shape[0]:
        group, inside = divmod(first + at, per)
        take = min(per - inside, value.shape[0] - at)
        ref[group, inside : inside + take, :] = value[at : at + take]
        at += take


def end_kernel(
    chunk, names, *refs
):
    own, refs = refs[:4], refs[4:]
    came, refs = unpack(names, refs)
    (h, q, recv, recv_t, send_t, slope, edge_out, node_low, node_high, edge_high, tail,
     mine, other) = refs
    local_grad = take_sum(own, came)
    to_recv, to_send = edge_backward(local_grad, edge_out[0], recv, recv_t, send_t, slope, chunk)
    low = [
        node_low[...],
        tmm(h[...], to_recv),
        tmm(h[...], to_send),
        tmm(q[...], local_grad),
    ]
    per = mine.shape[1] - EXTRA
    blank = jnp.zeros((mine.shape[0], EXTRA, mine.shape[2]), F32)

    def write(ref_high, ref_low):
        ref_high[:, per:, :] = blank
        ref_low[:, per:, :] = blank
        ref_high[0, per:, :] = tail[...]
        at = 0
        for value in low:
            split_rows(value, ref_low, at)
            at += value.shape[0]
        split_rows(node_high[...], ref_high, 0)
        split_rows(edge_high[...], ref_high, node_high.shape[0])

    first = lax.axis_index("sub") == 0
    pl.when(first)(lambda: write(mine, other))
    pl.when(jnp.logical_not(first))(lambda: write(other, mine))


def add_kernel(a, b, out):
    out[...] = a[...] + b[...]


def total_kernel(parts, out):
    total = jnp.sum(parts[...], axis=0)
    per = total.shape[0] - EXTRA
    body = total[: per + 1]
    squares = jnp.sum(jnp.sum(body * body, axis=0, keepdims=True), axis=1, keepdims=True)
    last = jnp.broadcast_to(squares, (1, total.shape[1]))
    total = jnp.concatenate([total[:-1], last], axis=0)
    out[...] = jnp.broadcast_to(total[None], out.shape)


def scale_kernel(
    params, count, mine, other, loss, edge_in, edge_out, node_in, node_out, decoder
):
    rows = mine.shape[1]
    per = rows - EXTRA
    width = mine.shape[2]
    squares = jnp.sum(
        mine[:, rows - 1 : rows, :] + other[:, rows - 1 : rows, :], axis=0
    )
    scale = 1.0 / jnp.sqrt(squares / params + 1e-06)

    def join(ref, first, size):
        parts = []
        at = 0
        while at < size:
            group, inside = divmod(first + at, per)
            take = min(per - inside, size - at)
            parts.append(ref[group, inside : inside + take, :])
            at += take
        return jnp.concatenate(parts, axis=0) * scale

    def write(high, low):
        for layer, ref in ((1, high), (0, low)):
            node_in[layer] = join(ref, 0, 2 * width)
            node_out[layer] = join(ref, 2 * width, width)
            edge_in[layer] = join(ref, 3 * width, 2 * width)
            edge_out[layer] = join(ref, 5 * width, width)
        decoder[...] = high[0, per : per + 1, :] * scale
        loss[...] = high[0, per + 1 : per + 2, :] / count

    first = lax.axis_index("sub") == 0
    pl.when(first)(lambda: write(mine, other))
    pl.when(jnp.logical_not(first))(lambda: write(other, mine))


def call(kernel, outs, *args):
    shapes = [jax.ShapeDtypeStruct(shape, dtype) for shape, dtype in outs]
    return pl.pallas_call(
        kernel,
        out_shape=shapes,
        in_specs=[VMEM] * len(args),
        out_specs=[VMEM] * len(shapes),
    )(*args)


def pairs(count, offset):
    found = []
    for low in range(offset, count - 1, 2):
        found += [(low, low + 1), (low + 1, low)]
    return found


def per_device(
    node_feats, edge_in, edge_out, node_in, node_out, decoder, edge_index, halo_index, target
):
    nodes, width = node_feats.shape
    edges = edge_index.shape[1]
    size = halo_index.shape[2]
    n_dom, n_sub = lax.axis_size("dom"), lax.axis_size("sub")
    count = nodes * n_dom * n_sub
    if edge_in.shape[0] != 2 or 4 * size != nodes:
        raise ValueError("unsupported sizes")
    chunk = 256
    routes = [("dom", 1), ("dom", 0), ("sub", 0), ("sub", 1)]
    order = [1, 0, 2, 3]
    links = [pairs(lax.axis_size(axis), offset) for axis, offset in routes]
    links = [links[1], links[0], links[2], links[3]]
    axes = ["dom", "dom", "sub", "sub"]
    names = tuple(1 if link else 0 for link in links)

    def exchange(blocks):
        came = [None] * 4
        for at in order:
            if links[at]:
                came[at] = lax.ppermute(blocks[at], axes[at], links[at])
        return [block for block in came if block is not None]

    node_shape = ((nodes, width), F32)
    edge_shape = ((edges, width), F32)
    block_shapes = [((size, width), F32)] * 4

    flat, recv, send, recv_t, send_t, h0, slope0, q0, *blocks = call(
        functools.partial(first_kernel, chunk),
        [
            ((nodes, 128), F32),
            ((edges, nodes), BF16), ((edges, nodes), BF16),
            ((nodes, edges), BF16), ((nodes, edges), BF16),
            node_shape, edge_shape, node_shape, *block_shapes,
        ],
        node_feats, edge_index, halo_index, edge_in, edge_out,
    )
    agg0, h1, act0, gate0, slope1, q1, *blocks = call(
        functools.partial(middle_kernel, chunk, 0, names),
        [node_shape, node_shape, node_shape, node_shape, edge_shape, node_shape, *block_shapes],
        *blocks, *exchange(blocks),
        h0, recv, send, recv_t, node_in, node_out, edge_in, edge_out,
    )
    agg1, act1, pre1, top1, through, pred, tail, *blocks = call(
        functools.partial(last_kernel, 1, count, names),
        [node_shape, node_shape, node_shape, node_shape, node_shape,
         ((1, nodes), F32), ((EXTRA, width), F32), *block_shapes],
        *blocks, *exchange(blocks),
        h1, flat, target.reshape(1, nodes), decoder.reshape(1, width), node_in, node_out,
    )
    grads_shape = [((3 * width, width), F32)]
    came = exchange(blocks)
    (node_high,) = call(node_grads_kernel, grads_shape, h1, agg1, act1, pre1, top1)
    local1, to_recv1, to_send1, top0, pre0, *blocks = call(
        functools.partial(back_kernel, chunk, 1, names),
        [node_shape, node_shape, node_shape, node_shape, node_shape, *block_shapes],
        *blocks, *came,
        through, gate0, recv, recv_t, send_t, slope1, edge_in, edge_out, node_in, node_out,
    )
    came = exchange(blocks)
    (edge_high,) = call(edge_grads_kernel, grads_shape, h1, q1, local1, to_recv1, to_send1)
    (node_low,) = call(node_grads_kernel, grads_shape, h0, agg0, act0, pre0, top0)
    per = 6 * width // n_dom
    if n_sub != 2 or per % 8 or 6 * width % n_dom:
        return slow_tail(
            count, blocks, came, names, chunk, h0, q0, recv, recv_t, send_t, slope0, edge_out,
            node_low, node_high, edge_high, tail, pred, nodes,
        )
    packed = ((n_dom, per + EXTRA, width), F32)
    mine, other = call(
        functools.partial(end_kernel, chunk, names),
        [packed, packed],
        *blocks, *came,
        h0, q0, recv, recv_t, send_t, slope0, edge_out, node_low, node_high, edge_high, tail,
    )
    swap = pairs(n_sub, 0)
    (halved,) = call(add_kernel, [packed], mine, lax.ppermute(other, "sub", swap))
    parts = lax.all_to_all(halved, "dom", 0, 0, tiled=True)
    (spread,) = call(total_kernel, [packed], parts)
    mine = lax.all_to_all(spread, "dom", 0, 0, tiled=True)
    other = lax.ppermute(mine, "sub", swap)
    params = 2 * 6 * width * width + width
    loss, g_edge_in, g_edge_out, g_node_in, g_node_out, g_decoder = call(
        functools.partial(scale_kernel, params, count),
        [
            ((1, width), F32),
            ((2, 2 * width, width), F32), ((2, width, width), F32),
            ((2, 2 * width, width), F32), ((2, width, width), F32),
            ((1, width), F32),
        ],
        mine, other,
    )
    return (
        loss[0, 0], pred.reshape(nodes), g_edge_in, g_edge_out, g_node_in, g_node_out,
        g_decoder.reshape(width),
    )


def low_kernel(chunk, names, *refs):
    own, refs = refs[:4], refs[4:]
    came, refs = unpack(names, refs)
    h, q, recv, recv_t, send_t, slope, edge_out, out = refs
    local_grad = take_sum(own, came)
    to_recv, to_send = edge_backward(local_grad, edge_out[0], recv, recv_t, send_t, slope, chunk)
    width = h.shape[1]
    out[0:width, :] = tmm(h[...], to_recv)
    out[width : 2 * width, :] = tmm(h[...], to_send)
    out[2 * width :, :] = tmm(q[...], local_grad)


def slow_tail(
    count, blocks, came, names, chunk, h0, q0, recv, recv_t, send_t, slope0, edge_out,
    node_low, node_high, edge_high, tail, pred, nodes,
):
    width = h0.shape[1]
    (edge_low,) = call(
        functools.partial(low_kernel, chunk, names), [((3 * width, width), F32)],
        *blocks, *came, h0, q0, recv, recv_t, send_t, slope0, edge_out,
    )
    total = lax.psum(
        jnp.concatenate([node_low, edge_low, node_high, edge_high, tail], 0), ("dom", "sub")
    )
    rows = 12 * width
    body = total[: rows + 1]
    params = (rows + 1) * width
    scale = 1.0 / jnp.sqrt(jnp.sum(body * body) / params + 1e-06)
    grads = (total[:rows] * scale).reshape(2, 2, 3 * width, width)
    return (
        total[rows + 1, 0] / count, pred.reshape(nodes),
        grads[:, 1, : 2 * width], grads[:, 1, 2 * width :],
        grads[:, 0, : 2 * width], grads[:, 0, 2 * width :],
        total[rows] * scale,
    )


def solution(mesh):
    placed = (
        P(("dom", "sub"), None),
        P(),
        P(),
        P(),
        P(),
        P(),
        P(None, ("dom", "sub")),
        P(("dom", "sub"), None, None),
        P(("dom", "sub")),
    )
    return jax.shard_map(
        per_device,
        mesh=mesh,
        in_specs=placed,
        out_specs=(P(), P(("dom", "sub")), P(), P(), P(), P(), P()),
        check_vma=False,
    )
```

profile of v0, /device:TPU:0, one launch (start us, length us, event | category | flops | bytes accessed | tf_op | source)
XLA Modules:
  0.0 110.7 jit_solution(1717516000347491916)
XLA Ops:
  0.6 3.9 %shard_map.144 = (f32[256,128]{1,0:T(8,128)}, bf16[1280,256]{1,0:T(8,128)(2,1)}, bf16[1280,256]{1,0:T(8,128)(2,1)}, bf16[256,1280]{1,0:T(8,128)(2,1)}, bf16[256,...) custom-call(f32[256,128]{1,0:T(8,128)} %feats.1, ...), custom_call_target="tpu_custom_call" | custom-call | tf_op jit(solution)/shard_map/pallas_call | solution.py:357
  4.5 3.0 %collective-permute-start = (f32[64,128]{1,0:T(8,128)}, f32[64,128]{1,0:T(8,128)S(1)}, u32[]{:S(2)}, u32[]{:S(2)}) collective-permute-start(f32[64,128]{1,0:T(8,128)} %get-tuple-element.57.refs_0_), channel_id=1, source_target_pairs={{0,2},{2,0},{4,6},{6,4},{8,10},{10,8},{12,14},{14,12},{16,18},{18,... | collective-permute-start | bytes 98312 | tf_op jit(solution)/shard_map/ppermute | solution.py:394
  8.2 1.4 %collective-permute-done.refs_4_ = f32[64,128]{1,0:T(8,128)S(1)} collective-permute-done((f32[64,128]{1,0:T(8,128)}, f32[64,128]{1,0:T(8,128)S(1)}, u32[]{:S(2)}, u32[]{:S(2)}) %collective-permute-start) | collective-permute-done | bytes 32800 | tf_op jit(solution)/shard_map/ppermute | solution.py:394
  10.3 4.3 %shard_map.145 = (f32[256,128]{1,0:T(8,128)}, f32[256,128]{1,0:T(8,128)}, f32[256,128]{1,0:T(8,128)}, f32[256,128]{1,0:T(8,128)}, f32[1280,128]{1,0:T(8,128)}, /...) custom-call(f32[64,128]{1,0:T(8,128)} %get-tuple-element.57.refs_0_, ...), custom_call_target="tpu_custom_call" | custom-call | tf_op jit(solution)/shard_map/pallas_call | solution.py:357
  14.5 4.9 %collective-permute-start.3 = (f32[64,128]{1,0:T(8,128)}, f32[64,128]{1,0:T(8,128)S(1)}, u32[]{:S(2)}, u32[]{:S(2)}) collective-permute-start(f32[64,128]{1,0:T(8,128)} %get-tuple-element.65.refs_0_), channel_id=1, source_target_pairs={{0,2},{2,0},{4,6},{6,4},{8,10},{10,8},{12,14},{14,12},{16,18},{18,... | collective-permute-start | bytes 98312 | tf_op jit(solution)/shard_map/ppermute | solution.py:394
  20.2 1.4 %collective-permute-done.3.refs_4_ = f32[64,128]{1,0:T(8,128)S(1)} collective-permute-done((f32[64,128]{1,0:T(8,128)}, f32[64,128]{1,0:T(8,128)S(1)}, u32[]{:S(2)}, u32[]{:S(2)}) %collective-permute-start.3) | collective-permute-done | bytes 32800 | tf_op jit(solution)/shard_map/ppermute | solution.py:394
  22.2 2.6 %shard_map.146 = (f32[256,128]{1,0:T(8,128)}, f32[256,128]{1,0:T(8,128)}, f32[256,128]{1,0:T(8,128)}, f32[256,128]{1,0:T(8,128)}, f32[256,128]{1,0:T(8,128)}, /*...) custom-call(f32[64,128]{1,0:T(8,128)} %get-tuple-element.65.refs_0_,, ...), custom_call_target="tpu_custom_call" | custom-call | tf_op jit(solution)/shard_map/pallas_call | solution.py:357
  24.8 6.3 %collective-permute-start.6 = (f32[64,128]{1,0:T(8,128)}, f32[64,128]{1,0:T(8,128)S(1)}, u32[]{:S(2)}, u32[]{:S(2)}) collective-permute-start(f32[64,128]{1,0:T(8,128)} %get-tuple-element.71.refs_0_), channel_id=1, source_target_pairs={{0,2},{2,0},{4,6},{6,4},{8,10},{10,8},{12,14},{14,12},{16,18},{18,... | collective-permute-start | bytes 98312 | tf_op jit(solution)/shard_map/ppermute | solution.py:394
  31.8 1.4 %collective-permute-done.6.refs_4_ = f32[64,128]{1,0:T(8,128)S(1)} collective-permute-done((f32[64,128]{1,0:T(8,128)}, f32[64,128]{1,0:T(8,128)S(1)}, u32[]{:S(2)}, u32[]{:S(2)}) %collective-permute-start.6) | collective-permute-done | bytes 32800 | tf_op jit(solution)/shard_map/ppermute | solution.py:394
  33.9 4.6 %shard_map.147 = (f32[256,128]{1,0:T(8,128)}, f32[256,128]{1,0:T(8,128)}, f32[256,128]{1,0:T(8,128)}, f32[256,128]{1,0:T(8,128)}, f32[256,128]{1,0:T(8,128)}, /*...) custom-call(f32[64,128]{1,0:T(8,128)} %get-tuple-element.71.refs_0_, ...), custom_call_target="tpu_custom_call" | custom-call | tf_op jit(solution)/shard_map/pallas_call | solution.py:357
  38.5 6.3 %collective-permute-start.9 = (f32[64,128]{1,0:T(8,128)}, f32[64,128]{1,0:T(8,128)S(1)}, u32[]{:S(2)}, u32[]{:S(2)}) collective-permute-start(f32[64,128]{1,0:T(8,128)} %get-tuple-element.79.refs_0_), channel_id=1, source_target_pairs={{0,2},{2,0},{4,6},{6,4},{8,10},{10,8},{12,14},{14,12},{16,18},{18,... | collective-permute-start | bytes 98312 | tf_op jit(solution)/shard_map/ppermute | solution.py:394
  45.6 2.2 %shard_map.149.refs_15_ = f32[384,128]{1,0:T(8,128)} custom-call(f32[256,128]{1,0:T(8,128)} %get-tuple-element.69.refs_7_.h, f32[256,128]{1,0:T(8,128)} %get-tuple-element.89.summed, f32[256,128]{1,0:T(8,128)} %get-tuple-element.90.act, f32[256,128]{1,0:T(8,128)} %get-tuple-element.91.pre_grad, f32[256,128]{1,0:T(8,128)} %get-tuple-element.92.top_grad), custom_call_target="tpu_custom_call" | custom-call | tf_op jit(solution)/shard_map/pallas_call | solution.py:357
  47.7 2.2 %shard_map.148.refs_14_ = f32[384,128]{1,0:T(8,128)} custom-call(f32[256,128]{1,0:T(8,128)} %get-tuple-element.61.refs_7_.h, f32[256,128]{1,0:T(8,128)} %get-tuple-element.85.summed, f32[256,128]{1,0:T(8,128)} %get-tuple-element.86.act, f32[256,128]{1,0:T(8,128)} %get-tuple-element.87.pre_grad, f32[256,128]{1,0:T(8,128)} %get-tuple-element.88.top_grad), custom_call_target="tpu_custom_call" | custom-call | tf_op jit(solution)/shard_map/pallas_call | solution.py:357
  49.9 2.1 %shard_map.150.refs_16_ = f32[384,128]{1,0:T(8,128)} custom-call(f32[256,128]{1,0:T(8,128)} %get-tuple-element.69.refs_7_.h, f32[256,128]{1,0:T(8,128)} %get-tuple-element.93.q, f32[256,128]{1,0:T(8,128)} %get-tuple-element.94.local_grad, f32[256,128]{1,0:T(8,128)} %get-tuple-element.95.to_recv, f32[256,128]{1,0:T(8,128)} %get-tuple-element.96.to_send), custom_call_target="tpu_custom_call" | custom-call | tf_op jit(solution)/shard_map/pallas_call | solution.py:357
  52.7 4.9 %shard_map.151 = (f32[16,56,128]{2,1,0:T(8,128)}, f32[16,56,128]{2,1,0:T(8,128)}) custom-call(f32[64,128]{1,0:T(8,128)} %get-tuple-element.79.refs_0_, f32[64,128]{1,0:T(8,128)} %get-tuple-element.80.refs_1_, f32[64,128]{1,0:T(8,128)} %get-tuple-element.81.refs_2_, f32[64,128]{1,0:T(8,128)} %get-tuple-element.82.refs_3_, f32[64,128]{1,0:T(8,128)} %copy-done.3, ...), custom_call_target="tpu_custom_call" | custom-call | tf_op jit(solution)/shard_map/pallas_call | solution.py:357
  58.1 1.7 %collective-permute-done.12.b = f32[16,56,128]{2,1,0:T(8,128)S(1)} collective-permute-done((f32[16,56,128]{2,1,0:T(8,128)}, f32[16,56,128]{2,1,0:T(8,128)S(1)}, u32[]{:S(2)}, u32[]{:S(2)}) %collective-permute-start.12) | collective-permute-done | bytes 458784 | tf_op jit(solution)/shard_map/ppermute | solution.py:450
  59.7 0.8 copy-done.2
  60.5 2.0 %shard_map.152 = f32[16,56,128]{2,1,0:T(8,128)} custom-call(f32[16,56,128]{2,1,0:T(8,128)} %get-tuple-element.98.a, f32[16,56,128]{2,1,0:T(8,128)} %copy-done.2), custom_call_target="tpu_custom_call" | custom-call | tf_op jit(solution)/shard_map/pallas_call | solution.py:357
  62.5 24.4 %all_to_all.10.parts = f32[16,56,128]{2,1,0:T(8,128)} all-to-all(f32[16,56,128]{2,1,0:T(8,128)} %shard_map.152), channel_id=1, replica_groups=mesh['dom'=16,'sub'=2] {'dom'}, dimensions={0} | all-to-all | bytes 917504 | tf_op jit(solution)/shard_map/all_to_all | solution.py:451
  86.9 1.9 %shard_map.153 = f32[16,56,128]{2,1,0:T(8,128)} custom-call(f32[16,56,128]{2,1,0:T(8,128)} %all_to_all.10.parts), custom_call_target="tpu_custom_call" | custom-call | tf_op jit(solution)/shard_map/pallas_call | solution.py:357
  88.8 17.1 %all_to_all.11.mine = f32[16,56,128]{2,1,0:T(8,128)S(1)} all-to-all(f32[16,56,128]{2,1,0:T(8,128)} %shard_map.153), channel_id=1, replica_groups=mesh['dom'=16,'sub'=2] {'dom'}, dimensions={0} | all-to-all | bytes 917504 | tf_op jit(solution)/shard_map/all_to_all | solution.py:453
  105.9 1.8 %collective-permute-done.13.other = f32[16,56,128]{2,1,0:T(8,128)S(1)} collective-permute-done((f32[16,56,128]{2,1,0:T(8,128)S(1)}, f32[16,56,128]{2,1,0:T(8,128)S(1)}, u32[]{:S(2)}, u32[]{:S(2)}) %collective-permute-start.13) | collective-permute-done | bytes 458784 | tf_op jit(solution)/shard_map/ppermute | solution.py:454
  107.7 0.8 copy-done.1
  108.5 2.1 %shard_map.154 = (f32[1,128]{1,0:T(1,128)}, f32[2,256,128]{2,1,0:T(8,128)}, f32[2,128,128]{2,1,0:T(8,128)}, f32[2,256,128]{2,1,0:T(8,128)}, f32[2,128,128]{2,1,0:T(8,128)}, /*index=5*/f32[1,128]{1,0:T(1,128)}) custom-call(f32[16,56,128]{2,1,0:T(8,128)} %copy-done, f32[16,56,128]{2,1,0:T(8,128)} %copy-done.1), custom_call_target="tpu_custom_call" | custom-call | tf_op jit(solution)/shard_map/pallas_call | solution.py:357
  (47 shorter events, 6.0 us)
Async XLA Ops:
  4.5 5.1 %collective-permute-start = (f32[64,128]{1,0:T(8,128)}, f32[64,128]{1,0:T(8,128)S(1)}, u32[]{:S(2)}, u32[]{:S(2)}) collective-permute-start(f32[64,128]{1,0:T(8,128)} %get-tuple-element.57.refs_0_), channel_id=1, source_target_pairs={{0,2},{2,0},{4,6},{6,4},{8,10},{10,8},{12,14},{14,12},{16,18},{18,... | collective-permute-start | bytes 98312 | tf_op jit(solution)/shard_map/ppermute | solution.py:394
  7.5 2.1 %collective-permute-start.1 = (f32[64,128]{1,0:T(8,128)}, f32[64,128]{1,0:T(8,128)S(1)}, u32[]{:S(2)}, u32[]{:S(2)}) collective-permute-start(f32[64,128]{1,0:T(8,128)} %get-tuple-element.58.refs_1_), channel_id=1, source_target_pairs={{2,4},{4,2},{6,8},{8,6},{10,12},{12,10},{14,16},{16,14},{18,20},{2... | collective-permute-start | bytes 98312 | tf_op jit(solution)/shard_map/ppermute | solution.py:394
  8.2 1.5 %collective-permute-start.2 = (f32[64,128]{1,0:T(8,128)}, f32[64,128]{1,0:T(8,128)S(1)}, u32[]{:S(2)}, u32[]{:S(2)}) collective-permute-start(f32[64,128]{1,0:T(8,128)} %get-tuple-element.59.refs_2_), channel_id=1, source_target_pairs={{0,1},{1,0},{2,3},{3,2},{4,5},{5,4},{6,7},{7,6},{8,9},{9,8},{10,11... | collective-permute-start | bytes 98312 | tf_op jit(solution)/shard_map/ppermute | solution.py:394
  9.6 0.6 copy-start.7
  9.6 0.6 copy-start.9
  14.5 7.0 %collective-permute-start.3 = (f32[64,128]{1,0:T(8,128)}, f32[64,128]{1,0:T(8,128)S(1)}, u32[]{:S(2)}, u32[]{:S(2)}) collective-permute-start(f32[64,128]{1,0:T(8,128)} %get-tuple-element.65.refs_0_), channel_id=1, source_target_pairs={{0,2},{2,0},{4,6},{6,4},{8,10},{10,8},{12,14},{14,12},{16,18},{18,... | collective-permute-start | bytes 98312 | tf_op jit(solution)/shard_map/ppermute | solution.py:394
  19.4 2.1 %collective-permute-start.4 = (f32[64,128]{1,0:T(8,128)}, f32[64,128]{1,0:T(8,128)S(1)}, u32[]{:S(2)}, u32[]{:S(2)}) collective-permute-start(f32[64,128]{1,0:T(8,128)} %get-tuple-element.66.refs_1_), channel_id=1, source_target_pairs={{2,4},{4,2},{6,8},{8,6},{10,12},{12,10},{14,16},{16,14},{18,20},{2... | collective-permute-start | bytes 98312 | tf_op jit(solution)/shard_map/ppermute | solution.py:394
  20.1 1.5 %collective-permute-start.5 = (f32[64,128]{1,0:T(8,128)}, f32[64,128]{1,0:T(8,128)S(1)}, u32[]{:S(2)}, u32[]{:S(2)}) collective-permute-start(f32[64,128]{1,0:T(8,128)} %get-tuple-element.67.refs_2_), channel_id=1, source_target_pairs={{0,1},{1,0},{2,3},{3,2},{4,5},{5,4},{6,7},{7,6},{8,9},{9,8},{10,11... | collective-permute-start | bytes 98312 | tf_op jit(solution)/shard_map/ppermute | solution.py:394
  21.6 0.6 copy-start.13
  24.8 8.4 %collective-permute-start.6 = (f32[64,128]{1,0:T(8,128)}, f32[64,128]{1,0:T(8,128)S(1)}, u32[]{:S(2)}, u32[]{:S(2)}) collective-permute-start(f32[64,128]{1,0:T(8,128)} %get-tuple-element.71.refs_0_), channel_id=1, source_target_pairs={{0,2},{2,0},{4,6},{6,4},{8,10},{10,8},{12,14},{14,12},{16,18},{18,... | collective-permute-start | bytes 98312 | tf_op jit(solution)/shard_map/ppermute | solution.py:394
  31.1 2.1 %collective-permute-start.7 = (f32[64,128]{1,0:T(8,128)}, f32[64,128]{1,0:T(8,128)S(1)}, u32[]{:S(2)}, u32[]{:S(2)}) collective-permute-start(f32[64,128]{1,0:T(8,128)} %get-tuple-element.72.refs_1_), channel_id=1, source_target_pairs={{2,4},{4,2},{6,8},{8,6},{10,12},{12,10},{14,16},{16,14},{18,20},{2... | collective-permute-start | bytes 98312 | tf_op jit(solution)/shard_map/ppermute | solution.py:394
  31.8 1.5 %collective-permute-start.8 = (f32[64,128]{1,0:T(8,128)}, f32[64,128]{1,0:T(8,128)S(1)}, u32[]{:S(2)}, u32[]{:S(2)}) collective-permute-start(f32[64,128]{1,0:T(8,128)} %get-tuple-element.73.refs_2_), channel_id=1, source_target_pairs={{0,1},{1,0},{2,3},{3,2},{4,5},{5,4},{6,7},{7,6},{8,9},{9,8},{10,11... | collective-permute-start | bytes 98312 | tf_op jit(solution)/shard_map/ppermute | solution.py:394
  33.2 0.6 copy-start.8
  33.3 0.6 copy-start.10
  38.5 13.5 %collective-permute-start.9 = (f32[64,128]{1,0:T(8,128)}, f32[64,128]{1,0:T(8,128)S(1)}, u32[]{:S(2)}, u32[]{:S(2)}) collective-permute-start(f32[64,128]{1,0:T(8,128)} %get-tuple-element.79.refs_0_), channel_id=1, source_target_pairs={{0,2},{2,0},{4,6},{6,4},{8,10},{10,8},{12,14},{14,12},{16,18},{18,... | collective-permute-start | bytes 98312 | tf_op jit(solution)/shard_map/ppermute | solution.py:394
  44.8 7.2 %collective-permute-start.10 = (f32[64,128]{1,0:T(8,128)}, f32[64,128]{1,0:T(8,128)S(1)}, u32[]{:S(2)}, u32[]{:S(2)}) collective-permute-start(f32[64,128]{1,0:T(8,128)} %get-tuple-element.80.refs_1_), channel_id=1, source_target_pairs={{2,4},{4,2},{6,8},{8,6},{10,12},{12,10},{14,16},{16,14},{18,20},{2... | collective-permute-start | bytes 98312 | tf_op jit(solution)/shard_map/ppermute | solution.py:394
  45.5 6.6 %collective-permute-start.11 = (f32[64,128]{1,0:T(8,128)}, f32[64,128]{1,0:T(8,128)S(1)}, u32[]{:S(2)}, u32[]{:S(2)}) collective-permute-start(f32[64,128]{1,0:T(8,128)} %get-tuple-element.81.refs_2_), channel_id=1, source_target_pairs={{0,1},{1,0},{2,3},{3,2},{4,5},{5,4},{6,7},{7,6},{8,9},{9,8},{10,11... | collective-permute-start | bytes 98312 | tf_op jit(solution)/shard_map/ppermute | solution.py:394
  52.0 0.6 copy-start.3
  52.0 0.6 copy-start.4
  57.6 2.2 %collective-permute-start.12 = (f32[16,56,128]{2,1,0:T(8,128)}, f32[16,56,128]{2,1,0:T(8,128)S(1)}, u32[]{:S(2)}, u32[]{:S(2)}) collective-permute-start(f32[16,56,128]{2,1,0:T(8,128)} %get-tuple-element.99), channel_id=1, source_target_pairs={{0,1},{1,0},{2,3},{3,2},{4,5},{5,4},{6,7},{7,6},{8,9},{9,8},{10,11... | collective-permute-start | bytes 1376264 | tf_op jit(solution)/shard_map/ppermute | solution.py:450
  59.7 0.8 copy-start.2
  105.9 1.8 %copy-start = (f32[16,56,128]{2,1,0:T(8,128)}, f32[16,56,128]{2,1,0:T(8,128)S(1)}, u32[]{:S(2)}) copy-start(f32[16,56,128]{2,1,0:T(8,128)S(1)} %all_to_all.11.mine) | copy-start | bytes 1376260
  105.9 1.8 %collective-permute-start.13 = (f32[16,56,128]{2,1,0:T(8,128)S(1)}, f32[16,56,128]{2,1,0:T(8,128)S(1)}, u32[]{:S(2)}, u32[]{:S(2)}) collective-permute-start(f32[16,56,128]{2,1,0:T(8,128)S(1)} %all_to_all.11.mine), channel_id=1, source_target_pairs={{0,1},{1,0},{2,3},{3,2},{4,5},{5,4},{6,7},{7,6},{8,9},{9,8},{10,11... | collective-permute-start | bytes 1376264 | tf_op jit(solution)/shard_map/ppermute | solution.py:454
  107.7 0.8 copy-start.1
  (5 other events, 3.0 us)
where the time goes:
time: 111 us
  blocking collectives  41.5 us (37%)
  Pallas kernels  32.8 us (30%)
  starting transfers between devices  23.9 us (22%)
  waiting for transfers between devices  7.68 us (7%)
  local copies, waits for them, and re-layouts  4.03 us (4%)
    pallas_call x11, Pallas kernels, call(): pl.pallas_call(kernel, out_shape=shapes, in_specs=[VMEM] * len(args), out...  32.8 us
    all_to_all x1, blocking collectives, per_device(): parts = lax.all_to_all(halved, 'dom', 0, 0, tiled=True)  24.4 us
    ppermute x12, starting transfers between devices, exchange(): came[at] = lax.ppermute(blocks[at], axes[at], links[at])  23.4 us
    all_to_all x1, blocking collectives, per_device(): mine = lax.all_to_all(spread, 'dom', 0, 0, tiled=True)  17.1 us
    ppermute x12, waiting for transfers between devices, exchange(): came[at] = lax.ppermute(blocks[at], axes[at], links[at])  4.21 us
    unnamed x30, local copies, waits for them, and re-layouts  4.03 us
  transfers between devices with their start and end apart: 14, of which 5 were waited for; matrix products, arithmetic and copies ran while one was open for 0% of the time, Pallas kernels for 6%

commit v1 on v0

--- a/solution.py
+++ b/solution.py
@@ -359,6 +359,7 @@
         out_shape=shapes,
         in_specs=[VMEM] * len(args),
         out_specs=[VMEM] * len(shapes),
+        compiler_params=pltpu.CompilerParams(vmem_limit_bytes=16 * 2**20),
     )(*args)
 
 

time: 111 us -> 91.5 us (0.82)
  Pallas kernels: 32.8 us -> 10.9 us
  local copies, waits for them, and re-layouts: 4.03 us -> 5.73 us
  blocking collectives: 41.5 us -> 42.8 us
    pallas_call x11, Pallas kernels: 32.8 us -> 10.9 us  [call(): pl.pallas_call(kernel, out_shape=shapes, in_specs=[VMEM] * len(args), out...]
    unnamed x30 -> x24, local copies, waits for them, and re-layouts: 4.03 us -> 5.73 us
    all_to_all x1, blocking collectives: 24.4 us -> 26 us  [per_device(): parts = lax.all_to_all(halved, 'dom', 0, 0, tiled=True)]
  transfers between devices with their start and end apart: 14 -> 14, of which waited for: 5 -> 6; matrix products, arithmetic and copies ran while one was open for 0% -> 0% of each run, Pallas kernels for 6% -> 1%
where the time goes in v1:
time: 91.5 us; the launch traced here: 91.1 us
  blocking collectives  42.8 us (47%)
  starting transfers between devices  23.7 us (26%)
  Pallas kernels  10.9 us (12%)
  waiting for transfers between devices  7.12 us (8%)
  local copies, waits for them, and re-layouts  5.73 us (6%)
    all_to_all x1, blocking collectives, per_device(): parts = lax.all_to_all(halved, 'dom', 0, 0, tiled=True)  26 us
    ppermute x12, starting transfers between devices, exchange(): came[at] = lax.ppermute(blocks[at], axes[at], links[at])  23.4 us
    all_to_all x1, blocking collectives, per_device(): mine = lax.all_to_all(spread, 'dom', 0, 0, tiled=True)  16.8 us
    pallas_call x11, Pallas kernels, call(): pl.pallas_call(kernel, out_shape=shapes, in_specs=[VMEM] * len(args), out...  10.9 us
    unnamed x24, local copies, waits for them, and re-layouts  5.73 us
    ppermute x12, waiting for transfers between devices, exchange(): came[at] = lax.ppermute(blocks[at], axes[at], links[at])  3.81 us
  transfers between devices with their start and end apart: 14, of which 6 were waited for; matrix products, arithmetic and copies ran while one was open for 0% of the time, Pallas kernels for 1%

profile of v1, /device:TPU:0, one launch (start us, length us, event | category | flops | bytes accessed | tf_op | source)
XLA Modules:
  0.0 91.1 jit_solution(17001246641979229846)
XLA Ops:
  0.6 0.9 %copy-done = f32[2,256,128]{2,1,0:T(8,128)S(1)} copy-done((f32[2,256,128]{2,1,0:T(8,128)S(1)}, f32[2,256,128]{2,1,0:T(8,128)}, u32[]{:S(2)}) %copy-start) | copy-done | bytes 262168
  1.6 0.9 copy-done.3
  2.5 0.9 copy-done.7
  3.4 0.7 copy-done.8
  4.1 0.7 copy-done.9
  4.8 2.0 %shard_map.144 = (f32[256,128]{1,0:T(8,128)S(1)}, bf16[1280,256]{1,0:T(8,128)(2,1)S(1)}, bf16[1280,256]{1,0:T(8,128)(2,1)S(1)}, bf16[256,1280]{1,0:T(8,128)(2,1)...) custom-call(f32[256,128]{1,0:T(8,128)S(1)} %copy-done.7, ...), custom_call_target="tpu_custom_call" | custom-call | tf_op jit(solution)/shard_map/pallas_call | solution.py:357
  6.8 3.0 %collective-permute-start = (f32[64,128]{1,0:T(8,128)S(1)}, f32[64,128]{1,0:T(8,128)S(1)}, u32[]{:S(2)}, u32[]{:S(2)}) collective-permute-start(f32[64,128]{1,0:T(8,128)S(1)} %get-tuple-element.57.refs_0_), channel_id=1, source_target_pairs={{0,2},{2,0},{4,6},{6,4},{8,10},{10,8},{12,14},{14,12},{16,18},{18,... | collective-permute-start | bytes 98312 | tf_op jit(solution)/shard_map/ppermute | solution.py:395
  10.5 1.2 %collective-permute-done.refs_4_ = f32[64,128]{1,0:T(8,128)S(1)} collective-permute-done((f32[64,128]{1,0:T(8,128)S(1)}, f32[64,128]{1,0:T(8,128)S(1)}, u32[]{:S(2)}, u32[]{:S(2)}) %collective-permute-start) | collective-permute-done | bytes 32800 | tf_op jit(solution)/shard_map/ppermute | solution.py:395
  11.7 0.9 copy-done.5
  12.6 1.8 %shard_map.145 = (f32[256,128]{1,0:T(8,128)S(1)}, f32[256,128]{1,0:T(8,128)S(1)}, f32[256,128]{1,0:T(8,128)S(1)}, f32[256,128]{1,0:T(8,128)S(1)}, f32[1280,128]{...) custom-call(f32[64,128]{1,0:T(8,128)S(1)} %get-tuple-element.57.refs, ...), custom_call_target="tpu_custom_call" | custom-call | tf_op jit(solution)/shard_map/pallas_call | solution.py:357
  14.4 4.9 %collective-permute-start.3 = (f32[64,128]{1,0:T(8,128)S(1)}, f32[64,128]{1,0:T(8,128)S(1)}, u32[]{:S(2)}, u32[]{:S(2)}) collective-permute-start(f32[64,128]{1,0:T(8,128)S(1)} %get-tuple-element.65.refs_0_), channel_id=1, source_target_pairs={{0,2},{2,0},{4,6},{6,4},{8,10},{10,8},{12,14},{14,12},{16,18},{18,... | collective-permute-start | bytes 98312 | tf_op jit(solution)/shard_map/ppermute | solution.py:395
  20.1 1.2 %collective-permute-done.3.refs_4_ = f32[64,128]{1,0:T(8,128)S(1)} collective-permute-done((f32[64,128]{1,0:T(8,128)S(1)}, f32[64,128]{1,0:T(8,128)S(1)}, u32[]{:S(2)}, u32[]{:S(2)}) %collective-permute-start.3) | collective-permute-done | bytes 32800 | tf_op jit(solution)/shard_map/ppermute | solution.py:395
  21.3 0.7 copy-done.10
  22.0 1.2 %shard_map.146 = (f32[256,128]{1,0:T(8,128)S(1)}, f32[256,128]{1,0:T(8,128)S(1)}, f32[256,128]{1,0:T(8,128)S(1)}, f32[256,128]{1,0:T(8,128)S(1)}, f32[256,128]{1...) custom-call(f32[64,128]{1,0:T(8,128)S(1)} %get-tuple-element.65.refs, ...), custom_call_target="tpu_custom_call" | custom-call | tf_op jit(solution)/shard_map/pallas_call | solution.py:357
  23.2 6.2 %collective-permute-start.6 = (f32[64,128]{1,0:T(8,128)S(1)}, f32[64,128]{1,0:T(8,128)S(1)}, u32[]{:S(2)}, u32[]{:S(2)}) collective-permute-start(f32[64,128]{1,0:T(8,128)S(1)} %get-tuple-element.71.refs_0_), channel_id=1, source_target_pairs={{0,2},{2,0},{4,6},{6,4},{8,10},{10,8},{12,14},{14,12},{16,18},{18,... | collective-permute-start | bytes 98312 | tf_op jit(solution)/shard_map/ppermute | solution.py:395
  30.1 1.2 %collective-permute-done.6.refs_4_ = f32[64,128]{1,0:T(8,128)S(1)} collective-permute-done((f32[64,128]{1,0:T(8,128)S(1)}, f32[64,128]{1,0:T(8,128)S(1)}, u32[]{:S(2)}, u32[]{:S(2)}) %collective-permute-start.6) | collective-permute-done | bytes 32800 | tf_op jit(solution)/shard_map/ppermute | solution.py:395
  31.3 1.9 %shard_map.147 = (f32[256,128]{1,0:T(8,128)S(1)}, f32[256,128]{1,0:T(8,128)S(1)}, f32[256,128]{1,0:T(8,128)S(1)}, f32[256,128]{1,0:T(8,128)S(1)}, f32[256,128]{1...) custom-call(f32[64,128]{1,0:T(8,128)S(1)} %get-tuple-element.71.refs, ...), custom_call_target="tpu_custom_call" | custom-call | tf_op jit(solution)/shard_map/pallas_call | solution.py:357
  33.3 6.3 %collective-permute-start.9 = (f32[64,128]{1,0:T(8,128)S(1)}, f32[64,128]{1,0:T(8,128)S(1)}, u32[]{:S(2)}, u32[]{:S(2)}) collective-permute-start(f32[64,128]{1,0:T(8,128)S(1)} %get-tuple-element.79.refs_0_), channel_id=1, source_target_pairs={{0,2},{2,0},{4,6},{6,4},{8,10},{10,8},{12,14},{14,12},{16,18},{18,... | collective-permute-start | bytes 98312 | tf_op jit(solution)/shard_map/ppermute | solution.py:395
  41.5 1.9 %shard_map.151 = (f32[16,56,128]{2,1,0:T(8,128)S(1)}, f32[16,56,128]{2,1,0:T(8,128)S(1)}) custom-call(f32[64,128]{1,0:T(8,128)S(1)} %get-tuple-element.79.refs_0_, f32[64,128]{1,0:T(8,128)S(1)} %get-tuple-element.80.refs_1_, f32[64,128]{1,0:T(8,128)S(1)} %get-tuple-element.81.refs_2_, f32[64,128]{1,0:T(8,128)S(1)} %get-tuple-element.82.refs_3_, ...), custom_call_target="tpu_custom_call" | custom-call | tf_op jit(solution)/shard_map/pallas_call | solution.py:357
  43.8 1.5 %collective-permute-done.12.b = f32[16,56,128]{2,1,0:T(8,128)S(1)} collective-permute-done((f32[16,56,128]{2,1,0:T(8,128)S(1)}, f32[16,56,128]{2,1,0:T(8,128)S(1)}, u32[]{:S(2)}, u32[]{:S(2)}) %collective-permute-start.12) | collective-permute-done | bytes 458784 | tf_op jit(solution)/shard_map/ppermute | solution.py:451
  45.3 26.0 %all_to_all.10.parts = f32[16,56,128]{2,1,0:T(8,128)S(1)} all-to-all(f32[16,56,128]{2,1,0:T(8,128)S(1)} %shard_map.152), channel_id=1, replica_groups=mesh['dom'=16,'sub'=2] {'dom'}, dimensions={0} | all-to-all | bytes 917504 | tf_op jit(solution)/shard_map/all_to_all | solution.py:452
  71.5 16.8 %all_to_all.11.mine = f32[16,56,128]{2,1,0:T(8,128)S(1)} all-to-all(f32[16,56,128]{2,1,0:T(8,128)S(1)} %shard_map.153), channel_id=1, replica_groups=mesh['dom'=16,'sub'=2] {'dom'}, dimensions={0} | all-to-all | bytes 917504 | tf_op jit(solution)/shard_map/all_to_all | solution.py:454
  88.3 1.8 %collective-permute-done.13.other = f32[16,56,128]{2,1,0:T(8,128)S(1)} collective-permute-done((f32[16,56,128]{2,1,0:T(8,128)S(1)}, f32[16,56,128]{2,1,0:T(8,128)S(1)}, u32[]{:S(2)}, u32[]{:S(2)}) %collective-permute-start.13) | collective-permute-done | bytes 458784 | tf_op jit(solution)/shard_map/ppermute | solution.py:455
  90.1 1.0 %shard_map.154 = (f32[1,128]{1,0:T(1,128)}, f32[2,256,128]{2,1,0:T(8,128)}, f32[2,128,128]{2,1,0:T(8,128)}, f32[2,256,128]{2,1,0:T(8,128)}, f32[2,128,128]{2,1,0:T(8,128)}, /*index=5*/f32[1,128]{1,0:T(1,128)}) custom-call(f32[16,56,128]{2,1,0:T(8,128)S(1)} %all_to_all.11.mine, f32[16,56,128]{2,1,0:T(8,128)S(1)} %collective-permute-done.13.other), custom_call_target="tpu_custom_call" | custom-call | tf_op jit(solution)/shard_map/pallas_call | solution.py:357
  (41 shorter events, 4.8 us)
Async XLA Ops:
  0.6 1.0 %copy-start = (f32[2,256,128]{2,1,0:T(8,128)S(1)}, f32[2,256,128]{2,1,0:T(8,128)}, u32[]{:S(2)}) copy-start(f32[2,256,128]{2,1,0:T(8,128)} %refs_13_.4) | copy-start | bytes 786436
  1.6 0.9 copy-start.3
  2.5 0.9 copy-start.7
  3.4 0.7 copy-start.8
  4.1 0.7 copy-start.9
  4.8 6.9 %copy-start.1 = (f32[2,256,128]{2,1,0:T(8,128)S(1)}, f32[2,256,128]{2,1,0:T(8,128)}, u32[]{:S(2)}) copy-start(f32[2,256,128]{2,1,0:T(8,128)} %refs_13_.4) | copy-start | bytes 786436
  4.8 6.9 %copy-start.2 = (f32[2,256,128]{2,1,0:T(8,128)S(1)}, f32[2,256,128]{2,1,0:T(8,128)}, u32[]{:S(2)}) copy-start(f32[2,256,128]{2,1,0:T(8,128)} %refs_15_.1) | copy-start | bytes 786436
  6.8 4.9 %collective-permute-start = (f32[64,128]{1,0:T(8,128)S(1)}, f32[64,128]{1,0:T(8,128)S(1)}, u32[]{:S(2)}, u32[]{:S(2)}) collective-permute-start(f32[64,128]{1,0:T(8,128)S(1)} %get-tuple-element.57.refs_0_), channel_id=1, source_target_pairs={{0,2},{2,0},{4,6},{6,4},{8,10},{10,8},{12,14},{14,12},{16,18},{18,... | collective-permute-start | bytes 98312 | tf_op jit(solution)/shard_map/ppermute | solution.py:395
  9.8 1.9 %collective-permute-start.1 = (f32[64,128]{1,0:T(8,128)S(1)}, f32[64,128]{1,0:T(8,128)S(1)}, u32[]{:S(2)}, u32[]{:S(2)}) collective-permute-start(f32[64,128]{1,0:T(8,128)S(1)} %get-tuple-element.58.refs_1_), channel_id=1, source_target_pairs={{2,4},{4,2},{6,8},{8,6},{10,12},{12,10},{14,16},{16,14},{18,20},{2... | collective-permute-start | bytes 98312 | tf_op jit(solution)/shard_map/ppermute | solution.py:395
  10.4 1.3 %collective-permute-start.2 = (f32[64,128]{1,0:T(8,128)S(1)}, f32[64,128]{1,0:T(8,128)S(1)}, u32[]{:S(2)}, u32[]{:S(2)}) collective-permute-start(f32[64,128]{1,0:T(8,128)S(1)} %get-tuple-element.59.refs_2_), channel_id=1, source_target_pairs={{0,1},{1,0},{2,3},{3,2},{4,5},{5,4},{6,7},{7,6},{8,9},{9,8},{10,11... | collective-permute-start | bytes 98312 | tf_op jit(solution)/shard_map/ppermute | solution.py:395
  11.7 0.9 copy-start.5
  14.4 6.8 %collective-permute-start.3 = (f32[64,128]{1,0:T(8,128)S(1)}, f32[64,128]{1,0:T(8,128)S(1)}, u32[]{:S(2)}, u32[]{:S(2)}) collective-permute-start(f32[64,128]{1,0:T(8,128)S(1)} %get-tuple-element.65.refs_0_), channel_id=1, source_target_pairs={{0,2},{2,0},{4,6},{6,4},{8,10},{10,8},{12,14},{14,12},{16,18},{18,... | collective-permute-start | bytes 98312 | tf_op jit(solution)/shard_map/ppermute | solution.py:395
  19.3 1.9 %collective-permute-start.4 = (f32[64,128]{1,0:T(8,128)S(1)}, f32[64,128]{1,0:T(8,128)S(1)}, u32[]{:S(2)}, u32[]{:S(2)}) collective-permute-start(f32[64,128]{1,0:T(8,128)S(1)} %get-tuple-element.66.refs_1_), channel_id=1, source_target_pairs={{2,4},{4,2},{6,8},{8,6},{10,12},{12,10},{14,16},{16,14},{18,20},{2... | collective-permute-start | bytes 98312 | tf_op jit(solution)/shard_map/ppermute | solution.py:395
  20.0 1.3 %collective-permute-start.5 = (f32[64,128]{1,0:T(8,128)S(1)}, f32[64,128]{1,0:T(8,128)S(1)}, u32[]{:S(2)}, u32[]{:S(2)}) collective-permute-start(f32[64,128]{1,0:T(8,128)S(1)} %get-tuple-element.67.refs_2_), channel_id=1, source_target_pairs={{0,1},{1,0},{2,3},{3,2},{4,5},{5,4},{6,7},{7,6},{8,9},{9,8},{10,11... | collective-permute-start | bytes 98312 | tf_op jit(solution)/shard_map/ppermute | solution.py:395
  22.0 9.4 %copy-start.4 = (f32[2,128,128]{2,1,0:T(8,128)S(1)}, f32[2,128,128]{2,1,0:T(8,128)}, u32[]{:S(2)}) copy-start(f32[2,128,128]{2,1,0:T(8,128)} %refs_13_.5) | copy-start | bytes 393220
  22.0 9.4 %copy-start.6 = (f32[2,128,128]{2,1,0:T(8,128)S(1)}, f32[2,128,128]{2,1,0:T(8,128)}, u32[]{:S(2)}) copy-start(f32[2,128,128]{2,1,0:T(8,128)} %refs_16_.1) | copy-start | bytes 393220
  23.2 8.1 %collective-permute-start.6 = (f32[64,128]{1,0:T(8,128)S(1)}, f32[64,128]{1,0:T(8,128)S(1)}, u32[]{:S(2)}, u32[]{:S(2)}) collective-permute-start(f32[64,128]{1,0:T(8,128)S(1)} %get-tuple-element.71.refs_0_), channel_id=1, source_target_pairs={{0,2},{2,0},{4,6},{6,4},{8,10},{10,8},{12,14},{14,12},{16,18},{18,... | collective-permute-start | bytes 98312 | tf_op jit(solution)/shard_map/ppermute | solution.py:395
  29.4 1.9 %collective-permute-start.7 = (f32[64,128]{1,0:T(8,128)S(1)}, f32[64,128]{1,0:T(8,128)S(1)}, u32[]{:S(2)}, u32[]{:S(2)}) collective-permute-start(f32[64,128]{1,0:T(8,128)S(1)} %get-tuple-element.72.refs_1_), channel_id=1, source_target_pairs={{2,4},{4,2},{6,8},{8,6},{10,12},{12,10},{14,16},{16,14},{18,20},{2... | collective-permute-start | bytes 98312 | tf_op jit(solution)/shard_map/ppermute | solution.py:395
  30.0 1.3 %collective-permute-start.8 = (f32[64,128]{1,0:T(8,128)S(1)}, f32[64,128]{1,0:T(8,128)S(1)}, u32[]{:S(2)}, u32[]{:S(2)}) collective-permute-start(f32[64,128]{1,0:T(8,128)S(1)} %get-tuple-element.73.refs_2_), channel_id=1, source_target_pairs={{0,1},{1,0},{2,3},{3,2},{4,5},{5,4},{6,7},{7,6},{8,9},{9,8},{10,11... | collective-permute-start | bytes 98312 | tf_op jit(solution)/shard_map/ppermute | solution.py:395
  33.3 8.2 %collective-permute-start.9 = (f32[64,128]{1,0:T(8,128)S(1)}, f32[64,128]{1,0:T(8,128)S(1)}, u32[]{:S(2)}, u32[]{:S(2)}) collective-permute-start(f32[64,128]{1,0:T(8,128)S(1)} %get-tuple-element.79.refs_0_), channel_id=1, source_target_pairs={{0,2},{2,0},{4,6},{6,4},{8,10},{10,8},{12,14},{14,12},{16,18},{18,... | collective-permute-start | bytes 98312 | tf_op jit(solution)/shard_map/ppermute | solution.py:395
  39.6 1.9 %collective-permute-start.10 = (f32[64,128]{1,0:T(8,128)S(1)}, f32[64,128]{1,0:T(8,128)S(1)}, u32[]{:S(2)}, u32[]{:S(2)}) collective-permute-start(f32[64,128]{1,0:T(8,128)S(1)} %get-tuple-element.80.refs_1_), channel_id=1, source_target_pairs={{2,4},{4,2},{6,8},{8,6},{10,12},{12,10},{14,16},{16,14},{18,20},{2... | collective-permute-start | bytes 98312 | tf_op jit(solution)/shard_map/ppermute | solution.py:395
  40.2 1.3 %collective-permute-start.11 = (f32[64,128]{1,0:T(8,128)S(1)}, f32[64,128]{1,0:T(8,128)S(1)}, u32[]{:S(2)}, u32[]{:S(2)}) collective-permute-start(f32[64,128]{1,0:T(8,128)S(1)} %get-tuple-element.81.refs_2_), channel_id=1, source_target_pairs={{0,1},{1,0},{2,3},{3,2},{4,5},{5,4},{6,7},{7,6},{8,9},{9,8},{10,11... | collective-permute-start | bytes 98312 | tf_op jit(solution)/shard_map/ppermute | solution.py:395
  43.4 1.9 %collective-permute-start.12 = (f32[16,56,128]{2,1,0:T(8,128)S(1)}, f32[16,56,128]{2,1,0:T(8,128)S(1)}, u32[]{:S(2)}, u32[]{:S(2)}) collective-permute-start(f32[16,56,128]{2,1,0:T(8,128)S(1)} %get-tuple-element.99), channel_id=1, source_target_pairs={{0,1},{1,0},{2,3},{3,2},{4,5},{5,4},{6,7},{7,6},{8,9},{9,8},{10,11... | collective-permute-start | bytes 1376264 | tf_op jit(solution)/shard_map/ppermute | solution.py:451
  88.3 1.8 %collective-permute-start.13 = (f32[16,56,128]{2,1,0:T(8,128)S(1)}, f32[16,56,128]{2,1,0:T(8,128)S(1)}, u32[]{:S(2)}, u32[]{:S(2)}) collective-permute-start(f32[16,56,128]{2,1,0:T(8,128)S(1)} %all_to_all.11.mine), channel_id=1, source_target_pairs={{0,1},{1,0},{2,3},{3,2},{4,5},{5,4},{6,7},{7,6},{8,9},{9,8},{10,11... | collective-permute-start | bytes 1376264 | tf_op jit(solution)/shard_map/ppermute | solution.py:455
  (2 other events, 1.4 us)

commit v2 on v1

--- a/solution.py
+++ b/solution.py
@@ -120,9 +120,25 @@
 
 
 def first_kernel(
-    chunk, feats, index, halo, weight_in, weight_out,
-    flat_out, recv, send, recv_t, send_t, h_out, slope, q_out, *blocks
+    chunk, feats_hbm, index_hbm, halo_hbm, target_hbm, decoder_hbm, *refs
 ):
+    weights_hbm, refs = refs[:4], refs[4:]
+    (target, decoder, edge_in, edge_out, node_in, node_out,
+     flat_out, recv, send, recv_t, send_t, h_out, slope, q_out) = refs[:14]
+    blocks, (feats, index, halo, sems) = refs[14:18], refs[18:]
+    copies = [
+        pltpu.make_async_copy(source, place, sems.at[at])
+        for at, (source, place) in enumerate(
+            zip(
+                (index_hbm, halo_hbm, feats_hbm, *weights_hbm, target_hbm, decoder_hbm),
+                (index, halo, feats, edge_in, edge_out, node_in, node_out, target, decoder),
+            )
+        )
+    ]
+    for copy in copies:
+        copy.start()
+    copies[0].wait()
+    copies[1].wait()
     nodes = feats.shape[0]
     edges = index.shape[1]
     lanes = 128
@@ -154,29 +170,16 @@
         recv_t[:, rows] = onehot(flat == table[b : b + 1])
         send_t[:, rows] = onehot(flat == table[count + b : count + b + 1])
     place = onehot(flat == lax.broadcasted_iota(jnp.int32, (nodes, nodes), 1).astype(F32))
+    copies[2].wait()
     features = fold(dot(place, side(feats[...])))
     h_out[...] = features
-    q = edge_forward(features, weight_in[0], recv, send, recv_t, slope, chunk)
+    copies[3].wait()
+    q = edge_forward(features, edge_in[0], recv, send, recv_t, slope, chunk)
     q_out[...] = q
-    put_blocks(mm(q, weight_out[0]), blocks)
-
-
-def middle_kernel(
-    chunk, layer, names, *refs
-):
-    own, refs = refs[:4], refs[4:]
-    came, refs = unpack(names, refs)
-    (h, recv, send, recv_t, node_in, node_out, edge_in, edge_out,
-     agg_out, h_out, node_act, node_slope, slope, q_out, *blocks) = refs
-    summed = take_sum(own, came)
-    agg_out[...] = summed
-    features, act, gate = node_forward(h[...], summed, node_in[layer], node_out[layer])
-    h_out[...] = features
-    node_act[...] = act
-    node_slope[...] = gate
-    q = edge_forward(features, edge_in[layer + 1], recv, send, recv_t, slope, chunk)
-    q_out[...] = q
-    put_blocks(mm(q, edge_out[layer + 1]), blocks)
+    copies[4].wait()
+    put_blocks(mm(q, edge_out[0]), blocks)
+    for copy in copies[5:]:
+        copy.wait()
 
 
 def unpack(names, refs):
@@ -188,79 +191,143 @@
     return came, refs[at:]
 
 
-def last_kernel(
-    layer, count, names, *refs
-):
+def middle_kernel(chunk, names, *refs):
     own, refs = refs[:4], refs[4:]
     came, refs = unpack(names, refs)
-    (h, flat_ref, target, decoder, node_in, node_out,
-     agg_out, node_act, pre_grad_out, top_grad_out, through_out, pred_out, tail_out, *blocks) = refs
+    (h, flat_ref, target, decoder, recv, send, recv_t, node_in, node_out, edge_in, edge_out,
+     agg_out, h_out, node_act, node_slope, slope, q_out, pre_out, known_out, *messages) = refs
     nodes, width = h.shape
     summed = take_sum(own, came)
     agg_out[...] = summed
-    features, act, gate = node_forward(h[...], summed, node_in[layer], node_out[layer])
+    features, act, gate = node_forward(h[...], summed, node_in[0], node_out[0])
+    h_out[...] = features
     node_act[...] = act
+    node_slope[...] = gate
+    pre = mm(features, node_in[1, :width])
+    pre_out[...] = pre
+    base = jnp.sum(features * decoder[...], axis=1, keepdims=True)
+    here = flat_ref[:, 0:1] == lax.broadcasted_iota(jnp.int32, (nodes, nodes), 1).astype(F32)
+    wanted = jnp.sum(jnp.where(here, target[...], 0.0), axis=1, keepdims=True)
+    first = lax.broadcasted_iota(jnp.int32, (nodes, width), 1) == 0
+    known_out[...] = jnp.where(first, base, wanted)
+    size = own[0].shape[0]
+    short = base - wanted
+    for at, message in enumerate(messages):
+        rows = slice(at * size, (at + 1) * size)
+        message[size : 2 * size, :] = pre[rows]
+        line = row_of(short[rows])
+        line = jnp.concatenate([line, jnp.zeros((1, width - size), F32)], axis=1)
+        message[2 * size :, :] = jnp.concatenate(
+            [line, jnp.ones((1, width), F32), jnp.zeros((EXTRA - 2, width), F32)], axis=0
+        )
+    q = edge_forward(features, edge_in[1], recv, send, recv_t, slope, chunk)
+    q_out[...] = q
+    local = mm(q, edge_out[1])
+    for at, message in enumerate(messages):
+        message[:size, :] = local[at * size : (at + 1) * size]
+
+
+def column_of(row):
+    n = row.shape[1]
+    eye = lax.broadcasted_iota(jnp.int32, (n, n), 0) == lax.broadcasted_iota(jnp.int32, (n, n), 1)
+    return jnp.sum(jnp.where(eye, row, 0.0), axis=1, keepdims=True)
+
+
+def row_product(row, weight):
+    return mm(jnp.broadcast_to(row, (8, row.shape[1])), weight)[0:1]
+
+
+def back_kernel(chunk, count, names, *refs):
+    own, refs = refs[:4], refs[4:]
+    came, refs = unpack(names, refs)
+    (flat_ref, decoder, pre_ref, known, node_slope, recv, recv_t, send_t, slope,
+     edge_in, edge_out, node_in, node_out,
+     agg_out, act_out, pre1_out, seed_out, local_out, recv_out, send_out, top_out, pre0_out,
+     pred_out, loss_out, *blocks) = refs
+    nodes, width = pre_ref.shape
+    size = blocks[0].shape[0]
+    summed = jnp.concatenate(
+        [
+            ref[:size, :] + came[at][:size, :] if came[at] is not None else ref[:size, :]
+            for at, ref in enumerate(own)
+        ],
+        axis=0,
+    )
+    agg_out[...] = summed
+    pre_agg = mm(summed, node_in[1, width:])
+    act, gate = silu_parts(pre_ref[...] + pre_agg)
+    act_out[...] = act
     weights = decoder[...]
-    predicted = jnp.sum(features * weights, axis=1, keepdims=True)
-    flat = flat_ref[:, 0:1]
-    here = flat == lax.broadcasted_iota(jnp.int32, (nodes, nodes), 1).astype(F32)
-    pred_out[...] = jnp.sum(jnp.where(here, predicted, 0.0), axis=0, keepdims=True)
-    wanted = jnp.sum(jnp.where(here, target[...], 0.0), axis=1, keepdims=True)
+    lead = row_of(jnp.sum(node_out[1] * weights, axis=1, keepdims=True))
+    base, wanted = known[:, 0:1], known[:, 1:2]
+    predicted = base + jnp.sum(act * lead, axis=1, keepdims=True)
     misfit = predicted - wanted
     seed = 2.0 * misfit / count
-    decoder_grad = jnp.sum(seed * features, axis=0, keepdims=True)
-    loss = jnp.broadcast_to(jnp.sum(misfit * misfit, axis=0, keepdims=True), (1, width))
-    tail_out[...] = jnp.concatenate([decoder_grad, loss, jnp.zeros((EXTRA - 2, width), F32)], 0)
-    top = seed * weights
-    top_grad_out[...] = top
-    pre_grad = mmt(top, node_out[layer]) * gate
-    pre_grad_out[...] = pre_grad
-    through_out[...] = top + mmt(pre_grad, node_in[layer, :width])
-    put_blocks(mmt(pre_grad, node_in[layer, width:]), blocks)
-
-
-def node_grads_kernel(h, summed, act, pre_grad, top_grad, out):
-    width = h.shape[1]
-    out[0:width, :] = tmm(h[...], pre_grad[...])
-    out[width : 2 * width, :] = tmm(summed[...], pre_grad[...])
-    out[2 * width :, :] = tmm(act[...], top_grad[...])
-
-
-def edge_grads_kernel(h, q, local_grad, to_recv, to_send, out):
-    width = h.shape[1]
-    out[0:width, :] = tmm(h[...], to_recv[...])
-    out[width : 2 * width, :] = tmm(h[...], to_send[...])
-    out[2 * width :, :] = tmm(q[...], local_grad[...])
-
-
-def back_kernel(
-    chunk, layer, names, *refs
-):
-    own, refs = refs[:4], refs[4:]
-    came, refs = unpack(names, refs)
-    (through, node_slope, recv, recv_t, send_t, slope, edge_in, edge_out, node_in, node_out,
-     local_out, recv_out, send_out, top_out, pre_out, *blocks) = refs
-    width = through.shape[1]
-    local_grad = take_sum(own, came)
+    seed_out[...] = jnp.broadcast_to(seed, seed_out.shape)
+    here = flat_ref[:, 0:1] == lax.broadcasted_iota(jnp.int32, (nodes, nodes), 1).astype(F32)
+    pred_out[...] = jnp.sum(jnp.where(here, predicted, 0.0), axis=0, keepdims=True)
+    loss_out[...] = jnp.broadcast_to(
+        jnp.sum(misfit * misfit, axis=0, keepdims=True), loss_out.shape
+    )
+    pre_grad = seed * lead * gate
+    pre1_out[...] = pre_grad
+    shared = []
+    for at in range(4):
+        rows = slice(at * size, (at + 1) * size)
+        if came[at] is None:
+            shared.append(pre_grad[rows])
+            continue
+        far_act, far_gate = silu_parts(came[at][size : 2 * size, :] + pre_agg[rows])
+        far_misfit = column_of(came[at][2 * size : 2 * size + 1, :size])
+        far_misfit = far_misfit + jnp.sum(far_act * lead, axis=1, keepdims=True)
+        there = came[at][2 * size + 1 : 2 * size + 2, 0:1]
+        far_seed = 2.0 * far_misfit / count * there
+        shared.append(pre_grad[rows] + far_seed * lead * far_gate)
+    local_grad = mmt(jnp.concatenate(shared, axis=0), node_in[1, width:])
     local_out[...] = local_grad
-    to_recv, to_send = edge_backward(
-        local_grad, edge_out[layer], recv, recv_t, send_t, slope, chunk
-    )
+    to_recv, to_send = edge_backward(local_grad, edge_out[1], recv, recv_t, send_t, slope, chunk)
     recv_out[...] = to_recv
     send_out[...] = to_send
     top = (
-        through[...]
-        + mmt(to_recv, edge_in[layer, :width])
-        + mmt(to_send, edge_in[layer, width:])
+        seed * weights
+        + mmt(pre_grad, node_in[1, :width])
+        + mmt(to_recv, edge_in[1, :width])
+        + mmt(to_send, edge_in[1, width:])
     )
     top_out[...] = top
-    pre_grad = mmt(top, node_out[layer - 1]) * node_slope[...]
-    pre_out[...] = pre_grad
-    put_blocks(mmt(pre_grad, node_in[layer - 1, width:]), blocks)
+    pre0 = mmt(top, node_out[0]) * node_slope[...]
+    pre0_out[...] = pre0
+    put_blocks(mmt(pre0, node_in[0, width:]), blocks)
+
+
+def grads_kernel(
+    h0, agg0, act0, pre0, top0, h1, agg1, act1, pre1, seed, q1, local1, to_recv1, to_send1,
+    decoder, node_out, loss, high, low, tail
+):
+    width = h0.shape[1]
+    rows = seed[...]
+    top1 = rows * decoder[...]
+    act = act1[...]
+    parts = [
+        tmm(h1[...], pre1[...]),
+        tmm(agg1[...], pre1[...]),
+        tmm(act, top1),
+        tmm(h1[...], to_recv1[...]),
+        tmm(h1[...], to_send1[...]),
+        tmm(q1[...], local1[...]),
+    ]
+    for at, part in enumerate(parts):
+        high[at * width : (at + 1) * width, :] = part
+    low[0:width, :] = tmm(h0[...], pre0[...])
+    low[width : 2 * width, :] = tmm(agg0[...], pre0[...])
+    low[2 * width :, :] = tmm(act0[...], top0[...])
+    line = jnp.sum(rows * h1[...], axis=0, keepdims=True)
+    line = line + row_product(jnp.sum(rows * act, axis=0, keepdims=True), node_out[1])
+    tail[...] = jnp.concatenate([line, loss[...], jnp.zeros((EXTRA - 2, width), F32)], axis=0)
 
 
 def split_rows(value, ref, first):
-    per = ref.shape[1] - EXTRA
+    per = ref.shape[1]
     at = 0
     while at < value.shape[0]:
         group, inside = divmod(first + at, per)
@@ -269,13 +336,10 @@
         at += take
 
 
-def end_kernel(
-    chunk, names, *refs
-):
+def end_kernel(chunk, names, *refs):
     own, refs = refs[:4], refs[4:]
     came, refs = unpack(names, refs)
-    (h, q, recv, recv_t, send_t, slope, edge_out, node_low, node_high, edge_high, tail,
-     mine, other) = refs
+    h, q, recv, recv_t, send_t, slope, edge_out, node_low, high, mine, other = refs
     local_grad = take_sum(own, came)
     to_recv, to_send = edge_backward(local_grad, edge_out[0], recv, recv_t, send_t, slope, chunk)
     low = [
@@ -284,19 +348,13 @@
         tmm(h[...], to_send),
         tmm(q[...], local_grad),
     ]
-    per = mine.shape[1] - EXTRA
-    blank = jnp.zeros((mine.shape[0], EXTRA, mine.shape[2]), F32)
 
     def write(ref_high, ref_low):
-        ref_high[:, per:, :] = blank
-        ref_low[:, per:, :] = blank
-        ref_high[0, per:, :] = tail[...]
         at = 0
         for value in low:
             split_rows(value, ref_low, at)
             at += value.shape[0]
-        split_rows(node_high[...], ref_high, 0)
-        split_rows(edge_high[...], ref_high, node_high.shape[0])
+        split_rows(high[...], ref_high, 0)
 
     first = lax.axis_index("sub") == 0
     pl.when(first)(lambda: write(mine, other))
@@ -307,13 +365,11 @@
     out[...] = a[...] + b[...]
 
 
-def total_kernel(parts, out):
+def total_kernel(parts, tail, out):
     total = jnp.sum(parts[...], axis=0)
-    per = total.shape[0] - EXTRA
-    body = total[: per + 1]
-    squares = jnp.sum(jnp.sum(body * body, axis=0, keepdims=True), axis=1, keepdims=True)
+    squares = jnp.sum(jnp.sum(total * total, axis=0, keepdims=True), axis=1, keepdims=True)
     last = jnp.broadcast_to(squares, (1, total.shape[1]))
-    total = jnp.concatenate([total[:-1], last], axis=0)
+    total = jnp.concatenate([total, tail[: EXTRA - 1, :], last], axis=0)
     out[...] = jnp.broadcast_to(total[None], out.shape)
 
 
@@ -323,9 +379,9 @@
     rows = mine.shape[1]
     per = rows - EXTRA
     width = mine.shape[2]
-    squares = jnp.sum(
-        mine[:, rows - 1 : rows, :] + other[:, rows - 1 : rows, :], axis=0
-    )
+    extra = jnp.sum(mine[:, per:, :] + other[:, per:, :], axis=0)
+    line = extra[0:1]
+    squares = extra[EXTRA - 1 : EXTRA] + jnp.sum(line * line, axis=1, keepdims=True)
     scale = 1.0 / jnp.sqrt(squares / params + 1e-06)
 
     def join(ref, first, size):
@@ -344,9 +400,9 @@
             node_out[layer] = join(ref, 2 * width, width)
             edge_in[layer] = join(ref, 3 * width, 2 * width)
             edge_out[layer] = join(ref, 5 * width, width)
-        decoder[...] = high[0, per : per + 1, :] * scale
-        loss[...] = high[0, per + 1 : per + 2, :] / count
-
+
+    decoder[...] = line * scale
+    loss[...] = extra[1:2] / count
     first = lax.axis_index("sub") == 0
     pl.when(first)(lambda: write(mine, other))
     pl.when(jnp.logical_not(first))(lambda: write(other, mine))
@@ -399,58 +455,72 @@
     edge_shape = ((edges, width), F32)
     block_shapes = [((size, width), F32)] * 4
 
-    flat, recv, send, recv_t, send_t, h0, slope0, q0, *blocks = call(
+    weights = (edge_in, edge_out, node_in, node_out)
+    sources = (
+        node_feats, edge_index, halo_index, target.reshape(1, nodes), decoder.reshape(1, width),
+        *weights,
+    )
+    shapes = [
+        ((1, nodes), F32), ((1, width), F32), *[(weight.shape, F32) for weight in weights],
+        ((nodes, 128), F32),
+        ((edges, nodes), BF16), ((edges, nodes), BF16),
+        ((nodes, edges), BF16), ((nodes, edges), BF16),
+        node_shape, edge_shape, node_shape, *block_shapes,
+    ]
+    (wanted, readout, edge_in, edge_out, node_in, node_out,
+     flat, recv, send, recv_t, send_t, h0, slope0, q0, *blocks) = pl.pallas_call(
         functools.partial(first_kernel, chunk),
-        [
-            ((nodes, 128), F32),
-            ((edges, nodes), BF16), ((edges, nodes), BF16),
-            ((nodes, edges), BF16), ((nodes, edges), BF16),
-            node_shape, edge_shape, node_shape, *block_shapes,
+        out_shape=[jax.ShapeDtypeStruct(shape, dtype) for shape, dtype in shapes],
+        in_specs=[pl.BlockSpec(memory_space=pltpu.HBM)] * len(sources),
+        out_specs=[VMEM] * len(shapes),
+        scratch_shapes=[
+            pltpu.VMEM(node_feats.shape, F32),
+            pltpu.VMEM(edge_index.shape, jnp.int32),
+            pltpu.VMEM(halo_index.shape, jnp.int32),
+            pltpu.SemaphoreType.DMA((len(sources),)),
         ],
-        node_feats, edge_index, halo_index, edge_in, edge_out,
-    )
-    agg0, h1, act0, gate0, slope1, q1, *blocks = call(
-        functools.partial(middle_kernel, chunk, 0, names),
-        [node_shape, node_shape, node_shape, node_shape, edge_shape, node_shape, *block_shapes],
+        compiler_params=pltpu.CompilerParams(vmem_limit_bytes=16 * 2**20),
+    )(*[pltpu.with_memory_space_constraint(source, pltpu.HBM) for source in sources])
+    message = ((2 * size + EXTRA, width), F32)
+    agg0, h1, act0, gate0, slope1, q1, pre, known, *messages = call(
+        functools.partial(middle_kernel, chunk, names),
+        [node_shape, node_shape, node_shape, node_shape, edge_shape, node_shape,
+         node_shape, node_shape, *[message] * 4],
         *blocks, *exchange(blocks),
-        h0, recv, send, recv_t, node_in, node_out, edge_in, edge_out,
-    )
-    agg1, act1, pre1, top1, through, pred, tail, *blocks = call(
-        functools.partial(last_kernel, 1, count, names),
-        [node_shape, node_shape, node_shape, node_shape, node_shape,
-         ((1, nodes), F32), ((EXTRA, width), F32), *block_shapes],
-        *blocks, *exchange(blocks),
-        h1, flat, target.reshape(1, nodes), decoder.reshape(1, width), node_in, node_out,
-    )
-    grads_shape = [((3 * width, width), F32)]
+        h0, flat, wanted, readout, recv, send, recv_t, node_in, node_out, edge_in, edge_out,
+    )
+    (agg1, act1, pre1, seed, local1, to_recv1, to_send1, top0, pre0, pred, loss,
+     *blocks) = call(
+        functools.partial(back_kernel, chunk, count, names),
+        [*[node_shape] * 9, ((1, nodes), F32), ((1, width), F32), *block_shapes],
+        *messages, *exchange(messages),
+        flat, readout, pre, known, gate0, recv, recv_t, send_t, slope1,
+        edge_in, edge_out, node_in, node_out,
+    )
     came = exchange(blocks)
-    (node_high,) = call(node_grads_kernel, grads_shape, h1, agg1, act1, pre1, top1)
-    local1, to_recv1, to_send1, top0, pre0, *blocks = call(
-        functools.partial(back_kernel, chunk, 1, names),
-        [node_shape, node_shape, node_shape, node_shape, node_shape, *block_shapes],
-        *blocks, *came,
-        through, gate0, recv, recv_t, send_t, slope1, edge_in, edge_out, node_in, node_out,
-    )
-    came = exchange(blocks)
-    (edge_high,) = call(edge_grads_kernel, grads_shape, h1, q1, local1, to_recv1, to_send1)
-    (node_low,) = call(node_grads_kernel, grads_shape, h0, agg0, act0, pre0, top0)
+    high, node_low, tail = call(
+        grads_kernel,
+        [((6 * width, width), F32), ((3 * width, width), F32), ((EXTRA, width), F32)],
+        h0, agg0, act0, pre0, top0, h1, agg1, act1, pre1, seed, q1, local1, to_recv1, to_send1,
+        readout, node_out, loss,
+    )
     per = 6 * width // n_dom
     if n_sub != 2 or per % 8 or 6 * width % n_dom:
         return slow_tail(
             count, blocks, came, names, chunk, h0, q0, recv, recv_t, send_t, slope0, edge_out,
-            node_low, node_high, edge_high, tail, pred, nodes,
+            node_low, high, tail, pred, nodes,
         )
+    halved = ((n_dom, per, width), F32)
     packed = ((n_dom, per + EXTRA, width), F32)
     mine, other = call(
         functools.partial(end_kernel, chunk, names),
-        [packed, packed],
-        *blocks, *came,
-        h0, q0, recv, recv_t, send_t, slope0, edge_out, node_low, node_high, edge_high, tail,
+        [halved, halved],
+        *blocks, *came, h0, q0, recv, recv_t, send_t, slope0, edge_out, node_low, high,
     )
     swap = pairs(n_sub, 0)
-    (halved,) = call(add_kernel, [packed], mine, lax.ppermute(other, "sub", swap))
-    parts = lax.all_to_all(halved, "dom", 0, 0, tiled=True)
-    (spread,) = call(total_kernel, [packed], parts)
+    (both,) = call(add_kernel, [halved], mine, lax.ppermute(other, "sub", swap))
+    parts = lax.all_to_all(both, "dom", 0, 0, tiled=True)
+    (spread,) = call(total_kernel, [packed], parts, tail)
     mine = lax.all_to_all(spread, "dom", 0, 0, tiled=True)
     other = lax.ppermute(mine, "sub", swap)
     params = 2 * 6 * width * width + width
@@ -484,7 +554,7 @@
 
 def slow_tail(
     count, blocks, came, names, chunk, h0, q0, recv, recv_t, send_t, slope0, edge_out,
-    node_low, node_high, edge_high, tail, pred, nodes,
+    node_low, high, tail, pred, nodes,
 ):
     width = h0.shape[1]
     (edge_low,) = call(
@@ -492,7 +562,7 @@
         *blocks, *came, h0, q0, recv, recv_t, send_t, slope0, edge_out,
     )
     total = lax.psum(
-        jnp.concatenate([node_low, edge_low, node_high, edge_high, tail], 0), ("dom", "sub")
+        jnp.concatenate([node_low, edge_low, high, tail], 0), ("dom", "sub")
     )
     rows = 12 * width
     body = total[: rows + 1]

time: 91.5 us -> 77.5 us (0.85)
  starting transfers between devices: 23.7 us -> 16.7 us
  local copies, waits for them, and re-layouts: 5.73 us -> 0 us
  blocking collectives: 42.8 us -> 41.5 us
    ppermute x12 -> x9, starting transfers between devices: 23.4 us -> 16.4 us  [exchange(): came[at] = lax.ppermute(blocks[at], axes[at], links[at])]
    unnamed x24 -> x0, local copies, waits for them, and re-layouts: 5.73 us -> none
    pallas_call x0 -> x1, Pallas kernels: none -> 3.48 us  [per_device(): pl.pallas_call(functools.partial(first_kernel, chunk), out_shape=[jax.Sha...]
    pallas_call x11 -> x7, Pallas kernels: 10.9 us -> 8.03 us  [call(): pl.pallas_call(kernel, out_shape=shapes, in_specs=[VMEM] * len(args), out...]
    all_to_all x1, blocking collectives: 26 us -> 24.8 us  [per_device(): parts = lax.all_to_all(both, 'dom', 0, 0, tiled=True)]
    ppermute x12 -> x9, waiting for transfers between devices: 3.81 us -> 3.39 us  [exchange(): came[at] = lax.ppermute(blocks[at], axes[at], links[at])]
  transfers between devices with their start and end apart: 14 -> 11, of which waited for: 6 -> 5; matrix products, arithmetic and copies ran while one was open for 0% -> 0% of each run, Pallas kernels for 1% -> 1%
where the time goes in v2:
time: 77.5 us; the launch traced here: 77.2 us
  blocking collectives  41.5 us (54%)
  starting transfers between devices  16.7 us (22%)
  Pallas kernels  11.5 us (15%)
  waiting for transfers between devices  6.75 us (9%)
    all_to_all x1, blocking collectives, per_device(): parts = lax.all_to_all(both, 'dom', 0, 0, tiled=True)  24.8 us
    all_to_all x1, blocking collectives, per_device(): mine = lax.all_to_all(spread, 'dom', 0, 0, tiled=True)  16.8 us
    ppermute x9, starting transfers between devices, exchange(): came[at] = lax.ppermute(blocks[at], axes[at], links[at])  16.4 us
    pallas_call x7, Pallas kernels, call(): pl.pallas_call(kernel, out_shape=shapes, in_specs=[VMEM] * len(args), out...  8.03 us
    pallas_call x1, Pallas kernels, per_device(): pl.pallas_call(functools.partial(first_kernel, chunk), out_shape=[jax.Sha...  3.48 us
    ppermute x9, waiting for transfers between devices, exchange(): came[at] = lax.ppermute(blocks[at], axes[at], links[at])  3.39 us
    ppermute x1, waiting for transfers between devices, per_device(): other = lax.ppermute(mine, 'sub', swap)  1.81 us
  transfers between devices with their start and end apart: 11, of which 5 were waited for; matrix products, arithmetic and copies ran while one was open for 0% of the time, Pallas kernels for 1%

profile of v2, /device:TPU:0, one launch (start us, length us, event | category | flops | bytes accessed | tf_op | source)
XLA Modules:
  0.0 77.2 jit_solution(16746676727988788830)
XLA Ops:
  0.6 3.5 %shard_map.144 = (f32[1,256]{1,0:T(1,128)S(1)}, f32[1,128]{1,0:T(1,128)S(1)}, f32[2,256,128]{2,1,0:T(8,128)S(1)}, f32[2,128,128]{2,1,0:T(8,128)S(1)}, f32[2,256,...) custom-call(f32[256,128]{1,0:T(8,128)} %feats_hbm.1, ...), custom_call_target="tpu_custom_call" | custom-call | tf_op jit(solution)/shard_map/pallas_call | solution.py:471
  4.1 3.0 %collective-permute-start = (f32[64,128]{1,0:T(8,128)S(1)}, f32[64,128]{1,0:T(8,128)S(1)}, u32[]{:S(2)}, u32[]{:S(2)}) collective-permute-start(f32[64,128]{1,0:T(8,128)S(1)} %get-tuple-element.63.refs_0_), channel_id=1, source_target_pairs={{0,2},{2,0},{4,6},{6,4},{8,10},{10,8},{12,14},{14,12},{16,18},{18,... | collective-permute-start | bytes 98312 | tf_op jit(solution)/shard_map/ppermute | solution.py:451
  7.2 0.7 collective-permute-start.1
  7.8 0.1 collective-permute-start.2
  7.9 1.2 %collective-permute-done.refs_4_ = f32[64,128]{1,0:T(8,128)S(1)} collective-permute-done((f32[64,128]{1,0:T(8,128)S(1)}, f32[64,128]{1,0:T(8,128)S(1)}, u32[]{:S(2)}, u32[]{:S(2)}) %collective-permute-start) | collective-permute-done | bytes 32800 | tf_op jit(solution)/shard_map/ppermute | solution.py:451
  9.1 1.9 %shard_map.145 = (f32[256,128]{1,0:T(8,128)S(1)}, f32[256,128]{1,0:T(8,128)S(1)}, f32[256,128]{1,0:T(8,128)S(1)}, f32[256,128]{1,0:T(8,128)S(1)}, f32[1280,128]{...) custom-call(f32[64,128]{1,0:T(8,128)S(1)} %get-tuple-element.63.refs, ...), custom_call_target="tpu_custom_call" | custom-call | tf_op jit(solution)/shard_map/pallas_call | solution.py:413
  11.0 4.9 %collective-permute-start.3 = (f32[136,128]{1,0:T(8,128)S(1)}, f32[136,128]{1,0:T(8,128)S(1)}, u32[]{:S(2)}, u32[]{:S(2)}) collective-permute-start(f32[136,128]{1,0:T(8,128)S(1)} %get-tuple-element.78.refs_0_), channel_id=1, source_target_pairs={{0,2},{2,0},{4,6},{6,4},{8,10},{10,8},{12,14},{14,12},{16,18},{18,... | collective-permute-start | bytes 208904 | tf_op jit(solution)/shard_map/ppermute | solution.py:451
  15.9 0.7 collective-permute-start.4
  16.5 0.1 collective-permute-start.5
  16.6 1.5 %collective-permute-done.3.refs_4_ = f32[136,128]{1,0:T(8,128)S(1)} collective-permute-done((f32[136,128]{1,0:T(8,128)S(1)}, f32[136,128]{1,0:T(8,128)S(1)}, u32[]{:S(2)}, u32[]{:S(2)}) %collective-permute-start.3) | collective-permute-done | bytes 69664 | tf_op jit(solution)/shard_map/ppermute | solution.py:451
  18.2 2.6 %shard_map.146 = (f32[256,128]{1,0:T(8,128)S(1)}, f32[256,128]{1,0:T(8,128)S(1)}, f32[256,128]{1,0:T(8,128)S(1)}, f32[256,128]{1,0:T(8,128)S(1)}, f32[256,128]{1...) custom-call(f32[136,128]{1,0:T(8,128)S(1)} %get-tuple-element.78.ref, ...), custom_call_target="tpu_custom_call" | custom-call | tf_op jit(solution)/shard_map/pallas_call | solution.py:413
  20.7 6.3 %collective-permute-start.6 = (f32[64,128]{1,0:T(8,128)S(1)}, f32[64,128]{1,0:T(8,128)S(1)}, u32[]{:S(2)}, u32[]{:S(2)}) collective-permute-start(f32[64,128]{1,0:T(8,128)S(1)} %get-tuple-element.87.refs_0_), channel_id=1, source_target_pairs={{0,2},{2,0},{4,6},{6,4},{8,10},{10,8},{12,14},{14,12},{16,18},{18,... | collective-permute-start | bytes 98312 | tf_op jit(solution)/shard_map/ppermute | solution.py:451
  27.0 0.7 collective-permute-start.7
  27.7 0.1 collective-permute-start.8
  27.8 0.5 shard_map.147
  28.3 0.6 collective-permute-done.6.refs_4_
  29.0 1.9 %shard_map.148 = (f32[16,48,128]{2,1,0:T(8,128)S(1)}, f32[16,48,128]{2,1,0:T(8,128)S(1)}) custom-call(f32[64,128]{1,0:T(8,128)S(1)} %get-tuple-element.87.refs_0_, f32[64,128]{1,0:T(8,128)S(1)} %get-tuple-element.88.refs_1_, f32[64,128]{1,0:T(8,128)S(1)} %get-tuple-element.89.refs_2_, f32[64,128]{1,0:T(8,128)S(1)} %get-tuple-element.90.refs_3_, ...), custom_call_target="tpu_custom_call" | custom-call | tf_op jit(solution)/shard_map/pallas_call | solution.py:413
  30.8 0.2 collective-permute-start.9
  31.1 1.5 %collective-permute-done.9.b = f32[16,48,128]{2,1,0:T(8,128)S(1)} collective-permute-done((f32[16,48,128]{2,1,0:T(8,128)S(1)}, f32[16,48,128]{2,1,0:T(8,128)S(1)}, u32[]{:S(2)}, u32[]{:S(2)}) %collective-permute-start.9) | collective-permute-done | bytes 393248 | tf_op jit(solution)/shard_map/ppermute | solution.py:521
  32.7 24.8 %all_to_all.10.parts = f32[16,48,128]{2,1,0:T(8,128)S(1)} all-to-all(f32[16,48,128]{2,1,0:T(8,128)S(1)} %shard_map.149), channel_id=1, replica_groups=mesh['dom'=16,'sub'=2] {'dom'}, dimensions={0} | all-to-all | bytes 786432 | tf_op jit(solution)/shard_map/all_to_all | solution.py:522
  57.4 0.1 shard_map.150
  57.5 16.8 %all_to_all.11.mine = f32[16,56,128]{2,1,0:T(8,128)S(1)} all-to-all(f32[16,56,128]{2,1,0:T(8,128)S(1)} %shard_map.150), channel_id=1, replica_groups=mesh['dom'=16,'sub'=2] {'dom'}, dimensions={0} | all-to-all | bytes 917504 | tf_op jit(solution)/shard_map/all_to_all | solution.py:524
  74.3 1.8 %collective-permute-done.10.other = f32[16,56,128]{2,1,0:T(8,128)S(1)} collective-permute-done((f32[16,56,128]{2,1,0:T(8,128)S(1)}, f32[16,56,128]{2,1,0:T(8,128)S(1)}, u32[]{:S(2)}, u32[]{:S(2)}) %collective-permute-start.10) | collective-permute-done | bytes 458784 | tf_op jit(solution)/shard_map/ppermute | solution.py:525
  76.1 1.0 %shard_map.151 = (f32[1,128]{1,0:T(1,128)}, f32[2,256,128]{2,1,0:T(8,128)}, f32[2,128,128]{2,1,0:T(8,128)}, f32[2,256,128]{2,1,0:T(8,128)}, f32[2,128,128]{2,1,0:T(8,128)}, /*index=5*/f32[1,128]{1,0:T(1,128)}) custom-call(f32[16,56,128]{2,1,0:T(8,128)S(1)} %all_to_all.11.mine, f32[16,56,128]{2,1,0:T(8,128)S(1)} %collective-permute-done.10.other), custom_call_target="tpu_custom_call" | custom-call | tf_op jit(solution)/shard_map/pallas_call | solution.py:413
  (8 shorter events, 0.1 us)
Async XLA Ops:
  4.1 4.9 %collective-permute-start = (f32[64,128]{1,0:T(8,128)S(1)}, f32[64,128]{1,0:T(8,128)S(1)}, u32[]{:S(2)}, u32[]{:S(2)}) collective-permute-start(f32[64,128]{1,0:T(8,128)S(1)} %get-tuple-element.63.refs_0_), channel_id=1, source_target_pairs={{0,2},{2,0},{4,6},{6,4},{8,10},{10,8},{12,14},{14,12},{16,18},{18,... | collective-permute-start | bytes 98312 | tf_op jit(solution)/shard_map/ppermute | solution.py:451
  7.2 1.9 %collective-permute-start.1 = (f32[64,128]{1,0:T(8,128)S(1)}, f32[64,128]{1,0:T(8,128)S(1)}, u32[]{:S(2)}, u32[]{:S(2)}) collective-permute-start(f32[64,128]{1,0:T(8,128)S(1)} %get-tuple-element.64.refs_1_), channel_id=1, source_target_pairs={{2,4},{4,2},{6,8},{8,6},{10,12},{12,10},{14,16},{16,14},{18,20},{2... | collective-permute-start | bytes 98312 | tf_op jit(solution)/shard_map/ppermute | solution.py:451
  7.8 1.3 %collective-permute-start.2 = (f32[64,128]{1,0:T(8,128)S(1)}, f32[64,128]{1,0:T(8,128)S(1)}, u32[]{:S(2)}, u32[]{:S(2)}) collective-permute-start(f32[64,128]{1,0:T(8,128)S(1)} %get-tuple-element.65.refs_2_), channel_id=1, source_target_pairs={{0,1},{1,0},{2,3},{3,2},{4,5},{5,4},{6,7},{7,6},{8,9},{9,8},{10,11... | collective-permute-start | bytes 98312 | tf_op jit(solution)/shard_map/ppermute | solution.py:451
  11.0 7.2 %collective-permute-start.3 = (f32[136,128]{1,0:T(8,128)S(1)}, f32[136,128]{1,0:T(8,128)S(1)}, u32[]{:S(2)}, u32[]{:S(2)}) collective-permute-start(f32[136,128]{1,0:T(8,128)S(1)} %get-tuple-element.78.refs_0_), channel_id=1, source_target_pairs={{0,2},{2,0},{4,6},{6,4},{8,10},{10,8},{12,14},{14,12},{16,18},{18,... | collective-permute-start | bytes 208904 | tf_op jit(solution)/shard_map/ppermute | solution.py:451
  15.9 2.3 %collective-permute-start.4 = (f32[136,128]{1,0:T(8,128)S(1)}, f32[136,128]{1,0:T(8,128)S(1)}, u32[]{:S(2)}, u32[]{:S(2)}) collective-permute-start(f32[136,128]{1,0:T(8,128)S(1)} %get-tuple-element.79.refs_1_), channel_id=1, source_target_pairs={{2,4},{4,2},{6,8},{8,6},{10,12},{12,10},{14,16},{16,14},{18,20},{2... | collective-permute-start | bytes 208904 | tf_op jit(solution)/shard_map/ppermute | solution.py:451
  16.5 1.6 %collective-permute-start.5 = (f32[136,128]{1,0:T(8,128)S(1)}, f32[136,128]{1,0:T(8,128)S(1)}, u32[]{:S(2)}, u32[]{:S(2)}) collective-permute-start(f32[136,128]{1,0:T(8,128)S(1)} %get-tuple-element.80.refs_2_), channel_id=1, source_target_pairs={{0,1},{1,0},{2,3},{3,2},{4,5},{5,4},{6,7},{7,6},{8,9},{9,8},{10,11... | collective-permute-start | bytes 208904 | tf_op jit(solution)/shard_map/ppermute | solution.py:451
  20.7 8.2 %collective-permute-start.6 = (f32[64,128]{1,0:T(8,128)S(1)}, f32[64,128]{1,0:T(8,128)S(1)}, u32[]{:S(2)}, u32[]{:S(2)}) collective-permute-start(f32[64,128]{1,0:T(8,128)S(1)} %get-tuple-element.87.refs_0_), channel_id=1, source_target_pairs={{0,2},{2,0},{4,6},{6,4},{8,10},{10,8},{12,14},{14,12},{16,18},{18,... | collective-permute-start | bytes 98312 | tf_op jit(solution)/shard_map/ppermute | solution.py:451
  27.0 1.9 %collective-permute-start.7 = (f32[64,128]{1,0:T(8,128)S(1)}, f32[64,128]{1,0:T(8,128)S(1)}, u32[]{:S(2)}, u32[]{:S(2)}) collective-permute-start(f32[64,128]{1,0:T(8,128)S(1)} %get-tuple-element.88.refs_1_), channel_id=1, source_target_pairs={{2,4},{4,2},{6,8},{8,6},{10,12},{12,10},{14,16},{16,14},{18,20},{2... | collective-permute-start | bytes 98312 | tf_op jit(solution)/shard_map/ppermute | solution.py:451
  27.7 1.3 %collective-permute-start.8 = (f32[64,128]{1,0:T(8,128)S(1)}, f32[64,128]{1,0:T(8,128)S(1)}, u32[]{:S(2)}, u32[]{:S(2)}) collective-permute-start(f32[64,128]{1,0:T(8,128)S(1)} %get-tuple-element.89.refs_2_), channel_id=1, source_target_pairs={{0,1},{1,0},{2,3},{3,2},{4,5},{5,4},{6,7},{7,6},{8,9},{9,8},{10,11... | collective-permute-start | bytes 98312 | tf_op jit(solution)/shard_map/ppermute | solution.py:451
  30.8 1.8 %collective-permute-start.9 = (f32[16,48,128]{2,1,0:T(8,128)S(1)}, f32[16,48,128]{2,1,0:T(8,128)S(1)}, u32[]{:S(2)}, u32[]{:S(2)}) collective-permute-start(f32[16,48,128]{2,1,0:T(8,128)S(1)} %get-tuple-element.110), channel_id=1, source_target_pairs={{0,1},{1,0},{2,3},{3,2},{4,5},{5,4},{6,7},{7,6},{8,9},{9,8},{10,11... | collective-permute-start | bytes 1179656 | tf_op jit(solution)/shard_map/ppermute | solution.py:521
  74.3 1.8 %collective-permute-start.10 = (f32[16,56,128]{2,1,0:T(8,128)S(1)}, f32[16,56,128]{2,1,0:T(8,128)S(1)}, u32[]{:S(2)}, u32[]{:S(2)}) collective-permute-start(f32[16,56,128]{2,1,0:T(8,128)S(1)} %all_to_all.11.mine), channel_id=1, source_target_pairs={{0,1},{1,0},{2,3},{3,2},{4,5},{5,4},{6,7},{7,6},{8,9},{9,8},{10,11... | collective-permute-start | bytes 1376264 | tf_op jit(solution)/shard_map/ppermute | solution.py:525

commit v3 on v2

--- a/solution.py
+++ b/solution.py
@@ -154,8 +154,8 @@
     dom_even, sub_even = even("dom"), even("sub")
     flat = jnp.concatenate(
         [
+            jnp.where(dom_even, by_dir[0], by_dir[1]),
             jnp.where(dom_even, by_dir[1], by_dir[0]),
-            jnp.where(dom_even, by_dir[0], by_dir[1]),
             jnp.where(sub_even, by_dir[3], by_dir[2]),
             jnp.where(sub_even, by_dir[2], by_dir[3]),
         ],
@@ -326,20 +326,15 @@
     tail[...] = jnp.concatenate([line, loss[...], jnp.zeros((EXTRA - 2, width), F32)], axis=0)
 
 
-def split_rows(value, ref, first):
-    per = ref.shape[1]
-    at = 0
-    while at < value.shape[0]:
-        group, inside = divmod(first + at, per)
-        take = min(per - inside, value.shape[0] - at)
-        ref[group, inside : inside + take, :] = value[at : at + take]
-        at += take
+def put_rows(ref, at, value):
+    ref[at : at + value.shape[0], :] = value
+    return at + value.shape[0]
 
 
 def end_kernel(chunk, names, *refs):
     own, refs = refs[:4], refs[4:]
     came, refs = unpack(names, refs)
-    h, q, recv, recv_t, send_t, slope, edge_out, node_low, high, mine, other = refs
+    h, q, recv, recv_t, send_t, slope, edge_out, node_low, high, tail, mine, other = refs
     local_grad = take_sum(own, came)
     to_recv, to_send = edge_backward(local_grad, edge_out[0], recv, recv_t, send_t, slope, chunk)
     low = [
@@ -347,65 +342,82 @@
         tmm(h[...], to_recv),
         tmm(h[...], to_send),
         tmm(q[...], local_grad),
+        tail[...],
     ]
 
     def write(ref_high, ref_low):
         at = 0
         for value in low:
-            split_rows(value, ref_low, at)
-            at += value.shape[0]
-        split_rows(high[...], ref_high, 0)
+            at = put_rows(ref_low, at, value)
+        put_rows(ref_high, put_rows(ref_high, 0, high[...]), tail[...])
 
     first = lax.axis_index("sub") == 0
     pl.when(first)(lambda: write(mine, other))
     pl.when(jnp.logical_not(first))(lambda: write(other, mine))
 
 
-def add_kernel(a, b, out):
+def quarters_kernel(mine, other, *outs):
+    per = outs[0].shape[0] - EXTRA
+    own = lax.rem(lax.axis_index("dom"), 4)
+    tail = mine[4 * per :, :] + other[4 * per :, :]
+    for away, out in enumerate(outs):
+        rows = pl.ds(pl.multiple_of(jnp.bitwise_xor(own, away) * per, 8), per)
+        out[:per, :] = mine[rows, :] + other[rows, :]
+        out[per:, :] = tail
+
+
+def four_kernel(a, b, c, d, out):
+    out[...] = (a[...] + b[...]) + (c[...] + d[...])
+
+
+def two_kernel(a, b, out):
     out[...] = a[...] + b[...]
 
 
-def total_kernel(parts, tail, out):
-    total = jnp.sum(parts[...], axis=0)
-    squares = jnp.sum(jnp.sum(total * total, axis=0, keepdims=True), axis=1, keepdims=True)
-    last = jnp.broadcast_to(squares, (1, total.shape[1]))
-    total = jnp.concatenate([total, tail[: EXTRA - 1, :], last], axis=0)
-    out[...] = jnp.broadcast_to(total[None], out.shape)
-
-
-def scale_kernel(
-    params, count, mine, other, loss, edge_in, edge_out, node_in, node_out, decoder
-):
-    rows = mine.shape[1]
-    per = rows - EXTRA
-    width = mine.shape[2]
-    extra = jnp.sum(mine[:, per:, :] + other[:, per:, :], axis=0)
-    line = extra[0:1]
-    squares = extra[EXTRA - 1 : EXTRA] + jnp.sum(line * line, axis=1, keepdims=True)
-    scale = 1.0 / jnp.sqrt(squares / params + 1e-06)
-
-    def join(ref, first, size):
-        parts = []
-        at = 0
-        while at < size:
-            group, inside = divmod(first + at, per)
-            take = min(per - inside, size - at)
-            parts.append(ref[group, inside : inside + take, :])
-            at += take
-        return jnp.concatenate(parts, axis=0) * scale
-
-    def write(high, low):
-        for layer, ref in ((1, high), (0, low)):
-            node_in[layer] = join(ref, 0, 2 * width)
-            node_out[layer] = join(ref, 2 * width, width)
-            edge_in[layer] = join(ref, 3 * width, 2 * width)
-            edge_out[layer] = join(ref, 5 * width, width)
-
+def last_sum_kernel(a, b, out, tail):
+    per = out.shape[0]
+    out[...] = a[:per, :] + b[:per, :]
+    tail[...] = a[per:, :] + b[per:, :]
+
+
+def scale_kernel(params, count, *refs):
+    near, far = refs[:4], refs[4:8]
+    tail, loss, edge_in, edge_out, node_in, node_out, decoder = refs[8:]
+    width = tail.shape[1]
+    line = tail[0:1]
+    squares = []
+    for group in (near, far):
+        sums = [jnp.sum(ref[...] * ref[...], axis=0, keepdims=True) for ref in group]
+        squares.append((sums[0] + sums[1]) + (sums[2] + sums[3]))
+    every = jnp.sum(squares[0] + squares[1] + line * line, axis=1, keepdims=True)
+    scale = 1.0 / jnp.sqrt(every / params + 1e-06)
     decoder[...] = line * scale
-    loss[...] = extra[1:2] / count
-    first = lax.axis_index("sub") == 0
-    pl.when(first)(lambda: write(mine, other))
-    pl.when(jnp.logical_not(first))(lambda: write(other, mine))
+    loss[...] = tail[1:2] / count
+    where = [(node_in, at) for at in range(2)] + [(node_out, 0)]
+    where = where + [(edge_in, at) for at in range(2)] + [(edge_out, 0)]
+
+    def write(own, layer, group):
+        per = group[0].shape[0]
+        for quarter in range(4):
+            ref = group[quarter ^ own]
+            at = 0
+            while at < per:
+                block, inside = divmod(quarter * per + at, width)
+                take = min(width - inside, per - at)
+                out, half = where[block]
+                first = half * width + inside
+                out[layer, first : first + take, :] = ref[at : at + take, :] * scale
+                at += take
+
+    here = lax.rem(lax.axis_index("dom"), 4)
+    side_here = lax.axis_index("sub")
+    for own in range(4):
+        for core in range(2):
+            def both(own=own, core=core):
+                write(own, 1 - core, near)
+                write(own, core, far)
+
+            pl.when(jnp.logical_and(here == own, side_here == core))(both)
 
 
 def call(kernel, outs, *args):
@@ -437,16 +449,13 @@
     if edge_in.shape[0] != 2 or 4 * size != nodes:
         raise ValueError("unsupported sizes")
     chunk = 256
-    routes = [("dom", 1), ("dom", 0), ("sub", 0), ("sub", 1)]
-    order = [1, 0, 2, 3]
-    links = [pairs(lax.axis_size(axis), offset) for axis, offset in routes]
-    links = [links[1], links[0], links[2], links[3]]
     axes = ["dom", "dom", "sub", "sub"]
+    links = [pairs(lax.axis_size(axis), offset) for axis, offset in zip(axes, (1, 0, 0, 1))]
     names = tuple(1 if link else 0 for link in links)
 
     def exchange(blocks):
         came = [None] * 4
-        for at in order:
+        for at in range(4):
             if links[at]:
                 came[at] = lax.ppermute(blocks[at], axes[at], links[at])
         return [block for block in came if block is not None]
@@ -504,25 +513,44 @@
         h0, agg0, act0, pre0, top0, h1, agg1, act1, pre1, seed, q1, local1, to_recv1, to_send1,
         readout, node_out, loss,
     )
-    per = 6 * width // n_dom
-    if n_sub != 2 or per % 8 or 6 * width % n_dom:
+    rows = 6 * width
+    groups = n_dom // 4
+    if n_sub != 2 or n_dom % 4 or groups & (groups - 1) or rows % 32:
         return slow_tail(
             count, blocks, came, names, chunk, h0, q0, recv, recv_t, send_t, slope0, edge_out,
             node_low, high, tail, pred, nodes,
         )
-    halved = ((n_dom, per, width), F32)
-    packed = ((n_dom, per + EXTRA, width), F32)
+    per = rows // 4
+    half = ((rows + EXTRA, width), F32)
+    quarter = ((per + EXTRA, width), F32)
     mine, other = call(
         functools.partial(end_kernel, chunk, names),
-        [halved, halved],
-        *blocks, *came, h0, q0, recv, recv_t, send_t, slope0, edge_out, node_low, high,
-    )
-    swap = pairs(n_sub, 0)
-    (both,) = call(add_kernel, [halved], mine, lax.ppermute(other, "sub", swap))
-    parts = lax.all_to_all(both, "dom", 0, 0, tiled=True)
-    (spread,) = call(total_kernel, [packed], parts, tail)
-    mine = lax.all_to_all(spread, "dom", 0, 0, tiled=True)
-    other = lax.ppermute(mine, "sub", swap)
+        [half, half],
+        *blocks, *came, h0, q0, recv, recv_t, send_t, slope0, edge_out, node_low, high, tail,
+    )
+
+    def swap(value):
+        return lax.ppermute(value, "sub", pairs(n_sub, 0))
+
+    def across(value, away):
+        return lax.ppermute(value, "dom", [(at, at ^ away) for at in range(n_dom)])
+
+    parts = call(quarters_kernel, [quarter] * 4, mine, swap(other))
+    came = [across(parts[away], away) for away in (3, 2, 1)]
+    (total,) = call(four_kernel, [quarter], parts[0], came[2], came[1], came[0])
+    away = 4
+    while away < n_dom // 2:
+        (total,) = call(two_kernel, [quarter], total, across(total, away))
+        away *= 2
+    if away < n_dom:
+        far = across(total, away)
+    else:
+        far = jnp.zeros_like(total)
+    total, tail = call(
+        last_sum_kernel, [((per, width), F32), ((EXTRA, width), F32)], total, far
+    )
+    near = [total] + [across(total, away) for away in range(1, 4)]
+    far = [swap(value) for value in near]
     params = 2 * 6 * width * width + width
     loss, g_edge_in, g_edge_out, g_node_in, g_node_out, g_decoder = call(
         functools.partial(scale_kernel, params, count),
@@ -532,7 +560,7 @@
             ((2, 2 * width, width), F32), ((2, width, width), F32),
             ((1, width), F32),
         ],
-        mine, other,
+        *near, *far, tail,
     )
     return (
         loss[0, 0], pred.reshape(nodes), g_edge_in, g_edge_out, g_node_in, g_node_out,

time: 77.5 us -> 66.3 us (0.86)
  blocking collectives: 41.5 us -> 0 us
  waiting for transfers between devices: 6.75 us -> 24.7 us
  starting transfers between devices: 16.7 us -> 29.1 us
    all_to_all x2 -> x0, blocking collectives: 41.5 us -> none  [the longest x1 24.8 us: per_device(): parts = lax.all_to_all(both, 'dom', 0, 0, tiled=True)]
    ppermute x2 -> x13, waiting for transfers between devices: 3.35 us -> 18 us  [the longest x8 15 us: across(): return lax.ppermute(value, 'dom', [(at, at ^ away) for at in range(n_dom)])]
    ppermute x2 -> x13, starting transfers between devices: 0.25 us -> 12.3 us  [the longest x8 12.2 us: across(): return lax.ppermute(value, 'dom', [(at, at ^ away) for at in range(n_dom)])]
    ppermute x9, waiting for transfers between devices: 3.39 us -> 6.7 us  [exchange(): came[at] = lax.ppermute(blocks[at], axes[at], links[at])]
    pallas_call x7 -> x9, Pallas kernels: 8.03 us -> 8.06 us  [call(): pl.pallas_call(kernel, out_shape=shapes, in_specs=[VMEM] * len(args), out...]
  transfers between devices with their start and end apart: 11 -> 22, of which waited for: 5 -> 14; matrix products, arithmetic and copies ran while one was open for 0% -> 0% of each run, Pallas kernels for 1% -> 1%
where the time goes in v3:
time: 66.3 us; the launch traced here: 66.1 us
  starting transfers between devices  29.1 us (44%)
  waiting for transfers between devices  24.7 us (37%)
  Pallas kernels  11.5 us (17%)
  between operations  0.74 us (1%)
    ppermute x9, starting transfers between devices, exchange(): came[at] = lax.ppermute(blocks[at], axes[at], links[at])  16.8 us
    ppermute x8, waiting for transfers between devices, across(): return lax.ppermute(value, 'dom', [(at, at ^ away) for at in range(n_dom)])  15 us
    ppermute x8, starting transfers between devices, across(): return lax.ppermute(value, 'dom', [(at, at ^ away) for at in range(n_dom)])  12.2 us
    pallas_call x9, Pallas kernels, call(): pl.pallas_call(kernel, out_shape=shapes, in_specs=[VMEM] * len(args), out...  8.06 us
    ppermute x9, waiting for transfers between devices, exchange(): came[at] = lax.ppermute(blocks[at], axes[at], links[at])  6.7 us
    pallas_call x1, Pallas kernels, per_device(): pl.pallas_call(functools.partial(first_kernel, chunk), out_shape=[jax.Sha...  3.48 us
    ppermute x5, waiting for transfers between devices, swap(): return lax.ppermute(value, 'sub', pairs(n_sub, 0))  3.01 us
  transfers between devices with their start and end apart: 22, of which 14 were waited for; matrix products, arithmetic and copies ran while one was open for 0% of the time, Pallas kernels for 1%

profile of v3, /device:TPU:0, one launch (start us, length us, event | category | flops | bytes accessed | tf_op | source)
XLA Modules:
  0.0 66.1 jit_solution(7025391324337791788)
XLA Ops:
  0.6 3.5 %shard_map.144 = (f32[1,256]{1,0:T(1,128)S(1)}, f32[1,128]{1,0:T(1,128)S(1)}, f32[2,256,128]{2,1,0:T(8,128)S(1)}, f32[2,128,128]{2,1,0:T(8,128)S(1)}, f32[2,256,...) custom-call(f32[256,128]{1,0:T(8,128)} %feats_hbm.1, ...), custom_call_target="tpu_custom_call" | custom-call | tf_op jit(solution)/shard_map/pallas_call | solution.py:480
  4.8 5.8 %collective-permute-start.1 = (f32[64,128]{1,0:T(8,128)S(1)}, f32[64,128]{1,0:T(8,128)S(1)}, u32[]{:S(2)}, u32[]{:S(2)}) collective-permute-start(f32[64,128]{1,0:T(8,128)S(1)} %get-tuple-element.70.refs_1_), channel_id=1, source_target_pairs={{0,2},{2,0},{4,6},{6,4},{8,10},{10,8},{12,14},{14,12},{16,18},{18,... | collective-permute-start | bytes 98312 | tf_op jit(solution)/shard_map/ppermute | solution.py:460
  10.6 2.1 %collective-permute-done.1.refs_5_ = f32[64,128]{1,0:T(8,128)S(1)} collective-permute-done((f32[64,128]{1,0:T(8,128)S(1)}, f32[64,128]{1,0:T(8,128)S(1)}, u32[]{:S(2)}, u32[]{:S(2)}) %collective-permute-start.1) | collective-permute-done | bytes 32800 | tf_op jit(solution)/shard_map/ppermute | solution.py:460
  12.7 1.9 %shard_map.145 = (f32[256,128]{1,0:T(8,128)S(1)}, f32[256,128]{1,0:T(8,128)S(1)}, f32[256,128]{1,0:T(8,128)S(1)}, f32[256,128]{1,0:T(8,128)S(1)}, f32[1280,128]{...) custom-call(f32[64,128]{1,0:T(8,128)S(1)} %get-tuple-element.69.refs, ...), custom_call_target="tpu_custom_call" | custom-call | tf_op jit(solution)/shard_map/pallas_call | solution.py:425
  15.3 4.5 %collective-permute-start.4 = (f32[136,128]{1,0:T(8,128)S(1)}, f32[136,128]{1,0:T(8,128)S(1)}, u32[]{:S(2)}, u32[]{:S(2)}) collective-permute-start(f32[136,128]{1,0:T(8,128)S(1)} %get-tuple-element.85.refs_1_), channel_id=1, source_target_pairs={{0,2},{2,0},{4,6},{6,4},{8,10},{10,8},{12,14},{14,12},{16,18},{18,... | collective-permute-start | bytes 208904 | tf_op jit(solution)/shard_map/ppermute | solution.py:460
  19.8 2.9 %collective-permute-done.4.refs_5_ = f32[136,128]{1,0:T(8,128)S(1)} collective-permute-done((f32[136,128]{1,0:T(8,128)S(1)}, f32[136,128]{1,0:T(8,128)S(1)}, u32[]{:S(2)}, u32[]{:S(2)}) %collective-permute-start.4) | collective-permute-done | bytes 69664 | tf_op jit(solution)/shard_map/ppermute | solution.py:460
  22.7 2.6 %shard_map.146 = (f32[256,128]{1,0:T(8,128)S(1)}, f32[256,128]{1,0:T(8,128)S(1)}, f32[256,128]{1,0:T(8,128)S(1)}, f32[256,128]{1,0:T(8,128)S(1)}, f32[256,128]{1...) custom-call(f32[136,128]{1,0:T(8,128)S(1)} %get-tuple-element.84.ref, ...), custom_call_target="tpu_custom_call" | custom-call | tf_op jit(solution)/shard_map/pallas_call | solution.py:425
  26.0 4.5 %collective-permute-start.7 = (f32[64,128]{1,0:T(8,128)S(1)}, f32[64,128]{1,0:T(8,128)S(1)}, u32[]{:S(2)}, u32[]{:S(2)}) collective-permute-start(f32[64,128]{1,0:T(8,128)S(1)} %get-tuple-element.94.refs_1_), channel_id=1, source_target_pairs={{0,2},{2,0},{4,6},{6,4},{8,10},{10,8},{12,14},{14,12},{16,18},{18,... | collective-permute-start | bytes 98312 | tf_op jit(solution)/shard_map/ppermute | solution.py:460
  31.0 1.6 %collective-permute-done.7.refs_5_ = f32[64,128]{1,0:T(8,128)S(1)} collective-permute-done((f32[64,128]{1,0:T(8,128)S(1)}, f32[64,128]{1,0:T(8,128)S(1)}, u32[]{:S(2)}, u32[]{:S(2)}) %collective-permute-start.7) | collective-permute-done | bytes 32800 | tf_op jit(solution)/shard_map/ppermute | solution.py:460
  32.6 1.9 %shard_map.148 = (f32[776,128]{1,0:T(8,128)S(1)}, f32[776,128]{1,0:T(8,128)S(1)}) custom-call(f32[64,128]{1,0:T(8,128)S(1)} %get-tuple-element.93.refs_0_, f32[64,128]{1,0:T(8,128)S(1)} %get-tuple-element.94.refs_1_, f32[64,128]{1,0:T(8,128)S(1)} %get-tuple-element.95.refs_2_, f32[64,128]{1,0:T(8,128)S(1)} %get-tuple-element.96.refs_3_, ...), custom_call_target="tpu_custom_call" | custom-call | tf_op jit(solution)/shard_map/pallas_call | solution.py:425
  34.6 1.7 %collective-permute-done.9.other = f32[776,128]{1,0:T(8,128)S(1)} collective-permute-done((f32[776,128]{1,0:T(8,128)S(1)}, f32[776,128]{1,0:T(8,128)S(1)}, u32[]{:S(2)}, u32[]{:S(2)}) %collective-permute-start.9) | collective-permute-done | bytes 397344 | tf_op jit(solution)/shard_map/ppermute | solution.py:533
  36.4 1.8 %collective-permute-start.10 = (f32[200,128]{1,0:T(8,128)S(1)}, f32[200,128]{1,0:T(8,128)S(1)}, u32[]{:S(2)}, u32[]{:S(2)}) collective-permute-start(f32[200,128]{1,0:T(8,128)S(1)} %get-tuple-element.119), channel_id=1, source_target_pairs={{0,2},{2,0},{4,6},{6,4},{8,10},{10,8},{12,14},{14,12},{16,18},{18,... | collective-permute-start | bytes 307208 | tf_op jit(solution)/shard_map/ppermute | solution.py:536
  38.2 2.3 %collective-permute-start.11 = (f32[200,128]{1,0:T(8,128)S(1)}, f32[200,128]{1,0:T(8,128)S(1)}, u32[]{:S(2)}, u32[]{:S(2)}) collective-permute-start(f32[200,128]{1,0:T(8,128)S(1)} %get-tuple-element.120), channel_id=1, source_target_pairs={{0,4},{2,6},{4,0},{6,2},{8,12},{10,14},{12,8},{14,10},{16,20},{18,... | collective-permute-start | bytes 307208 | tf_op jit(solution)/shard_map/ppermute | solution.py:536
  41.4 3.5 %collective-permute-done.11.c = f32[200,128]{1,0:T(8,128)S(1)} collective-permute-done((f32[200,128]{1,0:T(8,128)S(1)}, f32[200,128]{1,0:T(8,128)S(1)}, u32[]{:S(2)}, u32[]{:S(2)}) %collective-permute-start.11) | collective-permute-done | bytes 102432 | tf_op jit(solution)/shard_map/ppermute | solution.py:536
  44.9 1.2 %collective-permute-done.12.d = f32[200,128]{1,0:T(8,128)S(1)} collective-permute-done((f32[200,128]{1,0:T(8,128)S(1)}, f32[200,128]{1,0:T(8,128)S(1)}, u32[]{:S(2)}, u32[]{:S(2)}) %collective-permute-start.12) | collective-permute-done | bytes 102432 | tf_op jit(solution)/shard_map/ppermute | solution.py:536
  46.1 1.6 %collective-permute-start.13 = (f32[200,128]{1,0:T(8,128)S(1)}, f32[200,128]{1,0:T(8,128)S(1)}, u32[]{:S(2)}, u32[]{:S(2)}) collective-permute-start(f32[200,128]{1,0:T(8,128)S(1)} %shard_map.150.a), channel_id=1, source_target_pairs={{0,8},{2,10},{4,12},{6,14},{8,0},{10,2},{12,4},{14,6},{16,24},{18,... | collective-permute-start | bytes 307208 | tf_op jit(solution)/shard_map/ppermute | solution.py:536
  47.8 3.1 %collective-permute-done.13.b = f32[200,128]{1,0:T(8,128)S(1)} collective-permute-done((f32[200,128]{1,0:T(8,128)S(1)}, f32[200,128]{1,0:T(8,128)S(1)}, u32[]{:S(2)}, u32[]{:S(2)}) %collective-permute-start.13) | collective-permute-done | bytes 102432 | tf_op jit(solution)/shard_map/ppermute | solution.py:536
  50.9 2.9 %collective-permute-start.14 = (f32[200,128]{1,0:T(8,128)S(1)}, f32[200,128]{1,0:T(8,128)S(1)}, u32[]{:S(2)}, u32[]{:S(2)}) collective-permute-start(f32[200,128]{1,0:T(8,128)S(1)} %shard_map.151.a), channel_id=1, source_target_pairs={{0,16},{2,18},{4,20},{6,22},{8,24},{10,26},{12,28},{14,30},{16,0},... | collective-permute-start | bytes 307208 | tf_op jit(solution)/shard_map/ppermute | solution.py:536
  53.7 2.8 %collective-permute-done.14.b = f32[200,128]{1,0:T(8,128)S(1)} collective-permute-done((f32[200,128]{1,0:T(8,128)S(1)}, f32[200,128]{1,0:T(8,128)S(1)}, u32[]{:S(2)}, u32[]{:S(2)}) %collective-permute-start.14) | collective-permute-done | bytes 102432 | tf_op jit(solution)/shard_map/ppermute | solution.py:536
  56.5 1.1 %collective-permute-start.17 = (f32[192,128]{1,0:T(8,128)S(1)}, f32[192,128]{1,0:T(8,128)S(1)}, u32[]{:S(2)}, u32[]{:S(2)}) collective-permute-start(f32[192,128]{1,0:T(8,128)S(1)} %get-tuple-element.122.refs_0_), channel_id=1, source_target_pairs={{0,6},{2,4},{4,2},{6,0},{8,14},{10,12},{12,10},{14,8},{16,22},{18,... | collective-permute-start | bytes 294920 | tf_op jit(solution)/shard_map/ppermute | solution.py:536
  57.7 1.4 %collective-permute-start.16 = (f32[192,128]{1,0:T(8,128)S(1)}, f32[192,128]{1,0:T(8,128)S(1)}, u32[]{:S(2)}, u32[]{:S(2)}) collective-permute-start(f32[192,128]{1,0:T(8,128)S(1)} %get-tuple-element.122.refs_0_), channel_id=1, source_target_pairs={{0,4},{2,6},{4,0},{6,2},{8,12},{10,14},{12,8},{14,10},{16,20},{18,... | collective-permute-start | bytes 294920 | tf_op jit(solution)/shard_map/ppermute | solution.py:536
  59.1 1.0 %collective-permute-start.15 = (f32[192,128]{1,0:T(8,128)S(1)}, f32[192,128]{1,0:T(8,128)S(1)}, u32[]{:S(2)}, u32[]{:S(2)}) collective-permute-start(f32[192,128]{1,0:T(8,128)S(1)} %get-tuple-element.122.refs_0_), channel_id=1, source_target_pairs={{0,2},{2,0},{4,6},{6,4},{8,10},{10,8},{12,14},{14,12},{16,18},{18,... | collective-permute-start | bytes 294920 | tf_op jit(solution)/shard_map/ppermute | solution.py:536
  60.1 2.1 %collective-permute-done.17.refs_3_ = f32[192,128]{1,0:T(8,128)S(1)} collective-permute-done((f32[192,128]{1,0:T(8,128)S(1)}, f32[192,128]{1,0:T(8,128)S(1)}, u32[]{:S(2)}, u32[]{:S(2)}) %collective-permute-start.17) | collective-permute-done | bytes 98336 | tf_op jit(solution)/shard_map/ppermute | solution.py:536
  65.0 1.1 %shard_map.153 = (f32[1,128]{1,0:T(1,128)}, f32[2,256,128]{2,1,0:T(8,128)}, f32[2,128,128]{2,1,0:T(8,128)}, f32[2,256,128]{2,1,0:T(8,128)}, f32[2,128,128]{2,1,0:T(8,128)}, /*index=5*/f32[1,128]{1,0:T(1,128)}) custom-call(f32[192,128]{1,0:T(8,128)S(1)} %get-tuple-element.122.refs_0_, f32[192,128]{1,0:T(8,128)S(1)} %collective-permute-done.15.refs_1_, ...), custom_call_target="tpu_custom_call" | custom-call | tf_op jit(solution)/shard_map/pallas_call | solution.py:425
  (30 shorter events, 6.3 us)
Async XLA Ops:
  4.1 6.4 %collective-permute-start = (f32[64,128]{1,0:T(8,128)S(1)}, f32[64,128]{1,0:T(8,128)S(1)}, u32[]{:S(2)}, u32[]{:S(2)}) collective-permute-start(f32[64,128]{1,0:T(8,128)S(1)} %get-tuple-element.69.refs_0_), channel_id=1, source_target_pairs={{2,4},{4,2},{6,8},{8,6},{10,12},{12,10},{14,16},{16,14},{18,20},{2... | collective-permute-start | bytes 98312 | tf_op jit(solution)/shard_map/ppermute | solution.py:460
  4.8 7.9 %collective-permute-start.1 = (f32[64,128]{1,0:T(8,128)S(1)}, f32[64,128]{1,0:T(8,128)S(1)}, u32[]{:S(2)}, u32[]{:S(2)}) collective-permute-start(f32[64,128]{1,0:T(8,128)S(1)} %get-tuple-element.70.refs_1_), channel_id=1, source_target_pairs={{0,2},{2,0},{4,6},{6,4},{8,10},{10,8},{12,14},{14,12},{16,18},{18,... | collective-permute-start | bytes 98312 | tf_op jit(solution)/shard_map/ppermute | solution.py:460
  10.6 2.2 %collective-permute-start.2 = (f32[64,128]{1,0:T(8,128)S(1)}, f32[64,128]{1,0:T(8,128)S(1)}, u32[]{:S(2)}, u32[]{:S(2)}) collective-permute-start(f32[64,128]{1,0:T(8,128)S(1)} %get-tuple-element.71.refs_2_), channel_id=1, source_target_pairs={{0,1},{1,0},{2,3},{3,2},{4,5},{5,4},{6,7},{7,6},{8,9},{9,8},{10,11... | collective-permute-start | bytes 98312 | tf_op jit(solution)/shard_map/ppermute | solution.py:460
  14.6 5.2 %collective-permute-start.3 = (f32[136,128]{1,0:T(8,128)S(1)}, f32[136,128]{1,0:T(8,128)S(1)}, u32[]{:S(2)}, u32[]{:S(2)}) collective-permute-start(f32[136,128]{1,0:T(8,128)S(1)} %get-tuple-element.84.refs_0_), channel_id=1, source_target_pairs={{2,4},{4,2},{6,8},{8,6},{10,12},{12,10},{14,16},{16,14},{18,20},{2... | collective-permute-start | bytes 208904 | tf_op jit(solution)/shard_map/ppermute | solution.py:460
  15.3 7.4 %collective-permute-start.4 = (f32[136,128]{1,0:T(8,128)S(1)}, f32[136,128]{1,0:T(8,128)S(1)}, u32[]{:S(2)}, u32[]{:S(2)}) collective-permute-start(f32[136,128]{1,0:T(8,128)S(1)} %get-tuple-element.85.refs_1_), channel_id=1, source_target_pairs={{0,2},{2,0},{4,6},{6,4},{8,10},{10,8},{12,14},{14,12},{16,18},{18,... | collective-permute-start | bytes 208904 | tf_op jit(solution)/shard_map/ppermute | solution.py:460
  19.8 2.9 %collective-permute-start.5 = (f32[136,128]{1,0:T(8,128)S(1)}, f32[136,128]{1,0:T(8,128)S(1)}, u32[]{:S(2)}, u32[]{:S(2)}) collective-permute-start(f32[136,128]{1,0:T(8,128)S(1)} %get-tuple-element.86.refs_2_), channel_id=1, source_target_pairs={{0,1},{1,0},{2,3},{3,2},{4,5},{5,4},{6,7},{7,6},{8,9},{9,8},{10,11... | collective-permute-start | bytes 208904 | tf_op jit(solution)/shard_map/ppermute | solution.py:460
  25.3 5.8 %collective-permute-start.6 = (f32[64,128]{1,0:T(8,128)S(1)}, f32[64,128]{1,0:T(8,128)S(1)}, u32[]{:S(2)}, u32[]{:S(2)}) collective-permute-start(f32[64,128]{1,0:T(8,128)S(1)} %get-tuple-element.93.refs_0_), channel_id=1, source_target_pairs={{2,4},{4,2},{6,8},{8,6},{10,12},{12,10},{14,16},{16,14},{18,20},{2... | collective-permute-start | bytes 98312 | tf_op jit(solution)/shard_map/ppermute | solution.py:460
  26.0 6.7 %collective-permute-start.7 = (f32[64,128]{1,0:T(8,128)S(1)}, f32[64,128]{1,0:T(8,128)S(1)}, u32[]{:S(2)}, u32[]{:S(2)}) collective-permute-start(f32[64,128]{1,0:T(8,128)S(1)} %get-tuple-element.94.refs_1_), channel_id=1, source_target_pairs={{0,2},{2,0},{4,6},{6,4},{8,10},{10,8},{12,14},{14,12},{16,18},{18,... | collective-permute-start | bytes 98312 | tf_op jit(solution)/shard_map/ppermute | solution.py:460
  30.5 2.2 %collective-permute-start.8 = (f32[64,128]{1,0:T(8,128)S(1)}, f32[64,128]{1,0:T(8,128)S(1)}, u32[]{:S(2)}, u32[]{:S(2)}) collective-permute-start(f32[64,128]{1,0:T(8,128)S(1)} %get-tuple-element.95.refs_2_), channel_id=1, source_target_pairs={{0,1},{1,0},{2,3},{3,2},{4,5},{5,4},{6,7},{7,6},{8,9},{9,8},{10,11... | collective-permute-start | bytes 98312 | tf_op jit(solution)/shard_map/ppermute | solution.py:460
  34.5 1.8 %collective-permute-start.9 = (f32[776,128]{1,0:T(8,128)S(1)}, f32[776,128]{1,0:T(8,128)S(1)}, u32[]{:S(2)}, u32[]{:S(2)}) collective-permute-start(f32[776,128]{1,0:T(8,128)S(1)} %get-tuple-element.117), channel_id=1, source_target_pairs={{0,1},{1,0},{2,3},{3,2},{4,5},{5,4},{6,7},{7,6},{8,9},{9,8},{10,11... | collective-permute-start | bytes 1191944 | tf_op jit(solution)/shard_map/ppermute | solution.py:533
  36.4 5.0 %collective-permute-start.10 = (f32[200,128]{1,0:T(8,128)S(1)}, f32[200,128]{1,0:T(8,128)S(1)}, u32[]{:S(2)}, u32[]{:S(2)}) collective-permute-start(f32[200,128]{1,0:T(8,128)S(1)} %get-tuple-element.119), channel_id=1, source_target_pairs={{0,2},{2,0},{4,6},{6,4},{8,10},{10,8},{12,14},{14,12},{16,18},{18,... | collective-permute-start | bytes 307208 | tf_op jit(solution)/shard_map/ppermute | solution.py:536
  38.2 6.7 %collective-permute-start.11 = (f32[200,128]{1,0:T(8,128)S(1)}, f32[200,128]{1,0:T(8,128)S(1)}, u32[]{:S(2)}, u32[]{:S(2)}) collective-permute-start(f32[200,128]{1,0:T(8,128)S(1)} %get-tuple-element.120), channel_id=1, source_target_pairs={{0,4},{2,6},{4,0},{6,2},{8,12},{10,14},{12,8},{14,10},{16,20},{18,... | collective-permute-start | bytes 307208 | tf_op jit(solution)/shard_map/ppermute | solution.py:536
  40.6 5.6 %collective-permute-start.12 = (f32[200,128]{1,0:T(8,128)S(1)}, f32[200,128]{1,0:T(8,128)S(1)}, u32[]{:S(2)}, u32[]{:S(2)}) collective-permute-start(f32[200,128]{1,0:T(8,128)S(1)} %get-tuple-element.121), channel_id=1, source_target_pairs={{0,6},{2,4},{4,2},{6,0},{8,14},{10,12},{12,10},{14,8},{16,22},{18,... | collective-permute-start | bytes 307208 | tf_op jit(solution)/shard_map/ppermute | solution.py:536
  46.1 4.7 %collective-permute-start.13 = (f32[200,128]{1,0:T(8,128)S(1)}, f32[200,128]{1,0:T(8,128)S(1)}, u32[]{:S(2)}, u32[]{:S(2)}) collective-permute-start(f32[200,128]{1,0:T(8,128)S(1)} %shard_map.150.a), channel_id=1, source_target_pairs={{0,8},{2,10},{4,12},{6,14},{8,0},{10,2},{12,4},{14,6},{16,24},{18,... | collective-permute-start | bytes 307208 | tf_op jit(solution)/shard_map/ppermute | solution.py:536
  50.9 5.6 %collective-permute-start.14 = (f32[200,128]{1,0:T(8,128)S(1)}, f32[200,128]{1,0:T(8,128)S(1)}, u32[]{:S(2)}, u32[]{:S(2)}) collective-permute-start(f32[200,128]{1,0:T(8,128)S(1)} %shard_map.151.a), channel_id=1, source_target_pairs={{0,16},{2,18},{4,20},{6,22},{8,24},{10,26},{12,28},{14,30},{16,0},... | collective-permute-start | bytes 307208 | tf_op jit(solution)/shard_map/ppermute | solution.py:536
  56.5 5.7 %collective-permute-start.17 = (f32[192,128]{1,0:T(8,128)S(1)}, f32[192,128]{1,0:T(8,128)S(1)}, u32[]{:S(2)}, u32[]{:S(2)}) collective-permute-start(f32[192,128]{1,0:T(8,128)S(1)} %get-tuple-element.122.refs_0_), channel_id=1, source_target_pairs={{0,6},{2,4},{4,2},{6,0},{8,14},{10,12},{12,10},{14,8},{16,22},{18,... | collective-permute-start | bytes 294920 | tf_op jit(solution)/shard_map/ppermute | solution.py:536
  57.7 5.5 %collective-permute-start.16 = (f32[192,128]{1,0:T(8,128)S(1)}, f32[192,128]{1,0:T(8,128)S(1)}, u32[]{:S(2)}, u32[]{:S(2)}) collective-permute-start(f32[192,128]{1,0:T(8,128)S(1)} %get-tuple-element.122.refs_0_), channel_id=1, source_target_pairs={{0,4},{2,6},{4,0},{6,2},{8,12},{10,14},{12,8},{14,10},{16,20},{18,... | collective-permute-start | bytes 294920 | tf_op jit(solution)/shard_map/ppermute | solution.py:536
  59.1 4.6 %collective-permute-start.15 = (f32[192,128]{1,0:T(8,128)S(1)}, f32[192,128]{1,0:T(8,128)S(1)}, u32[]{:S(2)}, u32[]{:S(2)}) collective-permute-start(f32[192,128]{1,0:T(8,128)S(1)} %get-tuple-element.122.refs_0_), channel_id=1, source_target_pairs={{0,2},{2,0},{4,6},{6,4},{8,10},{10,8},{12,14},{14,12},{16,18},{18,... | collective-permute-start | bytes 294920 | tf_op jit(solution)/shard_map/ppermute | solution.py:536
  60.1 3.6 %collective-permute-start.18 = (f32[192,128]{1,0:T(8,128)S(1)}, f32[192,128]{1,0:T(8,128)S(1)}, u32[]{:S(2)}, u32[]{:S(2)}) collective-permute-start(f32[192,128]{1,0:T(8,128)S(1)} %get-tuple-element.122.refs_0_), channel_id=1, source_target_pairs={{0,1},{1,0},{2,3},{3,2},{4,5},{5,4},{6,7},{7,6},{8,9},{9,8},{10,11... | collective-permute-start | bytes 294920 | tf_op jit(solution)/shard_map/ppermute | solution.py:533
  62.2 1.5 %collective-permute-start.21 = (f32[192,128]{1,0:T(8,128)S(1)}, f32[192,128]{1,0:T(8,128)S(1)}, u32[]{:S(2)}, u32[]{:S(2)}) collective-permute-start(f32[192,128]{1,0:T(8,128)S(1)} %collective-permute-done.17.refs_3_), channel_id=1, source_target_pairs={{0,1},{1,0},{2,3},{3,2},{4,5},{5,4},{6,7},{7,6},{8,9},{9,8},{10,11... | collective-permute-start | bytes 294920 | tf_op jit(solution)/shard_map/ppermute | solution.py:533
  63.2 1.3 %collective-permute-start.20 = (f32[192,128]{1,0:T(8,128)S(1)}, f32[192,128]{1,0:T(8,128)S(1)}, u32[]{:S(2)}, u32[]{:S(2)}) collective-permute-start(f32[192,128]{1,0:T(8,128)S(1)} %collective-permute-done.16.refs_2_), channel_id=1, source_target_pairs={{0,1},{1,0},{2,3},{3,2},{4,5},{5,4},{6,7},{7,6},{8,9},{9,8},{10,11... | collective-permute-start | bytes 294920 | tf_op jit(solution)/shard_map/ppermute | solution.py:533
  63.7 1.3 %collective-permute-start.19 = (f32[192,128]{1,0:T(8,128)S(1)}, f32[192,128]{1,0:T(8,128)S(1)}, u32[]{:S(2)}, u32[]{:S(2)}) collective-permute-start(f32[192,128]{1,0:T(8,128)S(1)} %collective-permute-done.15.refs_1_), channel_id=1, source_target_pairs={{0,1},{1,0},{2,3},{3,2},{4,5},{5,4},{6,7},{7,6},{8,9},{9,8},{10,11... | collective-permute-start | bytes 294920 | tf_op jit(solution)/shard_map/ppermute | solution.py:533

commit v4 on v3

--- a/solution.py
+++ b/solution.py
@@ -6,6 +6,7 @@
 from jax.experimental import pallas as pl
 from jax.experimental.pallas import tpu as pltpu
 from jax.sharding import PartitionSpec as P
+
 
 F32 = jnp.float32
 BF16 = jnp.bfloat16
@@ -124,8 +125,8 @@
 ):
     weights_hbm, refs = refs[:4], refs[4:]
     (target, decoder, edge_in, edge_out, node_in, node_out,
-     flat_out, recv, send, recv_t, send_t, h_out, slope, q_out) = refs[:14]
-    blocks, (feats, index, halo, sems) = refs[14:18], refs[18:]
+     flat_out, recv, send, recv_t, send_t, h_out, slope, q_out, raw) = refs[:15]
+    blocks, (feats, index, halo, sems) = refs[15:19], refs[19:]
     copies = [
         pltpu.make_async_copy(source, place, sems.at[at])
         for at, (source, place) in enumerate(
@@ -161,6 +162,16 @@
         ],
         axis=0,
     )
+    raw[nodes:, :] = jnp.concatenate(
+        [
+            table,
+            jnp.where(dom_even, lists[0:1], lists[1:2]),
+            jnp.where(dom_even, lists[1:2], lists[0:1]),
+            jnp.where(sub_even, lists[3:4], lists[2:3]),
+            jnp.where(sub_even, lists[2:3], lists[3:4]),
+        ],
+        axis=0,
+    )
     flat_row = row_of(flat)
     flat_out[...] = jnp.broadcast_to(flat, flat_out.shape)
     for b in range(count):
@@ -171,7 +182,9 @@
         send_t[:, rows] = onehot(flat == table[count + b : count + b + 1])
     place = onehot(flat == lax.broadcasted_iota(jnp.int32, (nodes, nodes), 1).astype(F32))
     copies[2].wait()
-    features = fold(dot(place, side(feats[...])))
+    plain = feats[...]
+    raw[:nodes, :] = plain
+    features = fold(dot(place, side(plain)))
     h_out[...] = features
     copies[3].wait()
     q = edge_forward(features, edge_in[0], recv, send, recv_t, slope, chunk)
@@ -241,7 +254,7 @@
     own, refs = refs[:4], refs[4:]
     came, refs = unpack(names, refs)
     (flat_ref, decoder, pre_ref, known, node_slope, recv, recv_t, send_t, slope,
-     edge_in, edge_out, node_in, node_out,
+     edge_in, edge_out, node_in, node_out, _,
      agg_out, act_out, pre1_out, seed_out, local_out, recv_out, send_out, top_out, pre0_out,
      pred_out, loss_out, *blocks) = refs
     nodes, width = pre_ref.shape
@@ -302,7 +315,8 @@
 
 def grads_kernel(
     h0, agg0, act0, pre0, top0, h1, agg1, act1, pre1, seed, q1, local1, to_recv1, to_send1,
-    decoder, node_out, loss, high, low, tail
+    decoder, node_out, loss, block, raw, shared, far_slope, far_q, far_recv, far_recv_t, far_send_t,
+    edge_out, high, low, far, tail, *, chunk
 ):
     width = h0.shape[1]
     rows = seed[...]
@@ -321,11 +335,59 @@
     low[0:width, :] = tmm(h0[...], pre0[...])
     low[width : 2 * width, :] = tmm(agg0[...], pre0[...])
     low[2 * width :, :] = tmm(act0[...], top0[...])
+    to_recv, to_send = edge_backward(
+        block[...], edge_out[0], far_recv, far_recv_t, far_send_t, far_slope, chunk
+    )
+    far[0:width, :] = tmm(shared[...], to_recv)
+    far[width : 2 * width, :] = tmm(raw[: h0.shape[0], :], to_send)
+    far[2 * width :, :] = tmm(far_q[...], block[...])
     line = jnp.sum(rows * h1[...], axis=0, keepdims=True)
     line = line + row_product(jnp.sum(rows * act, axis=0, keepdims=True), node_out[1])
     tail[...] = jnp.concatenate([line, loss[...], jnp.zeros((EXTRA - 2, width), F32)], axis=0)
 
 
+def far_kernel(chunk, names, size, *refs):
+    raws, refs = unpack(names, refs)
+    edge_in, refs = refs[0], refs[1:]
+    at = 0
+    for place, raw in enumerate(raws):
+        if raw is None:
+            continue
+        shared_out, slope, q_out, recv, recv_t, send, send_t = refs[at : at + 7]
+        at += 7
+        edges, width = slope.shape
+        nodes = send_t.shape[0]
+        count = edges // width
+        block = jnp.concatenate(
+            [raw[nodes:, :], jnp.zeros((width + nodes - raw.shape[0], width), F32)], axis=0
+        )
+        columns = block.T
+        own = block[2 * count + place : 2 * count + place + 1, :size]
+        down = columns[:size, 2 * count + place : 2 * count + place + 1]
+        along = lax.broadcasted_iota(jnp.int32, (1, nodes), 1).astype(F32)
+        across = lax.broadcasted_iota(jnp.int32, (nodes, 1), 0).astype(F32)
+        for b in range(count):
+            rows = pl.ds(b * width, width)
+            recv[rows, :] = onehot(columns[:, b : b + 1] == own)
+            send[rows, :] = onehot(columns[:, count + b : count + b + 1] == along)
+            recv_t[:, rows] = onehot(down == block[b : b + 1])
+            send_t[:, rows] = onehot(across == block[count + b : count + b + 1])
+        features = raw[:nodes, :]
+        shared = fold(dot(onehot(down == along), side(features)))
+        shared_out[...] = shared
+        to_recv = side(mm(shared, edge_in[0, :width]))
+        to_send = side(mm(features, edge_in[0, width:]))
+        total = None
+        for start in range(0, edges, chunk):
+            rows = pl.ds(start, chunk)
+            pre = fold(dot(recv[rows, :], to_recv) + dot(send[rows, :], to_send))
+            act, rise = silu_parts(pre)
+            slope[rows, :] = rise
+            part = dot(recv_t[:, rows], side(act))
+            total = part if total is None else total + part
+        q_out[...] = fold(total)
+
+
 def put_rows(ref, at, value):
     ref[at : at + value.shape[0], :] = value
     return at + value.shape[0]
@@ -334,14 +396,15 @@
 def end_kernel(chunk, names, *refs):
     own, refs = refs[:4], refs[4:]
     came, refs = unpack(names, refs)
-    h, q, recv, recv_t, send_t, slope, edge_out, node_low, high, tail, mine, other = refs
+    h, q, recv, recv_t, send_t, slope, edge_out, node_low, high, far, tail, mine, other = refs
     local_grad = take_sum(own, came)
     to_recv, to_send = edge_backward(local_grad, edge_out[0], recv, recv_t, send_t, slope, chunk)
+    width = h.shape[1]
     low = [
         node_low[...],
-        tmm(h[...], to_recv),
-        tmm(h[...], to_send),
-        tmm(q[...], local_grad),
+        tmm(h[...], to_recv) + far[0:width, :],
+        tmm(h[...], to_send) + far[width : 2 * width, :],
+        tmm(q[...], local_grad) + far[2 * width :, :],
         tail[...],
     ]
 
@@ -446,16 +509,16 @@
     size = halo_index.shape[2]
     n_dom, n_sub = lax.axis_size("dom"), lax.axis_size("sub")
     count = nodes * n_dom * n_sub
-    if edge_in.shape[0] != 2 or 4 * size != nodes:
+    if n_dom < 3 or edge_in.shape[0] != 2 or 4 * size != nodes:
         raise ValueError("unsupported sizes")
     chunk = 256
     axes = ["dom", "dom", "sub", "sub"]
     links = [pairs(lax.axis_size(axis), offset) for axis, offset in zip(axes, (1, 0, 0, 1))]
     names = tuple(1 if link else 0 for link in links)
 
-    def exchange(blocks):
+    def exchange(blocks, last=4, first=0):
         came = [None] * 4
-        for at in range(4):
+        for at in range(first, last):
             if links[at]:
                 came[at] = lax.ppermute(blocks[at], axes[at], links[at])
         return [block for block in came if block is not None]
@@ -469,15 +532,16 @@
         node_feats, edge_index, halo_index, target.reshape(1, nodes), decoder.reshape(1, width),
         *weights,
     )
+    raw_shape = ((nodes + 2 * edges // width + 4, width), F32)
     shapes = [
         ((1, nodes), F32), ((1, width), F32), *[(weight.shape, F32) for weight in weights],
         ((nodes, 128), F32),
         ((edges, nodes), BF16), ((edges, nodes), BF16),
         ((nodes, edges), BF16), ((nodes, edges), BF16),
-        node_shape, edge_shape, node_shape, *block_shapes,
+        node_shape, edge_shape, node_shape, raw_shape, *block_shapes,
     ]
     (wanted, readout, edge_in, edge_out, node_in, node_out,
-     flat, recv, send, recv_t, send_t, h0, slope0, q0, *blocks) = pl.pallas_call(
+     flat, recv, send, recv_t, send_t, h0, slope0, q0, raw, *blocks) = pl.pallas_call(
         functools.partial(first_kernel, chunk),
         out_shape=[jax.ShapeDtypeStruct(shape, dtype) for shape, dtype in shapes],
         in_specs=[pl.BlockSpec(memory_space=pltpu.HBM)] * len(sources),
@@ -491,43 +555,55 @@
         compiler_params=pltpu.CompilerParams(vmem_limit_bytes=16 * 2**20),
     )(*[pltpu.with_memory_space_constraint(source, pltpu.HBM) for source in sources])
     message = ((2 * size + EXTRA, width), F32)
+    came = exchange(blocks)
+    far_names = (names[0], 0, 0, 0)
+    raws = exchange([raw], 1, 0)
     agg0, h1, act0, gate0, slope1, q1, pre, known, *messages = call(
         functools.partial(middle_kernel, chunk, names),
         [node_shape, node_shape, node_shape, node_shape, edge_shape, node_shape,
          node_shape, node_shape, *[message] * 4],
-        *blocks, *exchange(blocks),
+        *blocks, *came,
         h0, flat, wanted, readout, recv, send, recv_t, node_in, node_out, edge_in, edge_out,
     )
+    came = exchange(messages)
+    far_shapes = [
+        ((size, width), F32), edge_shape, ((size, width), F32),
+        ((edges, size), BF16), ((size, edges), BF16), ((edges, nodes), BF16), ((nodes, edges), BF16),
+    ]
+    fars = call(
+        functools.partial(far_kernel, chunk, far_names, size), far_shapes * len(raws), *raws, edge_in
+    )
+    shared, far_slope, far_q, far_recv, far_recv_t, _, far_send_t = fars
     (agg1, act1, pre1, seed, local1, to_recv1, to_send1, top0, pre0, pred, loss,
      *blocks) = call(
         functools.partial(back_kernel, chunk, count, names),
         [*[node_shape] * 9, ((1, nodes), F32), ((1, width), F32), *block_shapes],
-        *messages, *exchange(messages),
+        *messages, *came,
         flat, readout, pre, known, gate0, recv, recv_t, send_t, slope1,
-        edge_in, edge_out, node_in, node_out,
-    )
-    came = exchange(blocks)
-    high, node_low, tail = call(
-        grads_kernel,
-        [((6 * width, width), F32), ((3 * width, width), F32), ((EXTRA, width), F32)],
+        edge_in, edge_out, node_in, node_out, far_q,
+    )
+    came = exchange(blocks, 4, 1)
+    high, node_low, far, tail = call(
+        functools.partial(grads_kernel, chunk=chunk),
+        [((6 * width, width), F32), ((3 * width, width), F32), ((3 * width, width), F32),
+         ((EXTRA, width), F32)],
         h0, agg0, act0, pre0, top0, h1, agg1, act1, pre1, seed, q1, local1, to_recv1, to_send1,
-        readout, node_out, loss,
+        readout, node_out, loss, blocks[0], *raws, shared, far_slope, far_q, far_recv, far_recv_t,
+        far_send_t, edge_out,
     )
     rows = 6 * width
     groups = n_dom // 4
+    half = ((rows + EXTRA, width), F32)
+    end_grads = call(
+        functools.partial(end_kernel, chunk, (0,) + names[1:]),
+        [half, half],
+        *blocks, *came, h0, q0, recv, recv_t, send_t, slope0, edge_out, node_low, high, far, tail,
+    )
     if n_sub != 2 or n_dom % 4 or groups & (groups - 1) or rows % 32:
-        return slow_tail(
-            count, blocks, came, names, chunk, h0, q0, recv, recv_t, send_t, slope0, edge_out,
-            node_low, high, tail, pred, nodes,
-        )
+        return slow_tail(count, *end_grads, pred)
     per = rows // 4
-    half = ((rows + EXTRA, width), F32)
     quarter = ((per + EXTRA, width), F32)
-    mine, other = call(
-        functools.partial(end_kernel, chunk, names),
-        [half, half],
-        *blocks, *came, h0, q0, recv, recv_t, send_t, slope0, edge_out, node_low, high, tail,
-    )
+    mine, other = end_grads
 
     def swap(value):
         return lax.ppermute(value, "sub", pairs(n_sub, 0))
@@ -568,40 +644,22 @@
     )
 
 
-def low_kernel(chunk, names, *refs):
-    own, refs = refs[:4], refs[4:]
-    came, refs = unpack(names, refs)
-    h, q, recv, recv_t, send_t, slope, edge_out, out = refs
-    local_grad = take_sum(own, came)
-    to_recv, to_send = edge_backward(local_grad, edge_out[0], recv, recv_t, send_t, slope, chunk)
-    width = h.shape[1]
-    out[0:width, :] = tmm(h[...], to_recv)
-    out[width : 2 * width, :] = tmm(h[...], to_send)
-    out[2 * width :, :] = tmm(q[...], local_grad)
-
-
-def slow_tail(
-    count, blocks, came, names, chunk, h0, q0, recv, recv_t, send_t, slope0, edge_out,
-    node_low, high, tail, pred, nodes,
-):
-    width = h0.shape[1]
-    (edge_low,) = call(
-        functools.partial(low_kernel, chunk, names), [((3 * width, width), F32)],
-        *blocks, *came, h0, q0, recv, recv_t, send_t, slope0, edge_out,
-    )
-    total = lax.psum(
-        jnp.concatenate([node_low, edge_low, high, tail], 0), ("dom", "sub")
-    )
-    rows = 12 * width
-    body = total[: rows + 1]
-    params = (rows + 1) * width
+def slow_tail(count, mine, other, pred):
+    first = lax.axis_index("sub") == 0
+    width = mine.shape[1]
+    rows = mine.shape[0] - EXTRA
+    high = jnp.where(first, mine, other)
+    low = jnp.where(first, other, mine)
+    total = lax.psum(jnp.concatenate([low[:rows], high], axis=0), ("dom", "sub"))
+    body = total[: 2 * rows + 1]
+    params = (2 * rows + 1) * width
     scale = 1.0 / jnp.sqrt(jnp.sum(body * body) / params + 1e-06)
-    grads = (total[:rows] * scale).reshape(2, 2, 3 * width, width)
+    grads = (total[: 2 * rows] * scale).reshape(2, 2, 3 * width, width)
     return (
-        total[rows + 1, 0] / count, pred.reshape(nodes),
+        total[2 * rows + 1, 0] / count, pred.reshape(-1),
         grads[:, 1, : 2 * width], grads[:, 1, 2 * width :],
         grads[:, 0, : 2 * width], grads[:, 0, 2 * width :],
-        total[rows] * scale,
+        total[2 * rows] * scale,
     )
 
 

time: 66.3 us -> 66.3 us (level)
  Pallas kernels: 11.5 us -> 14.8 us
  waiting for transfers between devices: 24.7 us -> 21.6 us
    pallas_call x9 -> x10, Pallas kernels: 8.06 us -> 11.4 us  [call(): pl.pallas_call(kernel, out_shape=shapes, in_specs=[VMEM] * len(args), out...]
    ppermute x9, waiting for transfers between devices: 6.7 us -> 3.8 us  [exchange(): came[at] = lax.ppermute(blocks[at], axes[at], links[at])]
  transfers between devices with their start and end apart: 22 -> 22, of which waited for: 14 -> 14; matrix products, arithmetic and copies ran while one was open for 0% -> 0% of each run, Pallas kernels for 1% -> 9%
where the time goes in v4:
time: 66.3 us; the launch traced here: 66 us
  starting transfers between devices  28.8 us (43%)
  waiting for transfers between devices  21.6 us (33%)
  Pallas kernels  14.8 us (22%)
  between operations  0.73 us (1%)
    ppermute x9, starting transfers between devices, exchange(): came[at] = lax.ppermute(blocks[at], axes[at], links[at])  16.8 us
    ppermute x8, waiting for transfers between devices, across(): return lax.ppermute(value, 'dom', [(at, at ^ away) for at in range(n_dom)])  14.8 us
    ppermute x8, starting transfers between devices, across(): return lax.ppermute(value, 'dom', [(at, at ^ away) for at in range(n_dom)])  11.9 us
    pallas_call x10, Pallas kernels, call(): pl.pallas_call(kernel, out_shape=shapes, in_specs=[VMEM] * len(args), out...  11.4 us
    ppermute x9, waiting for transfers between devices, exchange(): came[at] = lax.ppermute(blocks[at], axes[at], links[at])  3.8 us
    pallas_call x1, Pallas kernels, per_device(): pl.pallas_call(functools.partial(first_kernel, chunk), out_shape=[jax.Sha...  3.48 us
    ppermute x5, waiting for transfers between devices, swap(): return lax.ppermute(value, 'sub', pairs(n_sub, 0))  3.01 us
  transfers between devices with their start and end apart: 22, of which 14 were waited for; matrix products, arithmetic and copies ran while one was open for 0% of the time, Pallas kernels for 9%

profile of v4, /device:TPU:0, one launch (start us, length us, event | category | flops | bytes accessed | tf_op | source)
XLA Modules:
  0.0 66.0 jit_solution(13664070837555035045)
XLA Ops:
  0.6 3.5 %shard_map.144 = (f32[1,256]{1,0:T(1,128)S(1)}, f32[1,128]{1,0:T(1,128)S(1)}, f32[2,256,128]{2,1,0:T(8,128)S(1)}, f32[2,128,128]{2,1,0:T(8,128)S(1)}, f32[2,256,...) custom-call(f32[256,128]{1,0:T(8,128)} %feats_hbm.1, ...), custom_call_target="tpu_custom_call" | custom-call | tf_op jit(solution)/shard_map/pallas_call | solution.py:544
  5.5 8.4 %collective-permute-start.1 = (f32[64,128]{1,0:T(8,128)S(1)}, f32[64,128]{1,0:T(8,128)S(1)}, u32[]{:S(2)}, u32[]{:S(2)}) collective-permute-start(f32[64,128]{1,0:T(8,128)S(1)} %get-tuple-element.78.refs_1_), channel_id=1, source_target_pairs={{0,2},{2,0},{4,6},{6,4},{8,10},{10,8},{12,14},{14,12},{16,18},{18,... | collective-permute-start | bytes 98312 | tf_op jit(solution)/shard_map/ppermute | solution.py:523
  13.9 2.1 %collective-permute-done.1.refs_5_ = f32[64,128]{1,0:T(8,128)S(1)} collective-permute-done((f32[64,128]{1,0:T(8,128)S(1)}, f32[64,128]{1,0:T(8,128)S(1)}, u32[]{:S(2)}, u32[]{:S(2)}) %collective-permute-start.1) | collective-permute-done | bytes 32800 | tf_op jit(solution)/shard_map/ppermute | solution.py:523
  16.1 1.9 %shard_map.145 = (f32[256,128]{1,0:T(8,128)S(1)}, f32[256,128]{1,0:T(8,128)S(1)}, f32[256,128]{1,0:T(8,128)S(1)}, f32[256,128]{1,0:T(8,128)S(1)}, f32[1280,128]{...) custom-call(f32[64,128]{1,0:T(8,128)S(1)} %get-tuple-element.77.refs, ...), custom_call_target="tpu_custom_call" | custom-call | tf_op jit(solution)/shard_map/pallas_call | solution.py:488
  18.6 4.9 %collective-permute-start.4 = (f32[136,128]{1,0:T(8,128)S(1)}, f32[136,128]{1,0:T(8,128)S(1)}, u32[]{:S(2)}, u32[]{:S(2)}) collective-permute-start(f32[136,128]{1,0:T(8,128)S(1)} %get-tuple-element.93.refs_1_), channel_id=1, source_target_pairs={{0,2},{2,0},{4,6},{6,4},{8,10},{10,8},{12,14},{14,12},{16,18},{18,... | collective-permute-start | bytes 208904 | tf_op jit(solution)/shard_map/ppermute | solution.py:523
  23.5 2.2 %shard_map.146 = (f32[64,128]{1,0:T(8,128)S(1)}, f32[1280,128]{1,0:T(8,128)S(1)}, f32[64,128]{1,0:T(8,128)S(1)}, bf16[1280,64]{1,0:T(8,128)(2,1)S(1)}, bf16[64,1...) custom-call(f32[280,128]{1,0:T(8,128)S(1)} %collective-permute-done.6.refs_0_.raw, ...), custom_call_target="tpu_custom_call" | custom-call | tf_op jit(solution)/shard_map/pallas_call | solution.py:488
  26.5 2.6 %shard_map.147 = (f32[256,128]{1,0:T(8,128)S(1)}, f32[256,128]{1,0:T(8,128)S(1)}, f32[256,128]{1,0:T(8,128)S(1)}, f32[256,128]{1,0:T(8,128)S(1)}, f32[256,128]{1...) custom-call(f32[136,128]{1,0:T(8,128)S(1)} %get-tuple-element.92.ref, ...), custom_call_target="tpu_custom_call" | custom-call | tf_op jit(solution)/shard_map/pallas_call | solution.py:488
  29.1 1.4 %collective-permute-start.7 = (f32[64,128]{1,0:T(8,128)S(1)}, f32[64,128]{1,0:T(8,128)S(1)}, u32[]{:S(2)}, u32[]{:S(2)}) collective-permute-start(f32[64,128]{1,0:T(8,128)S(1)} %get-tuple-element.104.refs_1_), channel_id=1, source_target_pairs={{0,2},{2,0},{4,6},{6,4},{8,10},{10,8},{12,14},{14,12},{16,18},{18,... | collective-permute-start | bytes 98312 | tf_op jit(solution)/shard_map/ppermute | solution.py:523
  30.5 1.6 %shard_map.148 = (f32[768,128]{1,0:T(8,128)S(1)}, f32[384,128]{1,0:T(8,128)S(1)}, f32[384,128]{1,0:T(8,128)S(1)}, f32[8,128]{1,0:T(8,128)S(1)}) custom-call(f32[256,128]{1,0:T(8,128)S(1)} %get-tuple-element.81.refs_7_.h0.refs_6_, f32[256,128]{1,0:T(8,128)S(1)} %get-tuple-element.109.agg0, f32[256,128]{1,0:T(8,128)S(1)} %get-tuple-element.110.act0, ...), custom_call_target="tpu_custom_call" | custom-call | tf_op jit(solution)/shard_map/pallas_call | solution.py:488
  33.0 1.9 %shard_map.149 = (f32[776,128]{1,0:T(8,128)S(1)}, f32[776,128]{1,0:T(8,128)S(1)}) custom-call(f32[64,128]{1,0:T(8,128)S(1)} %get-tuple-element.103.block.refs_0_, f32[64,128]{1,0:T(8,128)S(1)} %get-tuple-element.104.refs_1_, f32[64,128]{1,0:T(8,128)S(1)} %get-tuple-element.105.refs_2_, f32[64,128]{1,0:T(8,128)S(1)} %get-tuple-element.106.refs_3_, ...), custom_call_target="tpu_custom_call" | custom-call | tf_op jit(solution)/shard_map/pallas_call | solution.py:488
  35.0 1.7 %collective-permute-done.9.other = f32[776,128]{1,0:T(8,128)S(1)} collective-permute-done((f32[776,128]{1,0:T(8,128)S(1)}, f32[776,128]{1,0:T(8,128)S(1)}, u32[]{:S(2)}, u32[]{:S(2)}) %collective-permute-start.9) | collective-permute-done | bytes 397344 | tf_op jit(solution)/shard_map/ppermute | solution.py:609
  36.8 1.4 %collective-permute-start.10 = (f32[200,128]{1,0:T(8,128)S(1)}, f32[200,128]{1,0:T(8,128)S(1)}, u32[]{:S(2)}, u32[]{:S(2)}) collective-permute-start(f32[200,128]{1,0:T(8,128)S(1)} %get-tuple-element.135), channel_id=1, source_target_pairs={{0,2},{2,0},{4,6},{6,4},{8,10},{10,8},{12,14},{14,12},{16,18},{18,... | collective-permute-start | bytes 307208 | tf_op jit(solution)/shard_map/ppermute | solution.py:612
  38.2 2.3 %collective-permute-start.11 = (f32[200,128]{1,0:T(8,128)S(1)}, f32[200,128]{1,0:T(8,128)S(1)}, u32[]{:S(2)}, u32[]{:S(2)}) collective-permute-start(f32[200,128]{1,0:T(8,128)S(1)} %get-tuple-element.136), channel_id=1, source_target_pairs={{0,4},{2,6},{4,0},{6,2},{8,12},{10,14},{12,8},{14,10},{16,20},{18,... | collective-permute-start | bytes 307208 | tf_op jit(solution)/shard_map/ppermute | solution.py:612
  40.5 1.3 %collective-permute-done.10.b = f32[200,128]{1,0:T(8,128)S(1)} collective-permute-done((f32[200,128]{1,0:T(8,128)S(1)}, f32[200,128]{1,0:T(8,128)S(1)}, u32[]{:S(2)}, u32[]{:S(2)}) %collective-permute-start.10) | collective-permute-done | bytes 102432 | tf_op jit(solution)/shard_map/ppermute | solution.py:612
  41.8 3.1 %collective-permute-done.11.c = f32[200,128]{1,0:T(8,128)S(1)} collective-permute-done((f32[200,128]{1,0:T(8,128)S(1)}, f32[200,128]{1,0:T(8,128)S(1)}, u32[]{:S(2)}, u32[]{:S(2)}) %collective-permute-start.11) | collective-permute-done | bytes 102432 | tf_op jit(solution)/shard_map/ppermute | solution.py:612
  44.8 1.2 %collective-permute-done.12.d = f32[200,128]{1,0:T(8,128)S(1)} collective-permute-done((f32[200,128]{1,0:T(8,128)S(1)}, f32[200,128]{1,0:T(8,128)S(1)}, u32[]{:S(2)}, u32[]{:S(2)}) %collective-permute-start.12) | collective-permute-done | bytes 102432 | tf_op jit(solution)/shard_map/ppermute | solution.py:612
  46.1 1.7 %collective-permute-start.13 = (f32[200,128]{1,0:T(8,128)S(1)}, f32[200,128]{1,0:T(8,128)S(1)}, u32[]{:S(2)}, u32[]{:S(2)}) collective-permute-start(f32[200,128]{1,0:T(8,128)S(1)} %shard_map.151.a), channel_id=1, source_target_pairs={{0,8},{2,10},{4,12},{6,14},{8,0},{10,2},{12,4},{14,6},{16,24},{18,... | collective-permute-start | bytes 307208 | tf_op jit(solution)/shard_map/ppermute | solution.py:612
  47.8 3.0 %collective-permute-done.13.b = f32[200,128]{1,0:T(8,128)S(1)} collective-permute-done((f32[200,128]{1,0:T(8,128)S(1)}, f32[200,128]{1,0:T(8,128)S(1)}, u32[]{:S(2)}, u32[]{:S(2)}) %collective-permute-start.13) | collective-permute-done | bytes 102432 | tf_op jit(solution)/shard_map/ppermute | solution.py:612
  50.8 2.9 %collective-permute-start.14 = (f32[200,128]{1,0:T(8,128)S(1)}, f32[200,128]{1,0:T(8,128)S(1)}, u32[]{:S(2)}, u32[]{:S(2)}) collective-permute-start(f32[200,128]{1,0:T(8,128)S(1)} %shard_map.152.a), channel_id=1, source_target_pairs={{0,16},{2,18},{4,20},{6,22},{8,24},{10,26},{12,28},{14,30},{16,0},... | collective-permute-start | bytes 307208 | tf_op jit(solution)/shard_map/ppermute | solution.py:612
  53.8 2.7 %collective-permute-done.14.b = f32[200,128]{1,0:T(8,128)S(1)} collective-permute-done((f32[200,128]{1,0:T(8,128)S(1)}, f32[200,128]{1,0:T(8,128)S(1)}, u32[]{:S(2)}, u32[]{:S(2)}) %collective-permute-start.14) | collective-permute-done | bytes 102432 | tf_op jit(solution)/shard_map/ppermute | solution.py:612
  56.5 1.3 %collective-permute-start.17 = (f32[192,128]{1,0:T(8,128)S(1)}, f32[192,128]{1,0:T(8,128)S(1)}, u32[]{:S(2)}, u32[]{:S(2)}) collective-permute-start(f32[192,128]{1,0:T(8,128)S(1)} %get-tuple-element.138.refs_0_), channel_id=1, source_target_pairs={{0,6},{2,4},{4,2},{6,0},{8,14},{10,12},{12,10},{14,8},{16,22},{18,... | collective-permute-start | bytes 294920 | tf_op jit(solution)/shard_map/ppermute | solution.py:612
  57.8 1.2 %collective-permute-start.16 = (f32[192,128]{1,0:T(8,128)S(1)}, f32[192,128]{1,0:T(8,128)S(1)}, u32[]{:S(2)}, u32[]{:S(2)}) collective-permute-start(f32[192,128]{1,0:T(8,128)S(1)} %get-tuple-element.138.refs_0_), channel_id=1, source_target_pairs={{0,4},{2,6},{4,0},{6,2},{8,12},{10,14},{12,8},{14,10},{16,20},{18,... | collective-permute-start | bytes 294920 | tf_op jit(solution)/shard_map/ppermute | solution.py:612
  60.0 2.1 %collective-permute-done.17.refs_3_ = f32[192,128]{1,0:T(8,128)S(1)} collective-permute-done((f32[192,128]{1,0:T(8,128)S(1)}, f32[192,128]{1,0:T(8,128)S(1)}, u32[]{:S(2)}, u32[]{:S(2)}) %collective-permute-start.17) | collective-permute-done | bytes 98336 | tf_op jit(solution)/shard_map/ppermute | solution.py:612
  64.9 1.1 %shard_map.154 = (f32[1,128]{1,0:T(1,128)}, f32[2,256,128]{2,1,0:T(8,128)}, f32[2,128,128]{2,1,0:T(8,128)}, f32[2,256,128]{2,1,0:T(8,128)}, f32[2,128,128]{2,1,0:T(8,128)}, /*index=5*/f32[1,128]{1,0:T(1,128)}) custom-call(f32[192,128]{1,0:T(8,128)S(1)} %get-tuple-element.138.refs_0_, f32[192,128]{1,0:T(8,128)S(1)} %collective-permute-done.15.refs_1_, ...), custom_call_target="tpu_custom_call" | custom-call | tf_op jit(solution)/shard_map/pallas_call | solution.py:488
  (31 shorter events, 7.7 us)
Async XLA Ops:
  4.1 19.4 %collective-permute-start.6 = (f32[280,128]{1,0:T(8,128)S(1)}, f32[280,128]{1,0:T(8,128)S(1)}, u32[]{:S(2)}, u32[]{:S(2)}) collective-permute-start(f32[280,128]{1,0:T(8,128)S(1)} %get-tuple-element.101), channel_id=1, source_target_pairs={{2,4},{4,2},{6,8},{8,6},{10,12},{12,10},{14,16},{16,14},{18,20},{2... | collective-permute-start | bytes 430088 | tf_op jit(solution)/shard_map/ppermute | solution.py:523
  4.8 9.1 %collective-permute-start = (f32[64,128]{1,0:T(8,128)S(1)}, f32[64,128]{1,0:T(8,128)S(1)}, u32[]{:S(2)}, u32[]{:S(2)}) collective-permute-start(f32[64,128]{1,0:T(8,128)S(1)} %get-tuple-element.77.refs_0_), channel_id=1, source_target_pairs={{2,4},{4,2},{6,8},{8,6},{10,12},{12,10},{14,16},{16,14},{18,20},{2... | collective-permute-start | bytes 98312 | tf_op jit(solution)/shard_map/ppermute | solution.py:523
  5.5 10.6 %collective-permute-start.1 = (f32[64,128]{1,0:T(8,128)S(1)}, f32[64,128]{1,0:T(8,128)S(1)}, u32[]{:S(2)}, u32[]{:S(2)}) collective-permute-start(f32[64,128]{1,0:T(8,128)S(1)} %get-tuple-element.78.refs_1_), channel_id=1, source_target_pairs={{0,2},{2,0},{4,6},{6,4},{8,10},{10,8},{12,14},{14,12},{16,18},{18,... | collective-permute-start | bytes 98312 | tf_op jit(solution)/shard_map/ppermute | solution.py:523
  13.9 2.2 %collective-permute-start.2 = (f32[64,128]{1,0:T(8,128)S(1)}, f32[64,128]{1,0:T(8,128)S(1)}, u32[]{:S(2)}, u32[]{:S(2)}) collective-permute-start(f32[64,128]{1,0:T(8,128)S(1)} %get-tuple-element.79.refs_2_), channel_id=1, source_target_pairs={{0,1},{1,0},{2,3},{3,2},{4,5},{5,4},{6,7},{7,6},{8,9},{9,8},{10,11... | collective-permute-start | bytes 98312 | tf_op jit(solution)/shard_map/ppermute | solution.py:523
  17.9 7.8 %collective-permute-start.3 = (f32[136,128]{1,0:T(8,128)S(1)}, f32[136,128]{1,0:T(8,128)S(1)}, u32[]{:S(2)}, u32[]{:S(2)}) collective-permute-start(f32[136,128]{1,0:T(8,128)S(1)} %get-tuple-element.92.refs_0_), channel_id=1, source_target_pairs={{2,4},{4,2},{6,8},{8,6},{10,12},{12,10},{14,16},{16,14},{18,20},{2... | collective-permute-start | bytes 208904 | tf_op jit(solution)/shard_map/ppermute | solution.py:523
  18.6 7.9 %collective-permute-start.4 = (f32[136,128]{1,0:T(8,128)S(1)}, f32[136,128]{1,0:T(8,128)S(1)}, u32[]{:S(2)}, u32[]{:S(2)}) collective-permute-start(f32[136,128]{1,0:T(8,128)S(1)} %get-tuple-element.93.refs_1_), channel_id=1, source_target_pairs={{0,2},{2,0},{4,6},{6,4},{8,10},{10,8},{12,14},{14,12},{16,18},{18,... | collective-permute-start | bytes 208904 | tf_op jit(solution)/shard_map/ppermute | solution.py:523
  23.5 2.9 %collective-permute-start.5 = (f32[136,128]{1,0:T(8,128)S(1)}, f32[136,128]{1,0:T(8,128)S(1)}, u32[]{:S(2)}, u32[]{:S(2)}) collective-permute-start(f32[136,128]{1,0:T(8,128)S(1)} %get-tuple-element.94.refs_2_), channel_id=1, source_target_pairs={{0,1},{1,0},{2,3},{3,2},{4,5},{5,4},{6,7},{7,6},{8,9},{9,8},{10,11... | collective-permute-start | bytes 208904 | tf_op jit(solution)/shard_map/ppermute | solution.py:523
  29.1 4.0 %collective-permute-start.7 = (f32[64,128]{1,0:T(8,128)S(1)}, f32[64,128]{1,0:T(8,128)S(1)}, u32[]{:S(2)}, u32[]{:S(2)}) collective-permute-start(f32[64,128]{1,0:T(8,128)S(1)} %get-tuple-element.104.refs_1_), channel_id=1, source_target_pairs={{0,2},{2,0},{4,6},{6,4},{8,10},{10,8},{12,14},{14,12},{16,18},{18,... | collective-permute-start | bytes 98312 | tf_op jit(solution)/shard_map/ppermute | solution.py:523
  30.5 2.5 %collective-permute-start.8 = (f32[64,128]{1,0:T(8,128)S(1)}, f32[64,128]{1,0:T(8,128)S(1)}, u32[]{:S(2)}, u32[]{:S(2)}) collective-permute-start(f32[64,128]{1,0:T(8,128)S(1)} %get-tuple-element.105.refs_2_), channel_id=1, source_target_pairs={{0,1},{1,0},{2,3},{3,2},{4,5},{5,4},{6,7},{7,6},{8,9},{9,8},{10,11... | collective-permute-start | bytes 98312 | tf_op jit(solution)/shard_map/ppermute | solution.py:523
  34.9 1.8 %collective-permute-start.9 = (f32[776,128]{1,0:T(8,128)S(1)}, f32[776,128]{1,0:T(8,128)S(1)}, u32[]{:S(2)}, u32[]{:S(2)}) collective-permute-start(f32[776,128]{1,0:T(8,128)S(1)} %get-tuple-element.133), channel_id=1, source_target_pairs={{0,1},{1,0},{2,3},{3,2},{4,5},{5,4},{6,7},{7,6},{8,9},{9,8},{10,11... | collective-permute-start | bytes 1191944 | tf_op jit(solution)/shard_map/ppermute | solution.py:609
  36.8 5.0 %collective-permute-start.10 = (f32[200,128]{1,0:T(8,128)S(1)}, f32[200,128]{1,0:T(8,128)S(1)}, u32[]{:S(2)}, u32[]{:S(2)}) collective-permute-start(f32[200,128]{1,0:T(8,128)S(1)} %get-tuple-element.135), channel_id=1, source_target_pairs={{0,2},{2,0},{4,6},{6,4},{8,10},{10,8},{12,14},{14,12},{16,18},{18,... | collective-permute-start | bytes 307208 | tf_op jit(solution)/shard_map/ppermute | solution.py:612
  38.2 6.6 %collective-permute-start.11 = (f32[200,128]{1,0:T(8,128)S(1)}, f32[200,128]{1,0:T(8,128)S(1)}, u32[]{:S(2)}, u32[]{:S(2)}) collective-permute-start(f32[200,128]{1,0:T(8,128)S(1)} %get-tuple-element.136), channel_id=1, source_target_pairs={{0,4},{2,6},{4,0},{6,2},{8,12},{10,14},{12,8},{14,10},{16,20},{18,... | collective-permute-start | bytes 307208 | tf_op jit(solution)/shard_map/ppermute | solution.py:612
  40.5 5.6 %collective-permute-start.12 = (f32[200,128]{1,0:T(8,128)S(1)}, f32[200,128]{1,0:T(8,128)S(1)}, u32[]{:S(2)}, u32[]{:S(2)}) collective-permute-start(f32[200,128]{1,0:T(8,128)S(1)} %get-tuple-element.137), channel_id=1, source_target_pairs={{0,6},{2,4},{4,2},{6,0},{8,14},{10,12},{12,10},{14,8},{16,22},{18,... | collective-permute-start | bytes 307208 | tf_op jit(solution)/shard_map/ppermute | solution.py:612
  46.1 4.7 %collective-permute-start.13 = (f32[200,128]{1,0:T(8,128)S(1)}, f32[200,128]{1,0:T(8,128)S(1)}, u32[]{:S(2)}, u32[]{:S(2)}) collective-permute-start(f32[200,128]{1,0:T(8,128)S(1)} %shard_map.151.a), channel_id=1, source_target_pairs={{0,8},{2,10},{4,12},{6,14},{8,0},{10,2},{12,4},{14,6},{16,24},{18,... | collective-permute-start | bytes 307208 | tf_op jit(solution)/shard_map/ppermute | solution.py:612
  50.8 5.6 %collective-permute-start.14 = (f32[200,128]{1,0:T(8,128)S(1)}, f32[200,128]{1,0:T(8,128)S(1)}, u32[]{:S(2)}, u32[]{:S(2)}) collective-permute-start(f32[200,128]{1,0:T(8,128)S(1)} %shard_map.152.a), channel_id=1, source_target_pairs={{0,16},{2,18},{4,20},{6,22},{8,24},{10,26},{12,28},{14,30},{16,0},... | collective-permute-start | bytes 307208 | tf_op jit(solution)/shard_map/ppermute | solution.py:612
  56.5 5.7 %collective-permute-start.17 = (f32[192,128]{1,0:T(8,128)S(1)}, f32[192,128]{1,0:T(8,128)S(1)}, u32[]{:S(2)}, u32[]{:S(2)}) collective-permute-start(f32[192,128]{1,0:T(8,128)S(1)} %get-tuple-element.138.refs_0_), channel_id=1, source_target_pairs={{0,6},{2,4},{4,2},{6,0},{8,14},{10,12},{12,10},{14,8},{16,22},{18,... | collective-permute-start | bytes 294920 | tf_op jit(solution)/shard_map/ppermute | solution.py:612
  57.8 5.3 %collective-permute-start.16 = (f32[192,128]{1,0:T(8,128)S(1)}, f32[192,128]{1,0:T(8,128)S(1)}, u32[]{:S(2)}, u32[]{:S(2)}) collective-permute-start(f32[192,128]{1,0:T(8,128)S(1)} %get-tuple-element.138.refs_0_), channel_id=1, source_target_pairs={{0,4},{2,6},{4,0},{6,2},{8,12},{10,14},{12,8},{14,10},{16,20},{18,... | collective-permute-start | bytes 294920 | tf_op jit(solution)/shard_map/ppermute | solution.py:612
  59.0 4.6 %collective-permute-start.15 = (f32[192,128]{1,0:T(8,128)S(1)}, f32[192,128]{1,0:T(8,128)S(1)}, u32[]{:S(2)}, u32[]{:S(2)}) collective-permute-start(f32[192,128]{1,0:T(8,128)S(1)} %get-tuple-element.138.refs_0_), channel_id=1, source_target_pairs={{0,2},{2,0},{4,6},{6,4},{8,10},{10,8},{12,14},{14,12},{16,18},{18,... | collective-permute-start | bytes 294920 | tf_op jit(solution)/shard_map/ppermute | solution.py:612
  60.0 3.6 %collective-permute-start.18 = (f32[192,128]{1,0:T(8,128)S(1)}, f32[192,128]{1,0:T(8,128)S(1)}, u32[]{:S(2)}, u32[]{:S(2)}) collective-permute-start(f32[192,128]{1,0:T(8,128)S(1)} %get-tuple-element.138.refs_0_), channel_id=1, source_target_pairs={{0,1},{1,0},{2,3},{3,2},{4,5},{5,4},{6,7},{7,6},{8,9},{9,8},{10,11... | collective-permute-start | bytes 294920 | tf_op jit(solution)/shard_map/ppermute | solution.py:609
  62.1 1.5 %collective-permute-start.21 = (f32[192,128]{1,0:T(8,128)S(1)}, f32[192,128]{1,0:T(8,128)S(1)}, u32[]{:S(2)}, u32[]{:S(2)}) collective-permute-start(f32[192,128]{1,0:T(8,128)S(1)} %collective-permute-done.17.refs_3_), channel_id=1, source_target_pairs={{0,1},{1,0},{2,3},{3,2},{4,5},{5,4},{6,7},{7,6},{8,9},{9,8},{10,11... | collective-permute-start | bytes 294920 | tf_op jit(solution)/shard_map/ppermute | solution.py:609
  63.1 1.3 %collective-permute-start.20 = (f32[192,128]{1,0:T(8,128)S(1)}, f32[192,128]{1,0:T(8,128)S(1)}, u32[]{:S(2)}, u32[]{:S(2)}) collective-permute-start(f32[192,128]{1,0:T(8,128)S(1)} %collective-permute-done.16.refs_2_), channel_id=1, source_target_pairs={{0,1},{1,0},{2,3},{3,2},{4,5},{5,4},{6,7},{7,6},{8,9},{9,8},{10,11... | collective-permute-start | bytes 294920 | tf_op jit(solution)/shard_map/ppermute | solution.py:609
  63.6 1.3 %collective-permute-start.19 = (f32[192,128]{1,0:T(8,128)S(1)}, f32[192,128]{1,0:T(8,128)S(1)}, u32[]{:S(2)}, u32[]{:S(2)}) collective-permute-start(f32[192,128]{1,0:T(8,128)S(1)} %collective-permute-done.15.refs_1_), channel_id=1, source_target_pairs={{0,1},{1,0},{2,3},{3,2},{4,5},{5,4},{6,7},{7,6},{8,9},{9,8},{10,11... | collective-permute-start | bytes 294920 | tf_op jit(solution)/shard_map/ppermute | solution.py:609

commit v5 on v4

--- a/solution.py
+++ b/solution.py
@@ -108,9 +108,21 @@
         ref[...] = value[at * size : (at + 1) * size]
 
 
+AXES = ("dom", "dom", "sub", "sub")
+OFFSETS = (1, 0, 0, 1)
+
+
+def kept(at, value):
+    if pairs(lax.axis_size(AXES[at]), OFFSETS[at])[1]:
+        partner = jnp.bitwise_xor(lax.axis_index(AXES[at]) + OFFSETS[at], 1) - OFFSETS[at]
+        there = jnp.logical_and(partner >= 0, partner < lax.axis_size(AXES[at]))
+        return jnp.where(there, value, 0.0)
+    return value
+
+
 def take_sum(own, came):
     parts = [
-        ref[...] + came[at][...] if came[at] is not None else ref[...]
+        ref[...] + kept(at, came[at][...]) if came[at] is not None else ref[...]
         for at, ref in enumerate(own)
     ]
     return jnp.concatenate(parts, axis=0)
@@ -231,7 +243,7 @@
         line = row_of(short[rows])
         line = jnp.concatenate([line, jnp.zeros((1, width - size), F32)], axis=1)
         message[2 * size :, :] = jnp.concatenate(
-            [line, jnp.ones((1, width), F32), jnp.zeros((EXTRA - 2, width), F32)], axis=0
+            [line, jnp.zeros((EXTRA - 1, width), F32)], axis=0
         )
     q = edge_forward(features, edge_in[1], recv, send, recv_t, slope, chunk)
     q_out[...] = q
@@ -261,7 +273,7 @@
     size = blocks[0].shape[0]
     summed = jnp.concatenate(
         [
-            ref[:size, :] + came[at][:size, :] if came[at] is not None else ref[:size, :]
+            ref[:size, :] + kept(at, came[at][:size, :]) if came[at] is not None else ref[:size, :]
             for at, ref in enumerate(own)
         ],
         axis=0,
@@ -293,8 +305,7 @@
         far_act, far_gate = silu_parts(came[at][size : 2 * size, :] + pre_agg[rows])
         far_misfit = column_of(came[at][2 * size : 2 * size + 1, :size])
         far_misfit = far_misfit + jnp.sum(far_act * lead, axis=1, keepdims=True)
-        there = came[at][2 * size + 1 : 2 * size + 2, 0:1]
-        far_seed = 2.0 * far_misfit / count * there
+        far_seed = kept(at, 2.0 * far_misfit / count)
         shared.append(pre_grad[rows] + far_seed * lead * far_gate)
     local_grad = mmt(jnp.concatenate(shared, axis=0), node_in[1, width:])
     local_out[...] = local_grad
@@ -335,12 +346,13 @@
     low[0:width, :] = tmm(h0[...], pre0[...])
     low[width : 2 * width, :] = tmm(agg0[...], pre0[...])
     low[2 * width :, :] = tmm(act0[...], top0[...])
+    far_grad = kept(0, block[...])
     to_recv, to_send = edge_backward(
-        block[...], edge_out[0], far_recv, far_recv_t, far_send_t, far_slope, chunk
+        far_grad, edge_out[0], far_recv, far_recv_t, far_send_t, far_slope, chunk
     )
     far[0:width, :] = tmm(shared[...], to_recv)
     far[width : 2 * width, :] = tmm(raw[: h0.shape[0], :], to_send)
-    far[2 * width :, :] = tmm(far_q[...], block[...])
+    far[2 * width :, :] = tmm(far_q[...], far_grad)
     line = jnp.sum(rows * h1[...], axis=0, keepdims=True)
     line = line + row_product(jnp.sum(rows * act, axis=0, keepdims=True), node_out[1])
     tail[...] = jnp.concatenate([line, loss[...], jnp.zeros((EXTRA - 2, width), F32)], axis=0)
@@ -498,7 +510,23 @@
     found = []
     for low in range(offset, count - 1, 2):
         found += [(low, low + 1), (low + 1, low)]
-    return found
+    paired = [source for source, _ in found]
+    return found, [at for at in range(count) if found and at not in paired]
+
+
+def moves(n_dom, n_sub, at):
+    along, other = (n_dom, n_sub) if AXES[at] == "dom" else (n_sub, n_dom)
+    found, alone = pairs(along, OFFSETS[at])
+
+    def spot(here, there):
+        return here * n_sub + there if AXES[at] == "dom" else there * n_sub + here
+
+    listed = []
+    for there in range(other):
+        listed += [(spot(source, there), spot(target, there)) for source, target in found]
+        beside = there if other % 2 else there ^ 1
+        listed += [(spot(end, there), spot(end, beside)) for end in alone]
+    return listed
 
 
 def per_device(
@@ -512,15 +540,14 @@
     if n_dom < 3 or edge_in.shape[0] != 2 or 4 * size != nodes:
         raise ValueError("unsupported sizes")
     chunk = 256
-    axes = ["dom", "dom", "sub", "sub"]
-    links = [pairs(lax.axis_size(axis), offset) for axis, offset in zip(axes, (1, 0, 0, 1))]
+    links = [moves(n_dom, n_sub, at) for at in range(4)]
     names = tuple(1 if link else 0 for link in links)
 
     def exchange(blocks, last=4, first=0):
         came = [None] * 4
         for at in range(first, last):
             if links[at]:
-                came[at] = lax.ppermute(blocks[at], axes[at], links[at])
+                came[at] = lax.ppermute(blocks[at], ("dom", "sub"), links[at])
         return [block for block in came if block is not None]
 
     node_shape = ((nodes, width), F32)
@@ -606,22 +633,26 @@
     mine, other = end_grads
 
     def swap(value):
-        return lax.ppermute(value, "sub", pairs(n_sub, 0))
+        return lax.ppermute(value, "sub", pairs(n_sub, 0)[0])
 
     def across(value, away):
         return lax.ppermute(value, "dom", [(at, at ^ away) for at in range(n_dom)])
+
+    def beside(value, first, second):
+        moves = [
+            (at * n_sub + core, (at ^ away) * n_sub + core)
+            for at in range(n_dom)
+            for core, away in enumerate((first, second))
+        ]
+        return lax.ppermute(value, ("dom", "sub"), moves)
 
     parts = call(quarters_kernel, [quarter] * 4, mine, swap(other))
     came = [across(parts[away], away) for away in (3, 2, 1)]
     (total,) = call(four_kernel, [quarter], parts[0], came[2], came[1], came[0])
-    away = 4
-    while away < n_dom // 2:
-        (total,) = call(two_kernel, [quarter], total, across(total, away))
-        away *= 2
-    if away < n_dom:
-        far = across(total, away)
-    else:
-        far = jnp.zeros_like(total)
+    aways = [4 << at for at in range(groups.bit_length() - 1)]
+    for step in range(len(aways) - 1):
+        (total,) = call(two_kernel, [quarter], total, beside(total, aways[step], aways[-1 - step]))
+    far = beside(total, aways[-1], aways[0]) if aways else jnp.zeros_like(total)
     total, tail = call(
         last_sum_kernel, [((per, width), F32), ((EXTRA, width), F32)], total, far
     )

time: 66.3 us -> 61.2 us (0.923)
  starting transfers between devices: 28.8 us -> 22.2 us
  waiting for transfers between devices: 21.6 us -> 23.2 us
    ppermute x14 -> x16, waiting for transfers between devices: 6.8 us -> 14.2 us  [the longest x2 6.05 us: beside(): return lax.ppermute(value, ('dom', 'sub'), moves)]
    ppermute x8 -> x6, waiting for transfers between devices: 14.8 us -> 8.95 us  [across(): return lax.ppermute(value, 'dom', [(at, at ^ away) for at in range(n_dom)])]
    ppermute x8 -> x6, starting transfers between devices: 11.9 us -> 7.11 us  [across(): return lax.ppermute(value, 'dom', [(at, at ^ away) for at in range(n_dom)])]
    ppermute x14 -> x16, starting transfers between devices: 16.9 us -> 15.1 us  [the longest x9 10.6 us: exchange(): came[at] = lax.ppermute(blocks[at], ('dom', 'sub'), links[at])]
where the time goes in v5:
time: 61.2 us; the launch traced here: 60.9 us
  waiting for transfers between devices  23.2 us (38%)
  starting transfers between devices  22.2 us (36%)
  Pallas kernels  14.9 us (24%)
  between operations  0.72 us (1%)
    pallas_call x10, Pallas kernels, call(): pl.pallas_call(kernel, out_shape=shapes, in_specs=[VMEM] * len(args), out...  11.4 us
    ppermute x9, starting transfers between devices, exchange(): came[at] = lax.ppermute(blocks[at], ('dom', 'sub'), links[at])  10.6 us
    ppermute x6, waiting for transfers between devices, across(): return lax.ppermute(value, 'dom', [(at, at ^ away) for at in range(n_dom)])  8.95 us
    ppermute x6, starting transfers between devices, across(): return lax.ppermute(value, 'dom', [(at, at ^ away) for at in range(n_dom)])  7.11 us
    ppermute x2, waiting for transfers between devices, beside(): return lax.ppermute(value, ('dom', 'sub'), moves)  6.05 us
    ppermute x9, waiting for transfers between devices, exchange(): came[at] = lax.ppermute(blocks[at], ('dom', 'sub'), links[at])  5.29 us
    ppermute x2, starting transfers between devices, beside(): return lax.ppermute(value, ('dom', 'sub'), moves)  4.31 us
    pallas_call x1, Pallas kernels, per_device(): pl.pallas_call(functools.partial(first_kernel, chunk), out_shape=[jax.Sha...  3.48 us
  transfers between devices with their start and end apart: 22, of which 14 were waited for; matrix products, arithmetic and copies ran while one was open for 0% of the time, Pallas kernels for 9%

profile of v5, /device:TPU:0, one launch (start us, length us, event | category | flops | bytes accessed | tf_op | source)
XLA Modules:
  0.0 60.9 jit_solution(3498921286913025804)
XLA Ops:
  0.6 3.5 %shard_map.144 = (f32[1,256]{1,0:T(1,128)S(1)}, f32[1,128]{1,0:T(1,128)S(1)}, f32[2,256,128]{2,1,0:T(8,128)S(1)}, f32[2,128,128]{2,1,0:T(8,128)S(1)}, f32[2,256,...) custom-call(f32[256,128]{1,0:T(8,128)} %feats_hbm.1, ...), custom_call_target="tpu_custom_call" | custom-call | tf_op jit(solution)/shard_map/pallas_call | solution.py:571
  4.8 5.3 %collective-permute-start.1 = (f32[64,128]{1,0:T(8,128)S(1)}, f32[64,128]{1,0:T(8,128)S(1)}, u32[]{:S(2)}, u32[]{:S(2)}) collective-permute-start(f32[64,128]{1,0:T(8,128)S(1)} %get-tuple-element.78.refs_1_), channel_id=1, source_target_pairs={{0,2},{2,0},{4,6},{6,4},{8,10},{10,8},{12,14},{14,12},{16,18},{18,... | collective-permute-start | bytes 98312 | tf_op jit(solution)/shard_map/ppermute | solution.py:550
  10.1 3.4 %collective-permute-done.1.refs_5_ = f32[64,128]{1,0:T(8,128)S(1)} collective-permute-done((f32[64,128]{1,0:T(8,128)S(1)}, f32[64,128]{1,0:T(8,128)S(1)}, u32[]{:S(2)}, u32[]{:S(2)}) %collective-permute-start.1) | collective-permute-done | bytes 32800 | tf_op jit(solution)/shard_map/ppermute | solution.py:550
  13.5 1.9 %shard_map.145 = (f32[256,128]{1,0:T(8,128)S(1)}, f32[256,128]{1,0:T(8,128)S(1)}, f32[256,128]{1,0:T(8,128)S(1)}, f32[256,128]{1,0:T(8,128)S(1)}, f32[1280,128]{...) custom-call(f32[64,128]{1,0:T(8,128)S(1)} %get-tuple-element.77.refs, ...), custom_call_target="tpu_custom_call" | custom-call | tf_op jit(solution)/shard_map/pallas_call | solution.py:500
  15.5 2.6 %collective-permute-start.4 = (f32[136,128]{1,0:T(8,128)S(1)}, f32[136,128]{1,0:T(8,128)S(1)}, u32[]{:S(2)}, u32[]{:S(2)}) collective-permute-start(f32[136,128]{1,0:T(8,128)S(1)} %get-tuple-element.93.refs_1_), channel_id=1, source_target_pairs={{0,2},{2,0},{4,6},{6,4},{8,10},{10,8},{12,14},{14,12},{16,18},{18,... | collective-permute-start | bytes 208904 | tf_op jit(solution)/shard_map/ppermute | solution.py:550
  18.1 2.2 %shard_map.146 = (f32[64,128]{1,0:T(8,128)S(1)}, f32[1280,128]{1,0:T(8,128)S(1)}, f32[64,128]{1,0:T(8,128)S(1)}, bf16[1280,64]{1,0:T(8,128)(2,1)S(1)}, bf16[64,1...) custom-call(f32[280,128]{1,0:T(8,128)S(1)} %collective-permute-done.6.refs_0_.raw, ...), custom_call_target="tpu_custom_call" | custom-call | tf_op jit(solution)/shard_map/pallas_call | solution.py:500
  20.3 1.4 %collective-permute-done.4.refs_5_ = f32[136,128]{1,0:T(8,128)S(1)} collective-permute-done((f32[136,128]{1,0:T(8,128)S(1)}, f32[136,128]{1,0:T(8,128)S(1)}, u32[]{:S(2)}, u32[]{:S(2)}) %collective-permute-start.4) | collective-permute-done | bytes 69664 | tf_op jit(solution)/shard_map/ppermute | solution.py:550
  21.7 2.6 %shard_map.147 = (f32[256,128]{1,0:T(8,128)S(1)}, f32[256,128]{1,0:T(8,128)S(1)}, f32[256,128]{1,0:T(8,128)S(1)}, f32[256,128]{1,0:T(8,128)S(1)}, f32[256,128]{1...) custom-call(f32[136,128]{1,0:T(8,128)S(1)} %get-tuple-element.92.ref, ...), custom_call_target="tpu_custom_call" | custom-call | tf_op jit(solution)/shard_map/pallas_call | solution.py:500
  24.3 2.0 %collective-permute-start.7 = (f32[64,128]{1,0:T(8,128)S(1)}, f32[64,128]{1,0:T(8,128)S(1)}, u32[]{:S(2)}, u32[]{:S(2)}) collective-permute-start(f32[64,128]{1,0:T(8,128)S(1)} %get-tuple-element.104.refs_1_), channel_id=1, source_target_pairs={{0,2},{2,0},{4,6},{6,4},{8,10},{10,8},{12,14},{14,12},{16,18},{18,... | collective-permute-start | bytes 98312 | tf_op jit(solution)/shard_map/ppermute | solution.py:550
  26.3 1.6 %shard_map.148 = (f32[768,128]{1,0:T(8,128)S(1)}, f32[384,128]{1,0:T(8,128)S(1)}, f32[384,128]{1,0:T(8,128)S(1)}, f32[8,128]{1,0:T(8,128)S(1)}) custom-call(f32[256,128]{1,0:T(8,128)S(1)} %get-tuple-element.81.refs_7_.h0.refs_6_, f32[256,128]{1,0:T(8,128)S(1)} %get-tuple-element.109.agg0, f32[256,128]{1,0:T(8,128)S(1)} %get-tuple-element.110.act0, ...), custom_call_target="tpu_custom_call" | custom-call | tf_op jit(solution)/shard_map/pallas_call | solution.py:500
  28.3 1.9 %shard_map.149 = (f32[776,128]{1,0:T(8,128)S(1)}, f32[776,128]{1,0:T(8,128)S(1)}) custom-call(f32[64,128]{1,0:T(8,128)S(1)} %get-tuple-element.103.block.refs_0_, f32[64,128]{1,0:T(8,128)S(1)} %get-tuple-element.104.refs_1_, f32[64,128]{1,0:T(8,128)S(1)} %get-tuple-element.105.refs_2_, f32[64,128]{1,0:T(8,128)S(1)} %get-tuple-element.106.refs_3_, ...), custom_call_target="tpu_custom_call" | custom-call | tf_op jit(solution)/shard_map/pallas_call | solution.py:500
  30.4 1.6 %collective-permute-done.9.other = f32[776,128]{1,0:T(8,128)S(1)} collective-permute-done((f32[776,128]{1,0:T(8,128)S(1)}, f32[776,128]{1,0:T(8,128)S(1)}, u32[]{:S(2)}, u32[]{:S(2)}) %collective-permute-start.9) | collective-permute-done | bytes 397344 | tf_op jit(solution)/shard_map/ppermute | solution.py:636
  32.0 1.9 %collective-permute-start.10 = (f32[200,128]{1,0:T(8,128)S(1)}, f32[200,128]{1,0:T(8,128)S(1)}, u32[]{:S(2)}, u32[]{:S(2)}) collective-permute-start(f32[200,128]{1,0:T(8,128)S(1)} %get-tuple-element.135), channel_id=1, source_target_pairs={{0,2},{2,0},{4,6},{6,4},{8,10},{10,8},{12,14},{14,12},{16,18},{18,... | collective-permute-start | bytes 307208 | tf_op jit(solution)/shard_map/ppermute | solution.py:639
  34.0 1.3 %collective-permute-start.11 = (f32[200,128]{1,0:T(8,128)S(1)}, f32[200,128]{1,0:T(8,128)S(1)}, u32[]{:S(2)}, u32[]{:S(2)}) collective-permute-start(f32[200,128]{1,0:T(8,128)S(1)} %get-tuple-element.136), channel_id=1, source_target_pairs={{0,4},{2,6},{4,0},{6,2},{8,12},{10,14},{12,8},{14,10},{16,20},{18,... | collective-permute-start | bytes 307208 | tf_op jit(solution)/shard_map/ppermute | solution.py:639
  35.6 1.7 %collective-permute-done.10.b = f32[200,128]{1,0:T(8,128)S(1)} collective-permute-done((f32[200,128]{1,0:T(8,128)S(1)}, f32[200,128]{1,0:T(8,128)S(1)}, u32[]{:S(2)}, u32[]{:S(2)}) %collective-permute-start.10) | collective-permute-done | bytes 102432 | tf_op jit(solution)/shard_map/ppermute | solution.py:639
  37.2 2.5 %collective-permute-done.11.c = f32[200,128]{1,0:T(8,128)S(1)} collective-permute-done((f32[200,128]{1,0:T(8,128)S(1)}, f32[200,128]{1,0:T(8,128)S(1)}, u32[]{:S(2)}, u32[]{:S(2)}) %collective-permute-start.11) | collective-permute-done | bytes 102432 | tf_op jit(solution)/shard_map/ppermute | solution.py:639
  39.7 1.1 %collective-permute-done.12.d = f32[200,128]{1,0:T(8,128)S(1)} collective-permute-done((f32[200,128]{1,0:T(8,128)S(1)}, f32[200,128]{1,0:T(8,128)S(1)}, u32[]{:S(2)}, u32[]{:S(2)}) %collective-permute-start.12) | collective-permute-done | bytes 102432 | tf_op jit(solution)/shard_map/ppermute | solution.py:639
  40.9 1.6 %collective-permute-start.13 = (f32[200,128]{1,0:T(8,128)S(1)}, f32[200,128]{1,0:T(8,128)S(1)}, u32[]{:S(2)}, u32[]{:S(2)}) collective-permute-start(f32[200,128]{1,0:T(8,128)S(1)} %shard_map.151.a), channel_id=1, source_target_pairs={{0,8},{1,17},{2,10},{3,19},{4,12},{5,21},{6,14},{7,23},{8,0},{9,25... | collective-permute-start | bytes 307208 | tf_op jit(solution)/shard_map/ppermute | solution.py:647
  42.5 3.1 %collective-permute-done.13.b = f32[200,128]{1,0:T(8,128)S(1)} collective-permute-done((f32[200,128]{1,0:T(8,128)S(1)}, f32[200,128]{1,0:T(8,128)S(1)}, u32[]{:S(2)}, u32[]{:S(2)}) %collective-permute-start.13) | collective-permute-done | bytes 102432 | tf_op jit(solution)/shard_map/ppermute | solution.py:647
  45.6 2.7 %collective-permute-start.14 = (f32[200,128]{1,0:T(8,128)S(1)}, f32[200,128]{1,0:T(8,128)S(1)}, u32[]{:S(2)}, u32[]{:S(2)}) collective-permute-start(f32[200,128]{1,0:T(8,128)S(1)} %shard_map.152.a), channel_id=1, source_target_pairs={{0,16},{1,9},{2,18},{3,11},{4,20},{5,13},{6,22},{7,15},{8,24},{9,1... | collective-permute-start | bytes 307208 | tf_op jit(solution)/shard_map/ppermute | solution.py:647
  48.3 3.0 %collective-permute-done.14.b = f32[200,128]{1,0:T(8,128)S(1)} collective-permute-done((f32[200,128]{1,0:T(8,128)S(1)}, f32[200,128]{1,0:T(8,128)S(1)}, u32[]{:S(2)}, u32[]{:S(2)}) %collective-permute-start.14) | collective-permute-done | bytes 102432 | tf_op jit(solution)/shard_map/ppermute | solution.py:647
  51.3 1.5 %collective-permute-start.17 = (f32[192,128]{1,0:T(8,128)S(1)}, f32[192,128]{1,0:T(8,128)S(1)}, u32[]{:S(2)}, u32[]{:S(2)}) collective-permute-start(f32[192,128]{1,0:T(8,128)S(1)} %get-tuple-element.138.refs_0_), channel_id=1, source_target_pairs={{0,6},{2,4},{4,2},{6,0},{8,14},{10,12},{12,10},{14,8},{16,22},{18,... | collective-permute-start | bytes 294920 | tf_op jit(solution)/shard_map/ppermute | solution.py:639
  54.8 2.1 %collective-permute-done.17.refs_3_ = f32[192,128]{1,0:T(8,128)S(1)} collective-permute-done((f32[192,128]{1,0:T(8,128)S(1)}, f32[192,128]{1,0:T(8,128)S(1)}, u32[]{:S(2)}, u32[]{:S(2)}) %collective-permute-start.17) | collective-permute-done | bytes 98336 | tf_op jit(solution)/shard_map/ppermute | solution.py:639
  59.8 1.1 %shard_map.154 = (f32[1,128]{1,0:T(1,128)}, f32[2,256,128]{2,1,0:T(8,128)}, f32[2,128,128]{2,1,0:T(8,128)}, f32[2,256,128]{2,1,0:T(8,128)}, f32[2,128,128]{2,1,0:T(8,128)}, /*index=5*/f32[1,128]{1,0:T(1,128)}) custom-call(f32[192,128]{1,0:T(8,128)S(1)} %get-tuple-element.138.refs_0_, f32[192,128]{1,0:T(8,128)S(1)} %collective-permute-done.15.refs_1_, ...), custom_call_target="tpu_custom_call" | custom-call | tf_op jit(solution)/shard_map/pallas_call | solution.py:500
  (31 shorter events, 6.7 us)
Async XLA Ops:
  4.1 13.9 %collective-permute-start.6 = (f32[280,128]{1,0:T(8,128)S(1)}, f32[280,128]{1,0:T(8,128)S(1)}, u32[]{:S(2)}, u32[]{:S(2)}) collective-permute-start(f32[280,128]{1,0:T(8,128)S(1)} %get-tuple-element.101), channel_id=1, source_target_pairs={{2,4},{4,2},{6,8},{8,6},{10,12},{12,10},{14,16},{16,14},{18,20},{2... | collective-permute-start | bytes 430088 | tf_op jit(solution)/shard_map/ppermute | solution.py:550
  4.7 5.4 %collective-permute-start = (f32[64,128]{1,0:T(8,128)S(1)}, f32[64,128]{1,0:T(8,128)S(1)}, u32[]{:S(2)}, u32[]{:S(2)}) collective-permute-start(f32[64,128]{1,0:T(8,128)S(1)} %get-tuple-element.77.refs_0_), channel_id=1, source_target_pairs={{2,4},{4,2},{6,8},{8,6},{10,12},{12,10},{14,16},{16,14},{18,20},{2... | collective-permute-start | bytes 98312 | tf_op jit(solution)/shard_map/ppermute | solution.py:550
  4.8 8.8 %collective-permute-start.1 = (f32[64,128]{1,0:T(8,128)S(1)}, f32[64,128]{1,0:T(8,128)S(1)}, u32[]{:S(2)}, u32[]{:S(2)}) collective-permute-start(f32[64,128]{1,0:T(8,128)S(1)} %get-tuple-element.78.refs_1_), channel_id=1, source_target_pairs={{0,2},{2,0},{4,6},{6,4},{8,10},{10,8},{12,14},{14,12},{16,18},{18,... | collective-permute-start | bytes 98312 | tf_op jit(solution)/shard_map/ppermute | solution.py:550
  10.1 3.4 %collective-permute-start.2 = (f32[64,128]{1,0:T(8,128)S(1)}, f32[64,128]{1,0:T(8,128)S(1)}, u32[]{:S(2)}, u32[]{:S(2)}) collective-permute-start(f32[64,128]{1,0:T(8,128)S(1)} %get-tuple-element.79.refs_2_), channel_id=1, source_target_pairs={{0,1},{1,0},{2,3},{3,2},{4,5},{5,4},{6,7},{7,6},{8,9},{9,8},{10,11... | collective-permute-start | bytes 98312 | tf_op jit(solution)/shard_map/ppermute | solution.py:550
  15.4 4.9 %collective-permute-start.3 = (f32[136,128]{1,0:T(8,128)S(1)}, f32[136,128]{1,0:T(8,128)S(1)}, u32[]{:S(2)}, u32[]{:S(2)}) collective-permute-start(f32[136,128]{1,0:T(8,128)S(1)} %get-tuple-element.92.refs_0_), channel_id=1, source_target_pairs={{2,4},{4,2},{6,8},{8,6},{10,12},{12,10},{14,16},{16,14},{18,20},{2... | collective-permute-start | bytes 208904 | tf_op jit(solution)/shard_map/ppermute | solution.py:550
  15.5 6.2 %collective-permute-start.4 = (f32[136,128]{1,0:T(8,128)S(1)}, f32[136,128]{1,0:T(8,128)S(1)}, u32[]{:S(2)}, u32[]{:S(2)}) collective-permute-start(f32[136,128]{1,0:T(8,128)S(1)} %get-tuple-element.93.refs_1_), channel_id=1, source_target_pairs={{0,2},{2,0},{4,6},{6,4},{8,10},{10,8},{12,14},{14,12},{16,18},{18,... | collective-permute-start | bytes 208904 | tf_op jit(solution)/shard_map/ppermute | solution.py:550
  18.0 3.7 %collective-permute-start.5 = (f32[136,128]{1,0:T(8,128)S(1)}, f32[136,128]{1,0:T(8,128)S(1)}, u32[]{:S(2)}, u32[]{:S(2)}) collective-permute-start(f32[136,128]{1,0:T(8,128)S(1)} %get-tuple-element.94.refs_2_), channel_id=1, source_target_pairs={{0,1},{1,0},{2,3},{3,2},{4,5},{5,4},{6,7},{7,6},{8,9},{9,8},{10,11... | collective-permute-start | bytes 208904 | tf_op jit(solution)/shard_map/ppermute | solution.py:550
  24.3 4.0 %collective-permute-start.7 = (f32[64,128]{1,0:T(8,128)S(1)}, f32[64,128]{1,0:T(8,128)S(1)}, u32[]{:S(2)}, u32[]{:S(2)}) collective-permute-start(f32[64,128]{1,0:T(8,128)S(1)} %get-tuple-element.104.refs_1_), channel_id=1, source_target_pairs={{0,2},{2,0},{4,6},{6,4},{8,10},{10,8},{12,14},{14,12},{16,18},{18,... | collective-permute-start | bytes 98312 | tf_op jit(solution)/shard_map/ppermute | solution.py:550
  26.3 2.0 %collective-permute-start.8 = (f32[64,128]{1,0:T(8,128)S(1)}, f32[64,128]{1,0:T(8,128)S(1)}, u32[]{:S(2)}, u32[]{:S(2)}) collective-permute-start(f32[64,128]{1,0:T(8,128)S(1)} %get-tuple-element.105.refs_2_), channel_id=1, source_target_pairs={{0,1},{1,0},{2,3},{3,2},{4,5},{5,4},{6,7},{7,6},{8,9},{9,8},{10,11... | collective-permute-start | bytes 98312 | tf_op jit(solution)/shard_map/ppermute | solution.py:550
  30.2 1.8 %collective-permute-start.9 = (f32[776,128]{1,0:T(8,128)S(1)}, f32[776,128]{1,0:T(8,128)S(1)}, u32[]{:S(2)}, u32[]{:S(2)}) collective-permute-start(f32[776,128]{1,0:T(8,128)S(1)} %get-tuple-element.133), channel_id=1, source_target_pairs={{0,1},{1,0},{2,3},{3,2},{4,5},{5,4},{6,7},{7,6},{8,9},{9,8},{10,11... | collective-permute-start | bytes 1191944 | tf_op jit(solution)/shard_map/ppermute | solution.py:636
  32.0 5.2 %collective-permute-start.10 = (f32[200,128]{1,0:T(8,128)S(1)}, f32[200,128]{1,0:T(8,128)S(1)}, u32[]{:S(2)}, u32[]{:S(2)}) collective-permute-start(f32[200,128]{1,0:T(8,128)S(1)} %get-tuple-element.135), channel_id=1, source_target_pairs={{0,2},{2,0},{4,6},{6,4},{8,10},{10,8},{12,14},{14,12},{16,18},{18,... | collective-permute-start | bytes 307208 | tf_op jit(solution)/shard_map/ppermute | solution.py:639
  34.0 5.8 %collective-permute-start.11 = (f32[200,128]{1,0:T(8,128)S(1)}, f32[200,128]{1,0:T(8,128)S(1)}, u32[]{:S(2)}, u32[]{:S(2)}) collective-permute-start(f32[200,128]{1,0:T(8,128)S(1)} %get-tuple-element.136), channel_id=1, source_target_pairs={{0,4},{2,6},{4,0},{6,2},{8,12},{10,14},{12,8},{14,10},{16,20},{18,... | collective-permute-start | bytes 307208 | tf_op jit(solution)/shard_map/ppermute | solution.py:639
  35.3 5.6 %collective-permute-start.12 = (f32[200,128]{1,0:T(8,128)S(1)}, f32[200,128]{1,0:T(8,128)S(1)}, u32[]{:S(2)}, u32[]{:S(2)}) collective-permute-start(f32[200,128]{1,0:T(8,128)S(1)} %get-tuple-element.137), channel_id=1, source_target_pairs={{0,6},{2,4},{4,2},{6,0},{8,14},{10,12},{12,10},{14,8},{16,22},{18,... | collective-permute-start | bytes 307208 | tf_op jit(solution)/shard_map/ppermute | solution.py:639
  40.9 4.7 %collective-permute-start.13 = (f32[200,128]{1,0:T(8,128)S(1)}, f32[200,128]{1,0:T(8,128)S(1)}, u32[]{:S(2)}, u32[]{:S(2)}) collective-permute-start(f32[200,128]{1,0:T(8,128)S(1)} %shard_map.151.a), channel_id=1, source_target_pairs={{0,8},{1,17},{2,10},{3,19},{4,12},{5,21},{6,14},{7,23},{8,0},{9,25... | collective-permute-start | bytes 307208 | tf_op jit(solution)/shard_map/ppermute | solution.py:647
  45.6 5.6 %collective-permute-start.14 = (f32[200,128]{1,0:T(8,128)S(1)}, f32[200,128]{1,0:T(8,128)S(1)}, u32[]{:S(2)}, u32[]{:S(2)}) collective-permute-start(f32[200,128]{1,0:T(8,128)S(1)} %shard_map.152.a), channel_id=1, source_target_pairs={{0,16},{1,9},{2,18},{3,11},{4,20},{5,13},{6,22},{7,15},{8,24},{9,1... | collective-permute-start | bytes 307208 | tf_op jit(solution)/shard_map/ppermute | solution.py:647
  51.3 5.6 %collective-permute-start.17 = (f32[192,128]{1,0:T(8,128)S(1)}, f32[192,128]{1,0:T(8,128)S(1)}, u32[]{:S(2)}, u32[]{:S(2)}) collective-permute-start(f32[192,128]{1,0:T(8,128)S(1)} %get-tuple-element.138.refs_0_), channel_id=1, source_target_pairs={{0,6},{2,4},{4,2},{6,0},{8,14},{10,12},{12,10},{14,8},{16,22},{18,... | collective-permute-start | bytes 294920 | tf_op jit(solution)/shard_map/ppermute | solution.py:639
  52.8 5.1 %collective-permute-start.16 = (f32[192,128]{1,0:T(8,128)S(1)}, f32[192,128]{1,0:T(8,128)S(1)}, u32[]{:S(2)}, u32[]{:S(2)}) collective-permute-start(f32[192,128]{1,0:T(8,128)S(1)} %get-tuple-element.138.refs_0_), channel_id=1, source_target_pairs={{0,4},{2,6},{4,0},{6,2},{8,12},{10,14},{12,8},{14,10},{16,20},{18,... | collective-permute-start | bytes 294920 | tf_op jit(solution)/shard_map/ppermute | solution.py:639
  53.9 4.6 %collective-permute-start.15 = (f32[192,128]{1,0:T(8,128)S(1)}, f32[192,128]{1,0:T(8,128)S(1)}, u32[]{:S(2)}, u32[]{:S(2)}) collective-permute-start(f32[192,128]{1,0:T(8,128)S(1)} %get-tuple-element.138.refs_0_), channel_id=1, source_target_pairs={{0,2},{2,0},{4,6},{6,4},{8,10},{10,8},{12,14},{14,12},{16,18},{18,... | collective-permute-start | bytes 294920 | tf_op jit(solution)/shard_map/ppermute | solution.py:639
  54.8 3.7 %collective-permute-start.18 = (f32[192,128]{1,0:T(8,128)S(1)}, f32[192,128]{1,0:T(8,128)S(1)}, u32[]{:S(2)}, u32[]{:S(2)}) collective-permute-start(f32[192,128]{1,0:T(8,128)S(1)} %get-tuple-element.138.refs_0_), channel_id=1, source_target_pairs={{0,1},{1,0},{2,3},{3,2},{4,5},{5,4},{6,7},{7,6},{8,9},{9,8},{10,11... | collective-permute-start | bytes 294920 | tf_op jit(solution)/shard_map/ppermute | solution.py:636
  56.9 1.6 %collective-permute-start.21 = (f32[192,128]{1,0:T(8,128)S(1)}, f32[192,128]{1,0:T(8,128)S(1)}, u32[]{:S(2)}, u32[]{:S(2)}) collective-permute-start(f32[192,128]{1,0:T(8,128)S(1)} %collective-permute-done.17.refs_3_), channel_id=1, source_target_pairs={{0,1},{1,0},{2,3},{3,2},{4,5},{5,4},{6,7},{7,6},{8,9},{9,8},{10,11... | collective-permute-start | bytes 294920 | tf_op jit(solution)/shard_map/ppermute | solution.py:636
  57.9 1.3 %collective-permute-start.20 = (f32[192,128]{1,0:T(8,128)S(1)}, f32[192,128]{1,0:T(8,128)S(1)}, u32[]{:S(2)}, u32[]{:S(2)}) collective-permute-start(f32[192,128]{1,0:T(8,128)S(1)} %collective-permute-done.16.refs_2_), channel_id=1, source_target_pairs={{0,1},{1,0},{2,3},{3,2},{4,5},{5,4},{6,7},{7,6},{8,9},{9,8},{10,11... | collective-permute-start | bytes 294920 | tf_op jit(solution)/shard_map/ppermute | solution.py:636
  58.5 1.3 %collective-permute-start.19 = (f32[192,128]{1,0:T(8,128)S(1)}, f32[192,128]{1,0:T(8,128)S(1)}, u32[]{:S(2)}, u32[]{:S(2)}) collective-permute-start(f32[192,128]{1,0:T(8,128)S(1)} %collective-permute-done.15.refs_1_), channel_id=1, source_target_pairs={{0,1},{1,0},{2,3},{3,2},{4,5},{5,4},{6,7},{7,6},{8,9},{9,8},{10,11... | collective-permute-start | bytes 294920 | tf_op jit(solution)/shard_map/ppermute | solution.py:636

commit v6 on v5

--- a/solution.py
+++ b/solution.py
@@ -63,8 +63,8 @@
     return jnp.sum(jnp.where(eye, column, 0.0), axis=0, keepdims=True)
 
 
-def onehot(mask):
-    return jnp.where(mask, 1.0, 0.0).astype(BF16)
+def onehot(left, right):
+    return jnp.where(left.astype(BF16) == right.astype(BF16), BF16(1), BF16(0))
 
 
 def edge_forward(features, weight_in, recv, send, recv_t, slope_ref, chunk):
@@ -137,8 +137,8 @@
 ):
     weights_hbm, refs = refs[:4], refs[4:]
     (target, decoder, edge_in, edge_out, node_in, node_out,
-     flat_out, recv, send, recv_t, send_t, h_out, slope, q_out, raw) = refs[:15]
-    blocks, (feats, index, halo, sems) = refs[15:19], refs[19:]
+     flat_out, recv, send, recv_t, h_out, slope, q_out, raw) = refs[:14]
+    blocks, (feats, index, halo, sems) = refs[14:18], refs[18:]
     copies = [
         pltpu.make_async_copy(source, place, sems.at[at])
         for at, (source, place) in enumerate(
@@ -188,11 +188,10 @@
     flat_out[...] = jnp.broadcast_to(flat, flat_out.shape)
     for b in range(count):
         rows = pl.ds(b * lanes, lanes)
-        recv[rows, :] = onehot(columns[:, b : b + 1] == flat_row)
-        send[rows, :] = onehot(columns[:, count + b : count + b + 1] == flat_row)
-        recv_t[:, rows] = onehot(flat == table[b : b + 1])
-        send_t[:, rows] = onehot(flat == table[count + b : count + b + 1])
-    place = onehot(flat == lax.broadcasted_iota(jnp.int32, (nodes, nodes), 1).astype(F32))
+        recv[rows, :] = onehot(columns[:, b : b + 1], flat_row)
+        send[rows, :] = onehot(columns[:, count + b : count + b + 1], flat_row)
+        recv_t[:, rows] = onehot(flat, table[b : b + 1])
+    place = onehot(flat, lax.broadcasted_iota(jnp.int32, (1, nodes), 1).astype(F32))
     copies[2].wait()
     plain = feats[...]
     raw[:nodes, :] = plain
@@ -360,7 +359,15 @@
 
 def far_kernel(chunk, names, size, *refs):
     raws, refs = unpack(names, refs)
-    edge_in, refs = refs[0], refs[1:]
+    (edge_in, flat, mine, *refs), own_send_t = refs[:-1], refs[-1]
+    edges = own_send_t.shape[1]
+    lanes = edge_in.shape[2]
+    first = own_send_t.shape[0] + edges // lanes
+    flat_column = flat[:, 0:1]
+    for b in range(edges // lanes):
+        own_send_t[:, pl.ds(b * lanes, lanes)] = onehot(
+            flat_column, mine[first + b : first + b + 1, :]
+        )
     at = 0
     for place, raw in enumerate(raws):
         if raw is None:
@@ -380,12 +387,12 @@
         across = lax.broadcasted_iota(jnp.int32, (nodes, 1), 0).astype(F32)
         for b in range(count):
             rows = pl.ds(b * width, width)
-            recv[rows, :] = onehot(columns[:, b : b + 1] == own)
-            send[rows, :] = onehot(columns[:, count + b : count + b + 1] == along)
-            recv_t[:, rows] = onehot(down == block[b : b + 1])
-            send_t[:, rows] = onehot(across == block[count + b : count + b + 1])
+            recv[rows, :] = onehot(columns[:, b : b + 1], own)
+            send[rows, :] = onehot(columns[:, count + b : count + b + 1], along)
+            recv_t[:, rows] = onehot(down, block[b : b + 1])
+            send_t[:, rows] = onehot(across, block[count + b : count + b + 1])
         features = raw[:nodes, :]
-        shared = fold(dot(onehot(down == along), side(features)))
+        shared = fold(dot(onehot(down, along), side(features)))
         shared_out[...] = shared
         to_recv = side(mm(shared, edge_in[0, :width]))
         to_send = side(mm(features, edge_in[0, width:]))
@@ -537,7 +544,7 @@
     size = halo_index.shape[2]
     n_dom, n_sub = lax.axis_size("dom"), lax.axis_size("sub")
     count = nodes * n_dom * n_sub
-    if n_dom < 3 or edge_in.shape[0] != 2 or 4 * size != nodes:
+    if n_dom < 3 or nodes > 256 or edge_in.shape[0] != 2 or 4 * size != nodes:
         raise ValueError("unsupported sizes")
     chunk = 256
     links = [moves(n_dom, n_sub, at) for at in range(4)]
@@ -563,12 +570,11 @@
     shapes = [
         ((1, nodes), F32), ((1, width), F32), *[(weight.shape, F32) for weight in weights],
         ((nodes, 128), F32),
-        ((edges, nodes), BF16), ((edges, nodes), BF16),
-        ((nodes, edges), BF16), ((nodes, edges), BF16),
+        ((edges, nodes), BF16), ((edges, nodes), BF16), ((nodes, edges), BF16),
         node_shape, edge_shape, node_shape, raw_shape, *block_shapes,
     ]
     (wanted, readout, edge_in, edge_out, node_in, node_out,
-     flat, recv, send, recv_t, send_t, h0, slope0, q0, raw, *blocks) = pl.pallas_call(
+     flat, recv, send, recv_t, h0, slope0, q0, raw, *blocks) = pl.pallas_call(
         functools.partial(first_kernel, chunk),
         out_shape=[jax.ShapeDtypeStruct(shape, dtype) for shape, dtype in shapes],
         in_specs=[pl.BlockSpec(memory_space=pltpu.HBM)] * len(sources),
@@ -598,9 +604,11 @@
         ((edges, size), BF16), ((size, edges), BF16), ((edges, nodes), BF16), ((nodes, edges), BF16),
     ]
     fars = call(
-        functools.partial(far_kernel, chunk, far_names, size), far_shapes * len(raws), *raws, edge_in
-    )
-    shared, far_slope, far_q, far_recv, far_recv_t, _, far_send_t = fars
+        functools.partial(far_kernel, chunk, far_names, size),
+        far_shapes * len(raws) + [((nodes, edges), BF16)],
+        *raws, edge_in, flat, raw,
+    )
+    shared, far_slope, far_q, far_recv, far_recv_t, _, far_send_t, send_t = fars
     (agg1, act1, pre1, seed, local1, to_recv1, to_send1, top0, pre0, pred, loss,
      *blocks) = call(
         functools.partial(back_kernel, chunk, count, names),

time: 61.2 us -> 60.9 us (level)
  no operation moved by 1% of the time
where the time goes in v6:
time: 60.9 us; the launch traced here: 60.6 us
  waiting for transfers between devices  23.3 us (38%)
  starting transfers between devices  22.2 us (36%)
  Pallas kernels  14.5 us (24%)
  between operations  0.72 us (1%)
    pallas_call x10, Pallas kernels, call(): pl.pallas_call(kernel, out_shape=shapes, in_specs=[VMEM] * len(args), out...  11.3 us
    ppermute x9, starting transfers between devices, exchange(): came[at] = lax.ppermute(blocks[at], ('dom', 'sub'), links[at])  10.6 us
    ppermute x6, waiting for transfers between devices, across(): return lax.ppermute(value, 'dom', [(at, at ^ away) for at in range(n_dom)])  8.95 us
    ppermute x6, starting transfers between devices, across(): return lax.ppermute(value, 'dom', [(at, at ^ away) for at in range(n_dom)])  7.11 us
    ppermute x2, waiting for transfers between devices, beside(): return lax.ppermute(value, ('dom', 'sub'), moves)  6.06 us
    ppermute x9, waiting for transfers between devices, exchange(): came[at] = lax.ppermute(blocks[at], ('dom', 'sub'), links[at])  5.38 us
    ppermute x2, starting transfers between devices, beside(): return lax.ppermute(value, ('dom', 'sub'), moves)  4.3 us
    pallas_call x1, Pallas kernels, per_device(): pl.pallas_call(functools.partial(first_kernel, chunk), out_shape=[jax.Sha...  3.18 us
  transfers between devices with their start and end apart: 22, of which 14 were waited for; matrix products, arithmetic and copies ran while one was open for 0% of the time, Pallas kernels for 9%

profile of v6, /device:TPU:0, one launch (start us, length us, event | category | flops | bytes accessed | tf_op | source)
XLA Modules:
  0.0 60.6 jit_solution(633477880047783095)
XLA Ops:
  0.6 3.2 %shard_map.144 = (f32[1,256]{1,0:T(1,128)S(1)}, f32[1,128]{1,0:T(1,128)S(1)}, f32[2,256,128]{2,1,0:T(8,128)S(1)}, f32[2,128,128]{2,1,0:T(8,128)S(1)}, f32[2,256,...) custom-call(f32[256,128]{1,0:T(8,128)} %feats_hbm.1, ...), custom_call_target="tpu_custom_call" | custom-call | tf_op jit(solution)/shard_map/pallas_call | solution.py:577
  4.5 5.3 %collective-permute-start.1 = (f32[64,128]{1,0:T(8,128)S(1)}, f32[64,128]{1,0:T(8,128)S(1)}, u32[]{:S(2)}, u32[]{:S(2)}) collective-permute-start(f32[64,128]{1,0:T(8,128)S(1)} %get-tuple-element.78.refs_1_), channel_id=1, source_target_pairs={{0,2},{2,0},{4,6},{6,4},{8,10},{10,8},{12,14},{14,12},{16,18},{18,... | collective-permute-start | bytes 98312 | tf_op jit(solution)/shard_map/ppermute | solution.py:557
  9.8 3.4 %collective-permute-done.1.refs_5_ = f32[64,128]{1,0:T(8,128)S(1)} collective-permute-done((f32[64,128]{1,0:T(8,128)S(1)}, f32[64,128]{1,0:T(8,128)S(1)}, u32[]{:S(2)}, u32[]{:S(2)}) %collective-permute-start.1) | collective-permute-done | bytes 32800 | tf_op jit(solution)/shard_map/ppermute | solution.py:557
  13.2 1.9 %shard_map.145 = (f32[256,128]{1,0:T(8,128)S(1)}, f32[256,128]{1,0:T(8,128)S(1)}, f32[256,128]{1,0:T(8,128)S(1)}, f32[256,128]{1,0:T(8,128)S(1)}, f32[1280,128]{...) custom-call(f32[64,128]{1,0:T(8,128)S(1)} %get-tuple-element.77.refs, ...), custom_call_target="tpu_custom_call" | custom-call | tf_op jit(solution)/shard_map/pallas_call | solution.py:507
  15.2 2.6 %collective-permute-start.4 = (f32[136,128]{1,0:T(8,128)S(1)}, f32[136,128]{1,0:T(8,128)S(1)}, u32[]{:S(2)}, u32[]{:S(2)}) collective-permute-start(f32[136,128]{1,0:T(8,128)S(1)} %get-tuple-element.93.refs_1_), channel_id=1, source_target_pairs={{0,2},{2,0},{4,6},{6,4},{8,10},{10,8},{12,14},{14,12},{16,18},{18,... | collective-permute-start | bytes 208904 | tf_op jit(solution)/shard_map/ppermute | solution.py:557
  17.7 2.1 %shard_map.146 = (f32[64,128]{1,0:T(8,128)S(1)}, f32[1280,128]{1,0:T(8,128)S(1)}, f32[64,128]{1,0:T(8,128)S(1)}, bf16[1280,64]{1,0:T(8,128)(2,1)S(1)}, bf16[64,1...) custom-call(f32[280,128]{1,0:T(8,128)S(1)} %collective-permute-done., ...), custom_call_target="tpu_custom_call" | custom-call | tf_op jit(solution)/shard_map/pallas_call | solution.py:507
  19.9 1.5 %collective-permute-done.4.refs_5_ = f32[136,128]{1,0:T(8,128)S(1)} collective-permute-done((f32[136,128]{1,0:T(8,128)S(1)}, f32[136,128]{1,0:T(8,128)S(1)}, u32[]{:S(2)}, u32[]{:S(2)}) %collective-permute-start.4) | collective-permute-done | bytes 69664 | tf_op jit(solution)/shard_map/ppermute | solution.py:557
  21.4 2.6 %shard_map.147 = (f32[256,128]{1,0:T(8,128)S(1)}, f32[256,128]{1,0:T(8,128)S(1)}, f32[256,128]{1,0:T(8,128)S(1)}, f32[256,128]{1,0:T(8,128)S(1)}, f32[256,128]{1...) custom-call(f32[136,128]{1,0:T(8,128)S(1)} %get-tuple-element.92.ref, ...), custom_call_target="tpu_custom_call" | custom-call | tf_op jit(solution)/shard_map/pallas_call | solution.py:507
  24.0 1.9 %collective-permute-start.7 = (f32[64,128]{1,0:T(8,128)S(1)}, f32[64,128]{1,0:T(8,128)S(1)}, u32[]{:S(2)}, u32[]{:S(2)}) collective-permute-start(f32[64,128]{1,0:T(8,128)S(1)} %get-tuple-element.104.refs_1_), channel_id=1, source_target_pairs={{0,2},{2,0},{4,6},{6,4},{8,10},{10,8},{12,14},{14,12},{16,18},{18,... | collective-permute-start | bytes 98312 | tf_op jit(solution)/shard_map/ppermute | solution.py:557
  26.0 1.6 %shard_map.148 = (f32[768,128]{1,0:T(8,128)S(1)}, f32[384,128]{1,0:T(8,128)S(1)}, f32[384,128]{1,0:T(8,128)S(1)}, f32[8,128]{1,0:T(8,128)S(1)}) custom-call(f32[256,128]{1,0:T(8,128)S(1)} %get-tuple-element.81.refs_7_.h0.refs_6_, f32[256,128]{1,0:T(8,128)S(1)} %get-tuple-element.109.agg0, f32[256,128]{1,0:T(8,128)S(1)} %get-tuple-element.110.act0, ...), custom_call_target="tpu_custom_call" | custom-call | tf_op jit(solution)/shard_map/pallas_call | solution.py:507
  28.0 1.9 %shard_map.149 = (f32[776,128]{1,0:T(8,128)S(1)}, f32[776,128]{1,0:T(8,128)S(1)}) custom-call(f32[64,128]{1,0:T(8,128)S(1)} %get-tuple-element.103.block.refs_0_, f32[64,128]{1,0:T(8,128)S(1)} %get-tuple-element.104.refs_1_, f32[64,128]{1,0:T(8,128)S(1)} %get-tuple-element.105.refs_2_, f32[64,128]{1,0:T(8,128)S(1)} %get-tuple-element.106.refs_3_, ...), custom_call_target="tpu_custom_call" | custom-call | tf_op jit(solution)/shard_map/pallas_call | solution.py:507
  30.1 1.6 %collective-permute-done.9.other = f32[776,128]{1,0:T(8,128)S(1)} collective-permute-done((f32[776,128]{1,0:T(8,128)S(1)}, f32[776,128]{1,0:T(8,128)S(1)}, u32[]{:S(2)}, u32[]{:S(2)}) %collective-permute-start.9) | collective-permute-done | bytes 397344 | tf_op jit(solution)/shard_map/ppermute | solution.py:644
  31.7 1.9 %collective-permute-start.10 = (f32[200,128]{1,0:T(8,128)S(1)}, f32[200,128]{1,0:T(8,128)S(1)}, u32[]{:S(2)}, u32[]{:S(2)}) collective-permute-start(f32[200,128]{1,0:T(8,128)S(1)} %get-tuple-element.135), channel_id=1, source_target_pairs={{0,2},{2,0},{4,6},{6,4},{8,10},{10,8},{12,14},{14,12},{16,18},{18,... | collective-permute-start | bytes 307208 | tf_op jit(solution)/shard_map/ppermute | solution.py:647
  33.7 1.3 %collective-permute-start.11 = (f32[200,128]{1,0:T(8,128)S(1)}, f32[200,128]{1,0:T(8,128)S(1)}, u32[]{:S(2)}, u32[]{:S(2)}) collective-permute-start(f32[200,128]{1,0:T(8,128)S(1)} %get-tuple-element.136), channel_id=1, source_target_pairs={{0,4},{2,6},{4,0},{6,2},{8,12},{10,14},{12,8},{14,10},{16,20},{18,... | collective-permute-start | bytes 307208 | tf_op jit(solution)/shard_map/ppermute | solution.py:647
  35.3 1.7 %collective-permute-done.10.b = f32[200,128]{1,0:T(8,128)S(1)} collective-permute-done((f32[200,128]{1,0:T(8,128)S(1)}, f32[200,128]{1,0:T(8,128)S(1)}, u32[]{:S(2)}, u32[]{:S(2)}) %collective-permute-start.10) | collective-permute-done | bytes 102432 | tf_op jit(solution)/shard_map/ppermute | solution.py:647
  36.9 2.5 %collective-permute-done.11.c = f32[200,128]{1,0:T(8,128)S(1)} collective-permute-done((f32[200,128]{1,0:T(8,128)S(1)}, f32[200,128]{1,0:T(8,128)S(1)}, u32[]{:S(2)}, u32[]{:S(2)}) %collective-permute-start.11) | collective-permute-done | bytes 102432 | tf_op jit(solution)/shard_map/ppermute | solution.py:647
  39.4 1.1 %collective-permute-done.12.d = f32[200,128]{1,0:T(8,128)S(1)} collective-permute-done((f32[200,128]{1,0:T(8,128)S(1)}, f32[200,128]{1,0:T(8,128)S(1)}, u32[]{:S(2)}, u32[]{:S(2)}) %collective-permute-start.12) | collective-permute-done | bytes 102432 | tf_op jit(solution)/shard_map/ppermute | solution.py:647
  40.6 1.6 %collective-permute-start.13 = (f32[200,128]{1,0:T(8,128)S(1)}, f32[200,128]{1,0:T(8,128)S(1)}, u32[]{:S(2)}, u32[]{:S(2)}) collective-permute-start(f32[200,128]{1,0:T(8,128)S(1)} %shard_map.151.a), channel_id=1, source_target_pairs={{0,8},{1,17},{2,10},{3,19},{4,12},{5,21},{6,14},{7,23},{8,0},{9,25... | collective-permute-start | bytes 307208 | tf_op jit(solution)/shard_map/ppermute | solution.py:655
  42.2 3.1 %collective-permute-done.13.b = f32[200,128]{1,0:T(8,128)S(1)} collective-permute-done((f32[200,128]{1,0:T(8,128)S(1)}, f32[200,128]{1,0:T(8,128)S(1)}, u32[]{:S(2)}, u32[]{:S(2)}) %collective-permute-start.13) | collective-permute-done | bytes 102432 | tf_op jit(solution)/shard_map/ppermute | solution.py:655
  45.3 2.7 %collective-permute-start.14 = (f32[200,128]{1,0:T(8,128)S(1)}, f32[200,128]{1,0:T(8,128)S(1)}, u32[]{:S(2)}, u32[]{:S(2)}) collective-permute-start(f32[200,128]{1,0:T(8,128)S(1)} %shard_map.152.a), channel_id=1, source_target_pairs={{0,16},{1,9},{2,18},{3,11},{4,20},{5,13},{6,22},{7,15},{8,24},{9,1... | collective-permute-start | bytes 307208 | tf_op jit(solution)/shard_map/ppermute | solution.py:655
  48.0 3.0 %collective-permute-done.14.b = f32[200,128]{1,0:T(8,128)S(1)} collective-permute-done((f32[200,128]{1,0:T(8,128)S(1)}, f32[200,128]{1,0:T(8,128)S(1)}, u32[]{:S(2)}, u32[]{:S(2)}) %collective-permute-start.14) | collective-permute-done | bytes 102432 | tf_op jit(solution)/shard_map/ppermute | solution.py:655
  51.0 1.5 %collective-permute-start.17 = (f32[192,128]{1,0:T(8,128)S(1)}, f32[192,128]{1,0:T(8,128)S(1)}, u32[]{:S(2)}, u32[]{:S(2)}) collective-permute-start(f32[192,128]{1,0:T(8,128)S(1)} %get-tuple-element.138.refs_0_), channel_id=1, source_target_pairs={{0,6},{2,4},{4,2},{6,0},{8,14},{10,12},{12,10},{14,8},{16,22},{18,... | collective-permute-start | bytes 294920 | tf_op jit(solution)/shard_map/ppermute | solution.py:647
  54.5 2.1 %collective-permute-done.17.refs_3_ = f32[192,128]{1,0:T(8,128)S(1)} collective-permute-done((f32[192,128]{1,0:T(8,128)S(1)}, f32[192,128]{1,0:T(8,128)S(1)}, u32[]{:S(2)}, u32[]{:S(2)}) %collective-permute-start.17) | collective-permute-done | bytes 98336 | tf_op jit(solution)/shard_map/ppermute | solution.py:647
  59.5 1.1 %shard_map.154 = (f32[1,128]{1,0:T(1,128)}, f32[2,256,128]{2,1,0:T(8,128)}, f32[2,128,128]{2,1,0:T(8,128)}, f32[2,256,128]{2,1,0:T(8,128)}, f32[2,128,128]{2,1,0:T(8,128)}, /*index=5*/f32[1,128]{1,0:T(1,128)}) custom-call(f32[192,128]{1,0:T(8,128)S(1)} %get-tuple-element.138.refs_0_, f32[192,128]{1,0:T(8,128)S(1)} %collective-permute-done.15.refs_1_, ...), custom_call_target="tpu_custom_call" | custom-call | tf_op jit(solution)/shard_map/pallas_call | solution.py:507
  (31 shorter events, 6.7 us)
Async XLA Ops:
  3.8 13.9 %collective-permute-start.6 = (f32[280,128]{1,0:T(8,128)S(1)}, f32[280,128]{1,0:T(8,128)S(1)}, u32[]{:S(2)}, u32[]{:S(2)}) collective-permute-start(f32[280,128]{1,0:T(8,128)S(1)} %get-tuple-element.99.refs_3_), channel_id=1, source_target_pairs={{2,4},{4,2},{6,8},{8,6},{10,12},{12,10},{14,16},{16,14},{18,20},{2... | collective-permute-start | bytes 430088 | tf_op jit(solution)/shard_map/ppermute | solution.py:557
  4.4 5.4 %collective-permute-start = (f32[64,128]{1,0:T(8,128)S(1)}, f32[64,128]{1,0:T(8,128)S(1)}, u32[]{:S(2)}, u32[]{:S(2)}) collective-permute-start(f32[64,128]{1,0:T(8,128)S(1)} %get-tuple-element.77.refs_0_), channel_id=1, source_target_pairs={{2,4},{4,2},{6,8},{8,6},{10,12},{12,10},{14,16},{16,14},{18,20},{2... | collective-permute-start | bytes 98312 | tf_op jit(solution)/shard_map/ppermute | solution.py:557
  4.5 8.8 %collective-permute-start.1 = (f32[64,128]{1,0:T(8,128)S(1)}, f32[64,128]{1,0:T(8,128)S(1)}, u32[]{:S(2)}, u32[]{:S(2)}) collective-permute-start(f32[64,128]{1,0:T(8,128)S(1)} %get-tuple-element.78.refs_1_), channel_id=1, source_target_pairs={{0,2},{2,0},{4,6},{6,4},{8,10},{10,8},{12,14},{14,12},{16,18},{18,... | collective-permute-start | bytes 98312 | tf_op jit(solution)/shard_map/ppermute | solution.py:557
  9.8 3.4 %collective-permute-start.2 = (f32[64,128]{1,0:T(8,128)S(1)}, f32[64,128]{1,0:T(8,128)S(1)}, u32[]{:S(2)}, u32[]{:S(2)}) collective-permute-start(f32[64,128]{1,0:T(8,128)S(1)} %get-tuple-element.79.refs_2_), channel_id=1, source_target_pairs={{0,1},{1,0},{2,3},{3,2},{4,5},{5,4},{6,7},{7,6},{8,9},{9,8},{10,11... | collective-permute-start | bytes 98312 | tf_op jit(solution)/shard_map/ppermute | solution.py:557
  15.1 4.8 %collective-permute-start.3 = (f32[136,128]{1,0:T(8,128)S(1)}, f32[136,128]{1,0:T(8,128)S(1)}, u32[]{:S(2)}, u32[]{:S(2)}) collective-permute-start(f32[136,128]{1,0:T(8,128)S(1)} %get-tuple-element.92.refs_0_), channel_id=1, source_target_pairs={{2,4},{4,2},{6,8},{8,6},{10,12},{12,10},{14,16},{16,14},{18,20},{2... | collective-permute-start | bytes 208904 | tf_op jit(solution)/shard_map/ppermute | solution.py:557
  15.2 6.2 %collective-permute-start.4 = (f32[136,128]{1,0:T(8,128)S(1)}, f32[136,128]{1,0:T(8,128)S(1)}, u32[]{:S(2)}, u32[]{:S(2)}) collective-permute-start(f32[136,128]{1,0:T(8,128)S(1)} %get-tuple-element.93.refs_1_), channel_id=1, source_target_pairs={{0,2},{2,0},{4,6},{6,4},{8,10},{10,8},{12,14},{14,12},{16,18},{18,... | collective-permute-start | bytes 208904 | tf_op jit(solution)/shard_map/ppermute | solution.py:557
  17.7 3.7 %collective-permute-start.5 = (f32[136,128]{1,0:T(8,128)S(1)}, f32[136,128]{1,0:T(8,128)S(1)}, u32[]{:S(2)}, u32[]{:S(2)}) collective-permute-start(f32[136,128]{1,0:T(8,128)S(1)} %get-tuple-element.94.refs_2_), channel_id=1, source_target_pairs={{0,1},{1,0},{2,3},{3,2},{4,5},{5,4},{6,7},{7,6},{8,9},{9,8},{10,11... | collective-permute-start | bytes 208904 | tf_op jit(solution)/shard_map/ppermute | solution.py:557
  24.0 4.0 %collective-permute-start.7 = (f32[64,128]{1,0:T(8,128)S(1)}, f32[64,128]{1,0:T(8,128)S(1)}, u32[]{:S(2)}, u32[]{:S(2)}) collective-permute-start(f32[64,128]{1,0:T(8,128)S(1)} %get-tuple-element.104.refs_1_), channel_id=1, source_target_pairs={{0,2},{2,0},{4,6},{6,4},{8,10},{10,8},{12,14},{14,12},{16,18},{18,... | collective-permute-start | bytes 98312 | tf_op jit(solution)/shard_map/ppermute | solution.py:557
  26.0 2.0 %collective-permute-start.8 = (f32[64,128]{1,0:T(8,128)S(1)}, f32[64,128]{1,0:T(8,128)S(1)}, u32[]{:S(2)}, u32[]{:S(2)}) collective-permute-start(f32[64,128]{1,0:T(8,128)S(1)} %get-tuple-element.105.refs_2_), channel_id=1, source_target_pairs={{0,1},{1,0},{2,3},{3,2},{4,5},{5,4},{6,7},{7,6},{8,9},{9,8},{10,11... | collective-permute-start | bytes 98312 | tf_op jit(solution)/shard_map/ppermute | solution.py:557
  29.9 1.8 %collective-permute-start.9 = (f32[776,128]{1,0:T(8,128)S(1)}, f32[776,128]{1,0:T(8,128)S(1)}, u32[]{:S(2)}, u32[]{:S(2)}) collective-permute-start(f32[776,128]{1,0:T(8,128)S(1)} %get-tuple-element.133), channel_id=1, source_target_pairs={{0,1},{1,0},{2,3},{3,2},{4,5},{5,4},{6,7},{7,6},{8,9},{9,8},{10,11... | collective-permute-start | bytes 1191944 | tf_op jit(solution)/shard_map/ppermute | solution.py:644
  31.7 5.2 %collective-permute-start.10 = (f32[200,128]{1,0:T(8,128)S(1)}, f32[200,128]{1,0:T(8,128)S(1)}, u32[]{:S(2)}, u32[]{:S(2)}) collective-permute-start(f32[200,128]{1,0:T(8,128)S(1)} %get-tuple-element.135), channel_id=1, source_target_pairs={{0,2},{2,0},{4,6},{6,4},{8,10},{10,8},{12,14},{14,12},{16,18},{18,... | collective-permute-start | bytes 307208 | tf_op jit(solution)/shard_map/ppermute | solution.py:647
  33.7 5.8 %collective-permute-start.11 = (f32[200,128]{1,0:T(8,128)S(1)}, f32[200,128]{1,0:T(8,128)S(1)}, u32[]{:S(2)}, u32[]{:S(2)}) collective-permute-start(f32[200,128]{1,0:T(8,128)S(1)} %get-tuple-element.136), channel_id=1, source_target_pairs={{0,4},{2,6},{4,0},{6,2},{8,12},{10,14},{12,8},{14,10},{16,20},{18,... | collective-permute-start | bytes 307208 | tf_op jit(solution)/shard_map/ppermute | solution.py:647
  35.0 5.6 %collective-permute-start.12 = (f32[200,128]{1,0:T(8,128)S(1)}, f32[200,128]{1,0:T(8,128)S(1)}, u32[]{:S(2)}, u32[]{:S(2)}) collective-permute-start(f32[200,128]{1,0:T(8,128)S(1)} %get-tuple-element.137), channel_id=1, source_target_pairs={{0,6},{2,4},{4,2},{6,0},{8,14},{10,12},{12,10},{14,8},{16,22},{18,... | collective-permute-start | bytes 307208 | tf_op jit(solution)/shard_map/ppermute | solution.py:647
  40.6 4.7 %collective-permute-start.13 = (f32[200,128]{1,0:T(8,128)S(1)}, f32[200,128]{1,0:T(8,128)S(1)}, u32[]{:S(2)}, u32[]{:S(2)}) collective-permute-start(f32[200,128]{1,0:T(8,128)S(1)} %shard_map.151.a), channel_id=1, source_target_pairs={{0,8},{1,17},{2,10},{3,19},{4,12},{5,21},{6,14},{7,23},{8,0},{9,25... | collective-permute-start | bytes 307208 | tf_op jit(solution)/shard_map/ppermute | solution.py:655
  45.3 5.6 %collective-permute-start.14 = (f32[200,128]{1,0:T(8,128)S(1)}, f32[200,128]{1,0:T(8,128)S(1)}, u32[]{:S(2)}, u32[]{:S(2)}) collective-permute-start(f32[200,128]{1,0:T(8,128)S(1)} %shard_map.152.a), channel_id=1, source_target_pairs={{0,16},{1,9},{2,18},{3,11},{4,20},{5,13},{6,22},{7,15},{8,24},{9,1... | collective-permute-start | bytes 307208 | tf_op jit(solution)/shard_map/ppermute | solution.py:655
  51.0 5.6 %collective-permute-start.17 = (f32[192,128]{1,0:T(8,128)S(1)}, f32[192,128]{1,0:T(8,128)S(1)}, u32[]{:S(2)}, u32[]{:S(2)}) collective-permute-start(f32[192,128]{1,0:T(8,128)S(1)} %get-tuple-element.138.refs_0_), channel_id=1, source_target_pairs={{0,6},{2,4},{4,2},{6,0},{8,14},{10,12},{12,10},{14,8},{16,22},{18,... | collective-permute-start | bytes 294920 | tf_op jit(solution)/shard_map/ppermute | solution.py:647
  52.5 5.1 %collective-permute-start.16 = (f32[192,128]{1,0:T(8,128)S(1)}, f32[192,128]{1,0:T(8,128)S(1)}, u32[]{:S(2)}, u32[]{:S(2)}) collective-permute-start(f32[192,128]{1,0:T(8,128)S(1)} %get-tuple-element.138.refs_0_), channel_id=1, source_target_pairs={{0,4},{2,6},{4,0},{6,2},{8,12},{10,14},{12,8},{14,10},{16,20},{18,... | collective-permute-start | bytes 294920 | tf_op jit(solution)/shard_map/ppermute | solution.py:647
  53.6 4.6 %collective-permute-start.15 = (f32[192,128]{1,0:T(8,128)S(1)}, f32[192,128]{1,0:T(8,128)S(1)}, u32[]{:S(2)}, u32[]{:S(2)}) collective-permute-start(f32[192,128]{1,0:T(8,128)S(1)} %get-tuple-element.138.refs_0_), channel_id=1, source_target_pairs={{0,2},{2,0},{4,6},{6,4},{8,10},{10,8},{12,14},{14,12},{16,18},{18,... | collective-permute-start | bytes 294920 | tf_op jit(solution)/shard_map/ppermute | solution.py:647
  54.5 3.7 %collective-permute-start.18 = (f32[192,128]{1,0:T(8,128)S(1)}, f32[192,128]{1,0:T(8,128)S(1)}, u32[]{:S(2)}, u32[]{:S(2)}) collective-permute-start(f32[192,128]{1,0:T(8,128)S(1)} %get-tuple-element.138.refs_0_), channel_id=1, source_target_pairs={{0,1},{1,0},{2,3},{3,2},{4,5},{5,4},{6,7},{7,6},{8,9},{9,8},{10,11... | collective-permute-start | bytes 294920 | tf_op jit(solution)/shard_map/ppermute | solution.py:644
  56.6 1.6 %collective-permute-start.21 = (f32[192,128]{1,0:T(8,128)S(1)}, f32[192,128]{1,0:T(8,128)S(1)}, u32[]{:S(2)}, u32[]{:S(2)}) collective-permute-start(f32[192,128]{1,0:T(8,128)S(1)} %collective-permute-done.17.refs_3_), channel_id=1, source_target_pairs={{0,1},{1,0},{2,3},{3,2},{4,5},{5,4},{6,7},{7,6},{8,9},{9,8},{10,11... | collective-permute-start | bytes 294920 | tf_op jit(solution)/shard_map/ppermute | solution.py:644
  57.6 1.3 %collective-permute-start.20 = (f32[192,128]{1,0:T(8,128)S(1)}, f32[192,128]{1,0:T(8,128)S(1)}, u32[]{:S(2)}, u32[]{:S(2)}) collective-permute-start(f32[192,128]{1,0:T(8,128)S(1)} %collective-permute-done.16.refs_2_), channel_id=1, source_target_pairs={{0,1},{1,0},{2,3},{3,2},{4,5},{5,4},{6,7},{7,6},{8,9},{9,8},{10,11... | collective-permute-start | bytes 294920 | tf_op jit(solution)/shard_map/ppermute | solution.py:644
  58.2 1.3 %collective-permute-start.19 = (f32[192,128]{1,0:T(8,128)S(1)}, f32[192,128]{1,0:T(8,128)S(1)}, u32[]{:S(2)}, u32[]{:S(2)}) collective-permute-start(f32[192,128]{1,0:T(8,128)S(1)} %collective-permute-done.15.refs_1_), channel_id=1, source_target_pairs={{0,1},{1,0},{2,3},{3,2},{4,5},{5,4},{6,7},{7,6},{8,9},{9,8},{10,11... | collective-permute-start | bytes 294920 | tf_op jit(solution)/shard_map/ppermute | solution.py:644

commit v7 on v6

--- a/solution.py
+++ b/solution.py
@@ -326,7 +326,7 @@
 def grads_kernel(
     h0, agg0, act0, pre0, top0, h1, agg1, act1, pre1, seed, q1, local1, to_recv1, to_send1,
     decoder, node_out, loss, block, raw, shared, far_slope, far_q, far_recv, far_recv_t, far_send_t,
-    edge_out, high, low, far, tail, *, chunk
+    edge_out, high, low, far, tail, early, *, chunk
 ):
     width = h0.shape[1]
     rows = seed[...]
@@ -354,7 +354,20 @@
     far[2 * width :, :] = tmm(far_q[...], far_grad)
     line = jnp.sum(rows * h1[...], axis=0, keepdims=True)
     line = line + row_product(jnp.sum(rows * act, axis=0, keepdims=True), node_out[1])
-    tail[...] = jnp.concatenate([line, loss[...], jnp.zeros((EXTRA - 2, width), F32)], axis=0)
+    end = jnp.concatenate([line, loss[...], jnp.zeros((EXTRA - 2, width), F32)], axis=0)
+    tail[...] = end
+    rows_high = high.shape[0]
+    early[rows_high:, :] = end
+    first = lax.axis_index("sub") == 0
+
+    @pl.when(first)
+    def _():
+        early[: low.shape[0], :] = low[...]
+        early[low.shape[0] : rows_high, :] = jnp.zeros(low.shape, F32)
+
+    @pl.when(jnp.logical_not(first))
+    def _():
+        early[:rows_high, :] = high[...]
 
 
 def far_kernel(chunk, names, size, *refs):
@@ -407,45 +420,38 @@
         q_out[...] = fold(total)
 
 
-def put_rows(ref, at, value):
-    ref[at : at + value.shape[0], :] = value
-    return at + value.shape[0]
-
-
 def end_kernel(chunk, names, *refs):
     own, refs = refs[:4], refs[4:]
     came, refs = unpack(names, refs)
-    h, q, recv, recv_t, send_t, slope, edge_out, node_low, high, far, tail, mine, other = refs
+    h, q, recv, recv_t, send_t, slope, edge_out, far, out = refs
     local_grad = take_sum(own, came)
     to_recv, to_send = edge_backward(local_grad, edge_out[0], recv, recv_t, send_t, slope, chunk)
     width = h.shape[1]
-    low = [
-        node_low[...],
-        tmm(h[...], to_recv) + far[0:width, :],
-        tmm(h[...], to_send) + far[width : 2 * width, :],
-        tmm(q[...], local_grad) + far[2 * width :, :],
-        tail[...],
-    ]
-
-    def write(ref_high, ref_low):
-        at = 0
-        for value in low:
-            at = put_rows(ref_low, at, value)
-        put_rows(ref_high, put_rows(ref_high, 0, high[...]), tail[...])
-
-    first = lax.axis_index("sub") == 0
-    pl.when(first)(lambda: write(mine, other))
-    pl.when(jnp.logical_not(first))(lambda: write(other, mine))
-
-
-def quarters_kernel(mine, other, *outs):
+    out[0:width, :] = tmm(h[...], to_recv) + far[0:width, :]
+    out[width : 2 * width, :] = tmm(h[...], to_send) + far[width : 2 * width, :]
+    out[2 * width :, :] = tmm(q[...], local_grad) + far[2 * width :, :]
+
+
+def quarters_kernel(high, node_low, edge_low, tail, early, late, *refs):
+    outs, half = refs[:-1], refs[-1]
     per = outs[0].shape[0] - EXTRA
     own = lax.rem(lax.axis_index("dom"), 4)
-    tail = mine[4 * per :, :] + other[4 * per :, :]
+    first = lax.axis_index("sub") == 0
+
+    @pl.when(first)
+    def _():
+        half[...] = high[...] + early[: 4 * per, :]
+
+    @pl.when(jnp.logical_not(first))
+    def _():
+        half[: 2 * per, :] = node_low[...] + early[: 2 * per, :]
+        half[2 * per :, :] = edge_low[...] + late[...]
+
+    end = tail[...] + early[4 * per :, :]
     for away, out in enumerate(outs):
         rows = pl.ds(pl.multiple_of(jnp.bitwise_xor(own, away) * per, 8), per)
-        out[:per, :] = mine[rows, :] + other[rows, :]
-        out[per:, :] = tail
+        out[:per, :] = half[rows, :]
+        out[per:, :] = end
 
 
 def four_kernel(a, b, c, d, out):
@@ -618,27 +624,25 @@
         edge_in, edge_out, node_in, node_out, far_q,
     )
     came = exchange(blocks, 4, 1)
-    high, node_low, far, tail = call(
+    high, node_low, far, tail, early = call(
         functools.partial(grads_kernel, chunk=chunk),
         [((6 * width, width), F32), ((3 * width, width), F32), ((3 * width, width), F32),
-         ((EXTRA, width), F32)],
+         ((EXTRA, width), F32), ((6 * width + EXTRA, width), F32)],
         h0, agg0, act0, pre0, top0, h1, agg1, act1, pre1, seed, q1, local1, to_recv1, to_send1,
         readout, node_out, loss, blocks[0], *raws, shared, far_slope, far_q, far_recv, far_recv_t,
         far_send_t, edge_out,
     )
     rows = 6 * width
     groups = n_dom // 4
-    half = ((rows + EXTRA, width), F32)
-    end_grads = call(
+    (edge_low,) = call(
         functools.partial(end_kernel, chunk, (0,) + names[1:]),
-        [half, half],
-        *blocks, *came, h0, q0, recv, recv_t, send_t, slope0, edge_out, node_low, high, far, tail,
+        [((3 * width, width), F32)],
+        *blocks, *came, h0, q0, recv, recv_t, send_t, slope0, edge_out, far,
     )
     if n_sub != 2 or n_dom % 4 or groups & (groups - 1) or rows % 32:
-        return slow_tail(count, *end_grads, pred)
+        return slow_tail(count, [node_low, edge_low, high, tail], pred)
     per = rows // 4
     quarter = ((per + EXTRA, width), F32)
-    mine, other = end_grads
 
     def swap(value):
         return lax.ppermute(value, "sub", pairs(n_sub, 0)[0])
@@ -654,7 +658,14 @@
         ]
         return lax.ppermute(value, ("dom", "sub"), moves)
 
-    parts = call(quarters_kernel, [quarter] * 4, mine, swap(other))
+    parts = pl.pallas_call(
+        quarters_kernel,
+        out_shape=[jax.ShapeDtypeStruct(*quarter)] * 4,
+        in_specs=[VMEM] * 6,
+        out_specs=[VMEM] * 4,
+        scratch_shapes=[pltpu.VMEM((rows, width), F32)],
+        compiler_params=pltpu.CompilerParams(vmem_limit_bytes=16 * 2**20),
+    )(high, node_low, edge_low, tail, swap(early), swap(edge_low))
     came = [across(parts[away], away) for away in (3, 2, 1)]
     (total,) = call(four_kernel, [quarter], parts[0], came[2], came[1], came[0])
     aways = [4 << at for at in range(groups.bit_length() - 1)]
@@ -683,13 +694,10 @@
     )
 
 
-def slow_tail(count, mine, other, pred):
-    first = lax.axis_index("sub") == 0
-    width = mine.shape[1]
-    rows = mine.shape[0] - EXTRA
-    high = jnp.where(first, mine, other)
-    low = jnp.where(first, other, mine)
-    total = lax.psum(jnp.concatenate([low[:rows], high], axis=0), ("dom", "sub"))
+def slow_tail(count, parts, pred):
+    total = lax.psum(jnp.concatenate(parts, axis=0), ("dom", "sub"))
+    width = total.shape[1]
+    rows = (total.shape[0] - EXTRA) // 2
     body = total[: 2 * rows + 1]
     params = (2 * rows + 1) * width
     scale = 1.0 / jnp.sqrt(jnp.sum(body * body) / params + 1e-06)

time: 60.9 us -> 62.3 us (1.023)
  waiting for transfers between devices: 23.3 us -> 24.6 us
    ppermute x9, waiting for transfers between devices: 5.38 us -> 6.86 us  [exchange(): came[at] = lax.ppermute(blocks[at], ('dom', 'sub'), links[at])]
    ppermute x5 -> x6, waiting for transfers between devices: 2.88 us -> 2.72 us  [swap(): return lax.ppermute(value, 'sub', pairs(n_sub, 0)[0])]
    pallas_call x10 -> x9, Pallas kernels: 11.3 us -> 11.2 us  [call(): pl.pallas_call(kernel, out_shape=shapes, in_specs=[VMEM] * len(args), out...]
  transfers between devices with their start and end apart: 22 -> 23, of which waited for: 14 -> 14; matrix products, arithmetic and copies ran while one was open for 0% -> 0% of each run, Pallas kernels for 9% -> 9%
where the time goes in v7:
time: 62.3 us; the launch traced here: 62.1 us
  waiting for transfers between devices  24.6 us (39%)
  starting transfers between devices  22.3 us (36%)
  Pallas kernels  14.5 us (23%)
  between operations  0.74 us (1%)
    pallas_call x9, Pallas kernels, call(): pl.pallas_call(kernel, out_shape=shapes, in_specs=[VMEM] * len(args), out...  11.2 us
    ppermute x9, starting transfers between devices, exchange(): came[at] = lax.ppermute(blocks[at], ('dom', 'sub'), links[at])  10.7 us
    ppermute x6, waiting for transfers between devices, across(): return lax.ppermute(value, 'dom', [(at, at ^ away) for at in range(n_dom)])  8.95 us
    ppermute x6, starting transfers between devices, across(): return lax.ppermute(value, 'dom', [(at, at ^ away) for at in range(n_dom)])  7.11 us
    ppermute x9, waiting for transfers between devices, exchange(): came[at] = lax.ppermute(blocks[at], ('dom', 'sub'), links[at])  6.86 us
    ppermute x2, waiting for transfers between devices, beside(): return lax.ppermute(value, ('dom', 'sub'), moves)  6.04 us
    ppermute x2, starting transfers between devices, beside(): return lax.ppermute(value, ('dom', 'sub'), moves)  4.32 us
    pallas_call x1, Pallas kernels, per_device(): pl.pallas_call(functools.partial(first_kernel, chunk), out_shape=[jax.Sha...  3.18 us
  transfers between devices with their start and end apart: 23, of which 14 were waited for; matrix products, arithmetic and copies ran while one was open for 0% of the time, Pallas kernels for 9%

profile of v7, /device:TPU:0, one launch (start us, length us, event | category | flops | bytes accessed | tf_op | source)
XLA Modules:
  0.0 62.1 jit_solution(5727638194574582103)
XLA Ops:
  0.6 3.2 %shard_map.144 = (f32[1,256]{1,0:T(1,128)S(1)}, f32[1,128]{1,0:T(1,128)S(1)}, f32[2,256,128]{2,1,0:T(8,128)S(1)}, f32[2,128,128]{2,1,0:T(8,128)S(1)}, f32[2,256,...) custom-call(f32[256,128]{1,0:T(8,128)} %feats_hbm.1, ...), custom_call_target="tpu_custom_call" | custom-call | tf_op jit(solution)/shard_map/pallas_call | solution.py:583
  4.5 5.3 %collective-permute-start.1 = (f32[64,128]{1,0:T(8,128)S(1)}, f32[64,128]{1,0:T(8,128)S(1)}, u32[]{:S(2)}, u32[]{:S(2)}) collective-permute-start(f32[64,128]{1,0:T(8,128)S(1)} %get-tuple-element.78.refs_1_), channel_id=1, source_target_pairs={{0,2},{2,0},{4,6},{6,4},{8,10},{10,8},{12,14},{14,12},{16,18},{18,... | collective-permute-start | bytes 98312 | tf_op jit(solution)/shard_map/ppermute | solution.py:563
  9.8 3.4 %collective-permute-done.1.refs_5_ = f32[64,128]{1,0:T(8,128)S(1)} collective-permute-done((f32[64,128]{1,0:T(8,128)S(1)}, f32[64,128]{1,0:T(8,128)S(1)}, u32[]{:S(2)}, u32[]{:S(2)}) %collective-permute-start.1) | collective-permute-done | bytes 32800 | tf_op jit(solution)/shard_map/ppermute | solution.py:563
  13.2 1.9 %shard_map.145 = (f32[256,128]{1,0:T(8,128)S(1)}, f32[256,128]{1,0:T(8,128)S(1)}, f32[256,128]{1,0:T(8,128)S(1)}, f32[256,128]{1,0:T(8,128)S(1)}, f32[1280,128]{...) custom-call(f32[64,128]{1,0:T(8,128)S(1)} %get-tuple-element.77.refs, ...), custom_call_target="tpu_custom_call" | custom-call | tf_op jit(solution)/shard_map/pallas_call | solution.py:513
  15.2 2.6 %collective-permute-start.4 = (f32[136,128]{1,0:T(8,128)S(1)}, f32[136,128]{1,0:T(8,128)S(1)}, u32[]{:S(2)}, u32[]{:S(2)}) collective-permute-start(f32[136,128]{1,0:T(8,128)S(1)} %get-tuple-element.94.refs_1_), channel_id=1, source_target_pairs={{0,2},{2,0},{4,6},{6,4},{8,10},{10,8},{12,14},{14,12},{16,18},{18,... | collective-permute-start | bytes 208904 | tf_op jit(solution)/shard_map/ppermute | solution.py:563
  17.7 2.1 %shard_map.146 = (f32[64,128]{1,0:T(8,128)S(1)}, f32[1280,128]{1,0:T(8,128)S(1)}, f32[64,128]{1,0:T(8,128)S(1)}, bf16[1280,64]{1,0:T(8,128)(2,1)S(1)}, bf16[64,1...) custom-call(f32[280,128]{1,0:T(8,128)S(1)} %collective-permute-done., ...), custom_call_target="tpu_custom_call" | custom-call | tf_op jit(solution)/shard_map/pallas_call | solution.py:513
  19.9 1.5 %collective-permute-done.4.refs_5_ = f32[136,128]{1,0:T(8,128)S(1)} collective-permute-done((f32[136,128]{1,0:T(8,128)S(1)}, f32[136,128]{1,0:T(8,128)S(1)}, u32[]{:S(2)}, u32[]{:S(2)}) %collective-permute-start.4) | collective-permute-done | bytes 69664 | tf_op jit(solution)/shard_map/ppermute | solution.py:563
  21.4 2.6 %shard_map.147 = (f32[256,128]{1,0:T(8,128)S(1)}, f32[256,128]{1,0:T(8,128)S(1)}, f32[256,128]{1,0:T(8,128)S(1)}, f32[256,128]{1,0:T(8,128)S(1)}, f32[256,128]{1...) custom-call(f32[136,128]{1,0:T(8,128)S(1)} %get-tuple-element.93.ref, ...), custom_call_target="tpu_custom_call" | custom-call | tf_op jit(solution)/shard_map/pallas_call | solution.py:513
  24.0 1.7 %shard_map.148 = (f32[768,128]{1,0:T(8,128)S(1)}, f32[384,128]{1,0:T(8,128)S(1)}, f32[384,128]{1,0:T(8,128)S(1)}, f32[8,128]{1,0:T(8,128)S(1)}, f32[776,128]{1,0:T(8,128)S(1)}) custom-call(f32[256,128]{1,0:T(8,128)S(1)} %get-tuple-element.76.refs_7_.h0.refs_6_, f32[256,128]{1,0:T(8,128)S(1)} %get-tuple-element.91.agg0, ...), custom_call_target="tpu_custom_call" | custom-call | tf_op jit(solution)/shard_map/pallas_call | solution.py:513
  25.7 2.0 %collective-permute-start.7 = (f32[64,128]{1,0:T(8,128)S(1)}, f32[64,128]{1,0:T(8,128)S(1)}, u32[]{:S(2)}, u32[]{:S(2)}) collective-permute-start(f32[64,128]{1,0:T(8,128)S(1)} %get-tuple-element.124.refs_1_), channel_id=1, source_target_pairs={{0,2},{2,0},{4,6},{6,4},{8,10},{10,8},{12,14},{14,12},{16,18},{18,... | collective-permute-start | bytes 98312 | tf_op jit(solution)/shard_map/ppermute | solution.py:563
  27.9 1.9 %collective-permute-done.7.refs_4_ = f32[64,128]{1,0:T(8,128)S(1)} collective-permute-done((f32[64,128]{1,0:T(8,128)S(1)}, f32[64,128]{1,0:T(8,128)S(1)}, u32[]{:S(2)}, u32[]{:S(2)}) %collective-permute-start.7) | collective-permute-done | bytes 32800 | tf_op jit(solution)/shard_map/ppermute | solution.py:563
  29.7 1.8 %shard_map.149.edge_low = f32[384,128]{1,0:T(8,128)S(1)} custom-call(f32[64,128]{1,0:T(8,128)S(1)} %get-tuple-element.116.block.refs_0_, f32[64,128]{1,0:T(8,128)S(1)} %get-tuple-element.124.refs_1_, f32[64,128]{1,0:T(8,128)S(1)} %get-tuple-element.125.refs_2_, f32[64,128]{1,0:T(8,128)S(1)} %get-tuple-element.126.refs_3_, ...), custom_call_target="tpu_custom_call" | custom-call | tf_op jit(solution)/shard_map/pallas_call | solution.py:513
  31.6 1.4 %collective-permute-done.10.late = f32[384,128]{1,0:T(8,128)S(1)} collective-permute-done((f32[384,128]{1,0:T(8,128)S(1)}, f32[384,128]{1,0:T(8,128)S(1)}, u32[]{:S(2)}, u32[]{:S(2)}) %collective-permute-start.10) | collective-permute-done | bytes 196640 | tf_op jit(solution)/shard_map/ppermute | solution.py:648
  33.2 2.0 %collective-permute-start.11 = (f32[200,128]{1,0:T(8,128)S(1)}, f32[200,128]{1,0:T(8,128)S(1)}, u32[]{:S(2)}, u32[]{:S(2)}) collective-permute-start(f32[200,128]{1,0:T(8,128)S(1)} %get-tuple-element.133), channel_id=1, source_target_pairs={{0,2},{2,0},{4,6},{6,4},{8,10},{10,8},{12,14},{14,12},{16,18},{18,... | collective-permute-start | bytes 307208 | tf_op jit(solution)/shard_map/ppermute | solution.py:651
  35.1 1.3 %collective-permute-start.12 = (f32[200,128]{1,0:T(8,128)S(1)}, f32[200,128]{1,0:T(8,128)S(1)}, u32[]{:S(2)}, u32[]{:S(2)}) collective-permute-start(f32[200,128]{1,0:T(8,128)S(1)} %get-tuple-element.134), channel_id=1, source_target_pairs={{0,4},{2,6},{4,0},{6,2},{8,12},{10,14},{12,8},{14,10},{16,20},{18,... | collective-permute-start | bytes 307208 | tf_op jit(solution)/shard_map/ppermute | solution.py:651
  36.7 1.7 %collective-permute-done.11.b = f32[200,128]{1,0:T(8,128)S(1)} collective-permute-done((f32[200,128]{1,0:T(8,128)S(1)}, f32[200,128]{1,0:T(8,128)S(1)}, u32[]{:S(2)}, u32[]{:S(2)}) %collective-permute-start.11) | collective-permute-done | bytes 102432 | tf_op jit(solution)/shard_map/ppermute | solution.py:651
  38.4 2.5 %collective-permute-done.12.c = f32[200,128]{1,0:T(8,128)S(1)} collective-permute-done((f32[200,128]{1,0:T(8,128)S(1)}, f32[200,128]{1,0:T(8,128)S(1)}, u32[]{:S(2)}, u32[]{:S(2)}) %collective-permute-start.12) | collective-permute-done | bytes 102432 | tf_op jit(solution)/shard_map/ppermute | solution.py:651
  40.9 1.1 %collective-permute-done.13.d = f32[200,128]{1,0:T(8,128)S(1)} collective-permute-done((f32[200,128]{1,0:T(8,128)S(1)}, f32[200,128]{1,0:T(8,128)S(1)}, u32[]{:S(2)}, u32[]{:S(2)}) %collective-permute-start.13) | collective-permute-done | bytes 102432 | tf_op jit(solution)/shard_map/ppermute | solution.py:651
  42.0 1.7 %collective-permute-start.14 = (f32[200,128]{1,0:T(8,128)S(1)}, f32[200,128]{1,0:T(8,128)S(1)}, u32[]{:S(2)}, u32[]{:S(2)}) collective-permute-start(f32[200,128]{1,0:T(8,128)S(1)} %shard_map.151.a), channel_id=1, source_target_pairs={{0,8},{1,17},{2,10},{3,19},{4,12},{5,21},{6,14},{7,23},{8,0},{9,25... | collective-permute-start | bytes 307208 | tf_op jit(solution)/shard_map/ppermute | solution.py:659
  43.7 3.1 %collective-permute-done.14.b = f32[200,128]{1,0:T(8,128)S(1)} collective-permute-done((f32[200,128]{1,0:T(8,128)S(1)}, f32[200,128]{1,0:T(8,128)S(1)}, u32[]{:S(2)}, u32[]{:S(2)}) %collective-permute-start.14) | collective-permute-done | bytes 102432 | tf_op jit(solution)/shard_map/ppermute | solution.py:659
  46.8 2.7 %collective-permute-start.15 = (f32[200,128]{1,0:T(8,128)S(1)}, f32[200,128]{1,0:T(8,128)S(1)}, u32[]{:S(2)}, u32[]{:S(2)}) collective-permute-start(f32[200,128]{1,0:T(8,128)S(1)} %shard_map.152.a), channel_id=1, source_target_pairs={{0,16},{1,9},{2,18},{3,11},{4,20},{5,13},{6,22},{7,15},{8,24},{9,1... | collective-permute-start | bytes 307208 | tf_op jit(solution)/shard_map/ppermute | solution.py:659
  49.5 3.0 %collective-permute-done.15.b = f32[200,128]{1,0:T(8,128)S(1)} collective-permute-done((f32[200,128]{1,0:T(8,128)S(1)}, f32[200,128]{1,0:T(8,128)S(1)}, u32[]{:S(2)}, u32[]{:S(2)}) %collective-permute-start.15) | collective-permute-done | bytes 102432 | tf_op jit(solution)/shard_map/ppermute | solution.py:659
  52.4 1.5 %collective-permute-start.18 = (f32[192,128]{1,0:T(8,128)S(1)}, f32[192,128]{1,0:T(8,128)S(1)}, u32[]{:S(2)}, u32[]{:S(2)}) collective-permute-start(f32[192,128]{1,0:T(8,128)S(1)} %get-tuple-element.136.refs_0_), channel_id=1, source_target_pairs={{0,6},{2,4},{4,2},{6,0},{8,14},{10,12},{12,10},{14,8},{16,22},{18,... | collective-permute-start | bytes 294920 | tf_op jit(solution)/shard_map/ppermute | solution.py:651
  56.0 2.1 %collective-permute-done.18.refs_3_ = f32[192,128]{1,0:T(8,128)S(1)} collective-permute-done((f32[192,128]{1,0:T(8,128)S(1)}, f32[192,128]{1,0:T(8,128)S(1)}, u32[]{:S(2)}, u32[]{:S(2)}) %collective-permute-start.18) | collective-permute-done | bytes 98336 | tf_op jit(solution)/shard_map/ppermute | solution.py:651
  (33 shorter events, 7.5 us)
Async XLA Ops:
  3.8 13.9 %collective-permute-start.6 = (f32[280,128]{1,0:T(8,128)S(1)}, f32[280,128]{1,0:T(8,128)S(1)}, u32[]{:S(2)}, u32[]{:S(2)}) collective-permute-start(f32[280,128]{1,0:T(8,128)S(1)} %get-tuple-element.100.refs_3_), channel_id=1, source_target_pairs={{2,4},{4,2},{6,8},{8,6},{10,12},{12,10},{14,16},{16,14},{18,20},{2... | collective-permute-start | bytes 430088 | tf_op jit(solution)/shard_map/ppermute | solution.py:563
  4.4 5.4 %collective-permute-start = (f32[64,128]{1,0:T(8,128)S(1)}, f32[64,128]{1,0:T(8,128)S(1)}, u32[]{:S(2)}, u32[]{:S(2)}) collective-permute-start(f32[64,128]{1,0:T(8,128)S(1)} %get-tuple-element.77.refs_0_), channel_id=1, source_target_pairs={{2,4},{4,2},{6,8},{8,6},{10,12},{12,10},{14,16},{16,14},{18,20},{2... | collective-permute-start | bytes 98312 | tf_op jit(solution)/shard_map/ppermute | solution.py:563
  4.5 8.8 %collective-permute-start.1 = (f32[64,128]{1,0:T(8,128)S(1)}, f32[64,128]{1,0:T(8,128)S(1)}, u32[]{:S(2)}, u32[]{:S(2)}) collective-permute-start(f32[64,128]{1,0:T(8,128)S(1)} %get-tuple-element.78.refs_1_), channel_id=1, source_target_pairs={{0,2},{2,0},{4,6},{6,4},{8,10},{10,8},{12,14},{14,12},{16,18},{18,... | collective-permute-start | bytes 98312 | tf_op jit(solution)/shard_map/ppermute | solution.py:563
  9.8 3.4 %collective-permute-start.2 = (f32[64,128]{1,0:T(8,128)S(1)}, f32[64,128]{1,0:T(8,128)S(1)}, u32[]{:S(2)}, u32[]{:S(2)}) collective-permute-start(f32[64,128]{1,0:T(8,128)S(1)} %get-tuple-element.79.refs_2_), channel_id=1, source_target_pairs={{0,1},{1,0},{2,3},{3,2},{4,5},{5,4},{6,7},{7,6},{8,9},{9,8},{10,11... | collective-permute-start | bytes 98312 | tf_op jit(solution)/shard_map/ppermute | solution.py:563
  15.1 4.8 %collective-permute-start.3 = (f32[136,128]{1,0:T(8,128)S(1)}, f32[136,128]{1,0:T(8,128)S(1)}, u32[]{:S(2)}, u32[]{:S(2)}) collective-permute-start(f32[136,128]{1,0:T(8,128)S(1)} %get-tuple-element.93.refs_0_), channel_id=1, source_target_pairs={{2,4},{4,2},{6,8},{8,6},{10,12},{12,10},{14,16},{16,14},{18,20},{2... | collective-permute-start | bytes 208904 | tf_op jit(solution)/shard_map/ppermute | solution.py:563
  15.2 6.2 %collective-permute-start.4 = (f32[136,128]{1,0:T(8,128)S(1)}, f32[136,128]{1,0:T(8,128)S(1)}, u32[]{:S(2)}, u32[]{:S(2)}) collective-permute-start(f32[136,128]{1,0:T(8,128)S(1)} %get-tuple-element.94.refs_1_), channel_id=1, source_target_pairs={{0,2},{2,0},{4,6},{6,4},{8,10},{10,8},{12,14},{14,12},{16,18},{18,... | collective-permute-start | bytes 208904 | tf_op jit(solution)/shard_map/ppermute | solution.py:563
  17.7 3.7 %collective-permute-start.5 = (f32[136,128]{1,0:T(8,128)S(1)}, f32[136,128]{1,0:T(8,128)S(1)}, u32[]{:S(2)}, u32[]{:S(2)}) collective-permute-start(f32[136,128]{1,0:T(8,128)S(1)} %get-tuple-element.95.refs_2_), channel_id=1, source_target_pairs={{0,1},{1,0},{2,3},{3,2},{4,5},{5,4},{6,7},{7,6},{8,9},{9,8},{10,11... | collective-permute-start | bytes 208904 | tf_op jit(solution)/shard_map/ppermute | solution.py:563
  25.7 7.4 %collective-permute-start.9 = (f32[776,128]{1,0:T(8,128)S(1)}, f32[776,128]{1,0:T(8,128)S(1)}, u32[]{:S(2)}, u32[]{:S(2)}) collective-permute-start(f32[776,128]{1,0:T(8,128)S(1)} %get-tuple-element.131), channel_id=1, source_target_pairs={{0,1},{1,0},{2,3},{3,2},{4,5},{5,4},{6,7},{7,6},{8,9},{9,8},{10,11... | collective-permute-start | bytes 1191944 | tf_op jit(solution)/shard_map/ppermute | solution.py:648
  25.7 4.0 %collective-permute-start.7 = (f32[64,128]{1,0:T(8,128)S(1)}, f32[64,128]{1,0:T(8,128)S(1)}, u32[]{:S(2)}, u32[]{:S(2)}) collective-permute-start(f32[64,128]{1,0:T(8,128)S(1)} %get-tuple-element.124.refs_1_), channel_id=1, source_target_pairs={{0,2},{2,0},{4,6},{6,4},{8,10},{10,8},{12,14},{14,12},{16,18},{18,... | collective-permute-start | bytes 98312 | tf_op jit(solution)/shard_map/ppermute | solution.py:563
  27.7 2.0 %collective-permute-start.8 = (f32[64,128]{1,0:T(8,128)S(1)}, f32[64,128]{1,0:T(8,128)S(1)}, u32[]{:S(2)}, u32[]{:S(2)}) collective-permute-start(f32[64,128]{1,0:T(8,128)S(1)} %get-tuple-element.125.refs_2_), channel_id=1, source_target_pairs={{0,1},{1,0},{2,3},{3,2},{4,5},{5,4},{6,7},{7,6},{8,9},{9,8},{10,11... | collective-permute-start | bytes 98312 | tf_op jit(solution)/shard_map/ppermute | solution.py:563
  31.6 1.5 %collective-permute-start.10 = (f32[384,128]{1,0:T(8,128)S(1)}, f32[384,128]{1,0:T(8,128)S(1)}, u32[]{:S(2)}, u32[]{:S(2)}) collective-permute-start(f32[384,128]{1,0:T(8,128)S(1)} %shard_map.149.edge_low), channel_id=1, source_target_pairs={{0,1},{1,0},{2,3},{3,2},{4,5},{5,4},{6,7},{7,6},{8,9},{9,8},{10,11... | collective-permute-start | bytes 589832 | tf_op jit(solution)/shard_map/ppermute | solution.py:648
  33.2 5.2 %collective-permute-start.11 = (f32[200,128]{1,0:T(8,128)S(1)}, f32[200,128]{1,0:T(8,128)S(1)}, u32[]{:S(2)}, u32[]{:S(2)}) collective-permute-start(f32[200,128]{1,0:T(8,128)S(1)} %get-tuple-element.133), channel_id=1, source_target_pairs={{0,2},{2,0},{4,6},{6,4},{8,10},{10,8},{12,14},{14,12},{16,18},{18,... | collective-permute-start | bytes 307208 | tf_op jit(solution)/shard_map/ppermute | solution.py:651
  35.1 5.8 %collective-permute-start.12 = (f32[200,128]{1,0:T(8,128)S(1)}, f32[200,128]{1,0:T(8,128)S(1)}, u32[]{:S(2)}, u32[]{:S(2)}) collective-permute-start(f32[200,128]{1,0:T(8,128)S(1)} %get-tuple-element.134), channel_id=1, source_target_pairs={{0,4},{2,6},{4,0},{6,2},{8,12},{10,14},{12,8},{14,10},{16,20},{18,... | collective-permute-start | bytes 307208 | tf_op jit(solution)/shard_map/ppermute | solution.py:651
  36.5 5.6 %collective-permute-start.13 = (f32[200,128]{1,0:T(8,128)S(1)}, f32[200,128]{1,0:T(8,128)S(1)}, u32[]{:S(2)}, u32[]{:S(2)}) collective-permute-start(f32[200,128]{1,0:T(8,128)S(1)} %get-tuple-element.135), channel_id=1, source_target_pairs={{0,6},{2,4},{4,2},{6,0},{8,14},{10,12},{12,10},{14,8},{16,22},{18,... | collective-permute-start | bytes 307208 | tf_op jit(solution)/shard_map/ppermute | solution.py:651
  42.0 4.7 %collective-permute-start.14 = (f32[200,128]{1,0:T(8,128)S(1)}, f32[200,128]{1,0:T(8,128)S(1)}, u32[]{:S(2)}, u32[]{:S(2)}) collective-permute-start(f32[200,128]{1,0:T(8,128)S(1)} %shard_map.151.a), channel_id=1, source_target_pairs={{0,8},{1,17},{2,10},{3,19},{4,12},{5,21},{6,14},{7,23},{8,0},{9,25... | collective-permute-start | bytes 307208 | tf_op jit(solution)/shard_map/ppermute | solution.py:659
  46.8 5.6 %collective-permute-start.15 = (f32[200,128]{1,0:T(8,128)S(1)}, f32[200,128]{1,0:T(8,128)S(1)}, u32[]{:S(2)}, u32[]{:S(2)}) collective-permute-start(f32[200,128]{1,0:T(8,128)S(1)} %shard_map.152.a), channel_id=1, source_target_pairs={{0,16},{1,9},{2,18},{3,11},{4,20},{5,13},{6,22},{7,15},{8,24},{9,1... | collective-permute-start | bytes 307208 | tf_op jit(solution)/shard_map/ppermute | solution.py:659
  52.4 5.6 %collective-permute-start.18 = (f32[192,128]{1,0:T(8,128)S(1)}, f32[192,128]{1,0:T(8,128)S(1)}, u32[]{:S(2)}, u32[]{:S(2)}) collective-permute-start(f32[192,128]{1,0:T(8,128)S(1)} %get-tuple-element.136.refs_0_), channel_id=1, source_target_pairs={{0,6},{2,4},{4,2},{6,0},{8,14},{10,12},{12,10},{14,8},{16,22},{18,... | collective-permute-start | bytes 294920 | tf_op jit(solution)/shard_map/ppermute | solution.py:651
  53.9 5.1 %collective-permute-start.17 = (f32[192,128]{1,0:T(8,128)S(1)}, f32[192,128]{1,0:T(8,128)S(1)}, u32[]{:S(2)}, u32[]{:S(2)}) collective-permute-start(f32[192,128]{1,0:T(8,128)S(1)} %get-tuple-element.136.refs_0_), channel_id=1, source_target_pairs={{0,4},{2,6},{4,0},{6,2},{8,12},{10,14},{12,8},{14,10},{16,20},{18,... | collective-permute-start | bytes 294920 | tf_op jit(solution)/shard_map/ppermute | solution.py:651
  55.1 4.6 %collective-permute-start.16 = (f32[192,128]{1,0:T(8,128)S(1)}, f32[192,128]{1,0:T(8,128)S(1)}, u32[]{:S(2)}, u32[]{:S(2)}) collective-permute-start(f32[192,128]{1,0:T(8,128)S(1)} %get-tuple-element.136.refs_0_), channel_id=1, source_target_pairs={{0,2},{2,0},{4,6},{6,4},{8,10},{10,8},{12,14},{14,12},{16,18},{18,... | collective-permute-start | bytes 294920 | tf_op jit(solution)/shard_map/ppermute | solution.py:651
  56.0 3.7 %collective-permute-start.19 = (f32[192,128]{1,0:T(8,128)S(1)}, f32[192,128]{1,0:T(8,128)S(1)}, u32[]{:S(2)}, u32[]{:S(2)}) collective-permute-start(f32[192,128]{1,0:T(8,128)S(1)} %get-tuple-element.136.refs_0_), channel_id=1, source_target_pairs={{0,1},{1,0},{2,3},{3,2},{4,5},{5,4},{6,7},{7,6},{8,9},{9,8},{10,11... | collective-permute-start | bytes 294920 | tf_op jit(solution)/shard_map/ppermute | solution.py:648
  58.1 1.6 %collective-permute-start.22 = (f32[192,128]{1,0:T(8,128)S(1)}, f32[192,128]{1,0:T(8,128)S(1)}, u32[]{:S(2)}, u32[]{:S(2)}) collective-permute-start(f32[192,128]{1,0:T(8,128)S(1)} %collective-permute-done.18.refs_3_), channel_id=1, source_target_pairs={{0,1},{1,0},{2,3},{3,2},{4,5},{5,4},{6,7},{7,6},{8,9},{9,8},{10,11... | collective-permute-start | bytes 294920 | tf_op jit(solution)/shard_map/ppermute | solution.py:648
  59.1 1.3 %collective-permute-start.21 = (f32[192,128]{1,0:T(8,128)S(1)}, f32[192,128]{1,0:T(8,128)S(1)}, u32[]{:S(2)}, u32[]{:S(2)}) collective-permute-start(f32[192,128]{1,0:T(8,128)S(1)} %collective-permute-done.17.refs_2_), channel_id=1, source_target_pairs={{0,1},{1,0},{2,3},{3,2},{4,5},{5,4},{6,7},{7,6},{8,9},{9,8},{10,11... | collective-permute-start | bytes 294920 | tf_op jit(solution)/shard_map/ppermute | solution.py:648
  59.7 1.3 %collective-permute-start.20 = (f32[192,128]{1,0:T(8,128)S(1)}, f32[192,128]{1,0:T(8,128)S(1)}, u32[]{:S(2)}, u32[]{:S(2)}) collective-permute-start(f32[192,128]{1,0:T(8,128)S(1)} %collective-permute-done.16.refs_1_), channel_id=1, source_target_pairs={{0,1},{1,0},{2,3},{3,2},{4,5},{5,4},{6,7},{7,6},{8,9},{9,8},{10,11... | collective-permute-start | bytes 294920 | tf_op jit(solution)/shard_map/ppermute | solution.py:648
